TPU v7x, 32 devices: a whole 2x2x4 slice. The times are simulated.
32 devices in a mesh: seq: 8 (over y, x, core), head: 4 (over z).
Axes of the slice: x: 2, y: 2, z: 4, core: 2. Of those that a mesh axis runs over, the one named last changes fastest.
Arguments:
- token_ids: int32 [6144], replicated, may hold values from 0 to 31999
- completion: int32 [6144], replicated, may hold values from 0 to 1, as said below
- decay_rate: float32 [1, 4], P(None, 'head'), may hold values from 0 to 0.05
- w_mixer: bfloat16 [1, 1024, 6144], P(None, 'seq', 'head'), may hold values from -0.1875 to 0.1875
- w_output: bfloat16 [1, 2048, 1024], P(None, 'head', 'seq'), may hold values from -0.125 to 0.125
- w_expand: bfloat16 [1, 1024, 4096], P(None, 'seq', 'head'), may hold values from -0.1875 to 0.1875
- w_contract: bfloat16 [1, 2048, 1024], P(None, 'head', 'seq'), may hold values from -0.125 to 0.125
- norm_gains: bfloat16 [3, 1024], P(None, 'seq'), may hold values from 0.5 to 1.5
- embedding: bfloat16 [32000, 1024], P('seq'), may hold values from -0.375 to 0.375
- mom_mixer: float32 [1, 1024, 6144], P(None, 'seq', 'head'), may hold values from -0.0010764359 to 0.0010764359
- var_mixer: float32 [1, 1024, 6144], P(None, 'seq', 'head'), may hold values from 2.5431315e-09 to 1.0172526e-08
- mom_output: float32 [1, 2048, 1024], P(None, 'head', 'seq'), may hold values from -0.0010764359 to 0.0010764359
- var_output: float32 [1, 2048, 1024], P(None, 'head', 'seq'), may hold values from 2.5431315e-09 to 1.0172526e-08
- mom_expand: float32 [1, 1024, 4096], P(None, 'seq', 'head'), may hold values from -0.0010764359 to 0.0010764359
- var_expand: float32 [1, 1024, 4096], P(None, 'seq', 'head'), may hold values from 2.5431315e-09 to 1.0172526e-08
- mom_contract: float32 [1, 2048, 1024], P(None, 'head', 'seq'), may hold values from -0.0010764359 to 0.0010764359
- var_contract: float32 [1, 2048, 1024], P(None, 'head', 'seq'), may hold values from 2.5431315e-09 to 1.0172526e-08
- mom_gains: float32 [3, 1024], P(None, 'seq'), may hold values from -0.0010764359 to 0.0010764359
- var_gains: float32 [3, 1024], P(None, 'seq'), may hold values from 2.5431315e-09 to 1.0172526e-08
- mom_embed: float32 [32000, 1024], P('seq', 'head'), may hold values from -0.0010764359 to 0.0010764359
- var_embed: float32 [32000, 1024], P('seq', 'head'), may hold values from 2.5431315e-09 to 1.0172526e-08
Outputs:
- mean_loss: float32 [], replicated
- trust_square_sums: float32 [8, 2], replicated
- new_mom_mixer: float32 [1, 1024, 6144], P(None, 'seq', 'head')
- new_var_mixer: float32 [1, 1024, 6144], P(None, 'seq', 'head')
- new_w_mixer: float32 [1, 1024, 6144], P(None, 'seq', 'head')
- new_mom_output: float32 [1, 2048, 1024], P(None, 'head', 'seq')
- new_var_output: float32 [1, 2048, 1024], P(None, 'head', 'seq')
- new_w_output: float32 [1, 2048, 1024], P(None, 'head', 'seq')
- new_mom_expand: float32 [1, 1024, 4096], P(None, 'seq', 'head')
- new_var_expand: float32 [1, 1024, 4096], P(None, 'seq', 'head')
- new_w_expand: float32 [1, 1024, 4096], P(None, 'seq', 'head')
- new_mom_contract: float32 [1, 2048, 1024], P(None, 'head', 'seq')
- new_var_contract: float32 [1, 2048, 1024], P(None, 'head', 'seq')
- new_w_contract: float32 [1, 2048, 1024], P(None, 'head', 'seq')
- new_mom_gains: float32 [3, 1024], P(None, 'seq')
- new_var_gains: float32 [3, 1024], P(None, 'seq')
- new_w_gains: float32 [3, 1024], P(None, 'seq')
- new_mom_embed: float32 [32000, 1024], P('seq', 'head')
- new_var_embed: float32 [32000, 1024], P('seq', 'head')
- new_w_embed: float32 [32000, 1024], P('seq', 'head')
Inputs may be any that keep to these rules, and one draw needn't show every extreme that they name: `completion`: each span of 768 tokens (one index of seq) holds at most 384 ones, and one span holds exactly 384.
All inputs are finite; a program needn't handle non-finite values.
Results may differ from a plain program's by a relative error of at most 0.018.
Values may be sent and summed in bfloat16 or wider, within the bound.
A program may use at most 192 MiB of HBM per device.

v0:
```python
import jax
import jax.numpy as jnp
from jax import lax
from jax.sharding import PartitionSpec as P

KD = 256
VD = 512
STEP = 10


NORM_EPS = 1e-05
BETA_ONE = 0.9
BETA_TWO = 0.999
ADAM_EPS = 1e-08
DECAY_WT = 0.01
LEARN_RATE = 0.2
TRUST_EPSILON = 1e-06


def prefix(value, axis, join, neutral, backward):
    count, mine = (lax.axis_size(axis), lax.axis_index(axis))
    pieces = jax.tree.map(lambda part: lax.all_gather(part, axis), value)
    if backward:
        pieces = jax.tree.map(lambda part: part[::-1], pieces)
        mine = count - 1 - mine
    subtotal = jax.tree.map(
        lambda part, zero: jnp.full_like(part, 0) + jnp.asarray(zero, part.dtype), value, neutral
    )

    def prefix_step(position, subtotal):
        longer = join(subtotal, jax.tree.map(lambda part: part[position], pieces))
        return jax.tree.map(lambda new, old: jnp.where(position < mine, new, old), longer, subtotal)

    return lax.fori_loop(0, count - 1, prefix_step, subtotal)


def joined(shard, axis, combine):
    everything = jax.tree.map(lambda part: lax.all_gather(part, axis), shard)
    leading = jax.tree.map(lambda part: part[0], everything)

    def joined_step(k, so_far):
        return combine(so_far, jax.tree.map(lambda part: part[k], everything))

    return lax.fori_loop(1, lax.axis_size(axis), joined_step, leading)


def contract_dims(left_side, right_side, left_dim, right_dim):
    return lax.dot_general(
        left_side,
        right_side,
        (((left_dim,), (right_dim,)), ((), ())),
        preferred_element_type=jnp.float32,
    )


def layer_norm(values, gain_row):
    centred = values - jnp.mean(values, axis=-1, keepdims=True)
    spread_sq = jnp.mean(centred * centred, axis=-1, keepdims=True)
    return centred * lax.rsqrt(spread_sq + NORM_EPS) * gain_row


def rotary_tables(positions, width_in):
    halfway = width_in // 2
    frequency = jnp.exp(-jnp.log(10000.0) * jnp.arange(halfway).astype(jnp.float32) / halfway)
    phases = positions.astype(jnp.float32)[:, None] * frequency[None, :]
    return (jnp.cos(phases), jnp.sin(phases))


def rotate(values, cosines, sines):
    halfway = values.shape[-1] // 2
    leading = values[..., :halfway]
    trailing = values[..., halfway:]
    return jnp.concatenate(
        [leading * cosines - trailing * sines, leading * sines + trailing * cosines], axis=-1
    )


def gate_norm(gate_pre, retained):
    scaled = retained * lax.rsqrt(jnp.mean(retained * retained, axis=-1, keepdims=True) + NORM_EPS)
    return gate_pre * jax.nn.sigmoid(gate_pre) * scaled


def gelu_gate(gate_part, up_part):
    return jax.nn.gelu(gate_part) * up_part


def sum_heads_fwd(values):
    return lax.psum(values, "head")


def sum_heads_back(values):
    return lax.psum(values, "head")


def chain_join(earlier, later_part):
    return (earlier[0] * later_part[0], later_part[0] * earlier[1] + later_part[1])


def state_prefix(block_decay, weight_update):
    identity = (jnp.ones((), jnp.float32), jnp.zeros_like(weight_update))
    return prefix((block_decay, weight_update), "seq", chain_join, identity, False)[1]


def state_suffix(block_decay, grad_state):
    identity = (jnp.ones((), jnp.float32), jnp.zeros_like(grad_state))
    return prefix((block_decay, grad_state), "seq", chain_join, identity, True)[1]


def decay_tables(rate_value, span_len):
    steps_in = jnp.arange(span_len).astype(jnp.float32)
    offsets = steps_in[:, None] - steps_in[None, :]
    within = jnp.where(offsets >= 0, jnp.exp(-rate_value * jnp.maximum(offsets, 0.0)), 0.0)
    tail_decay = jnp.exp(-rate_value * (span_len - 1.0 - steps_in))
    lead_decay = jnp.exp(-rate_value * (steps_in + 1.0))
    block_decay = jnp.exp(-rate_value * span_len)
    return (within, tail_decay, lead_decay, block_decay)


def layer_fwd(
    residual, mixer, output, expand, contract, gain_a, gain_b, rate_value, cosines, sines
):
    span_len = residual.shape[0]
    within, tail_decay, lead_decay, block_decay = decay_tables(rate_value, span_len)
    normed = layer_norm(residual, gain_a).astype(jnp.bfloat16)
    proj = jnp.dot(normed, mixer, preferred_element_type=jnp.float32)
    q_pre = proj[:, :KD]
    k_pre = proj[:, KD : 2 * KD]
    gate_pre = proj[:, 2 * KD + VD :]
    query_bf = rotate(q_pre, cosines, sines).astype(jnp.bfloat16)
    keys_bf = (rotate(k_pre, cosines, sines) * KD ** (-0.5)).astype(jnp.bfloat16)
    values_bf = proj[:, 2 * KD : 2 * KD + VD].astype(jnp.bfloat16)
    scores = contract_dims(query_bf, keys_bf, 1, 1)
    weights_blk = (scores * within).astype(jnp.bfloat16)
    inner_part = jnp.dot(weights_blk, values_bf, preferred_element_type=jnp.float32)
    weighted_values = (keys_bf.astype(jnp.float32) * tail_decay[:, None]).astype(jnp.bfloat16)
    weight_update = contract_dims(weighted_values, values_bf, 0, 0)
    state_low = state_prefix(block_decay, weight_update).astype(jnp.bfloat16)
    cross_part = jnp.dot(query_bf, state_low, preferred_element_type=jnp.float32)
    retained = inner_part + lead_decay[:, None] * cross_part
    gated_out = gate_norm(gate_pre, retained).astype(jnp.bfloat16)
    residual_mid = residual + sum_heads_fwd(
        jnp.dot(gated_out, output, preferred_element_type=jnp.float32)
    )
    normed_b = layer_norm(residual_mid, gain_b).astype(jnp.bfloat16)
    gate_up = jnp.dot(normed_b, expand, preferred_element_type=jnp.float32)
    width_ff = gate_up.shape[1] // 2
    hidden = gelu_gate(gate_up[:, :width_ff], gate_up[:, width_ff:]).astype(jnp.bfloat16)
    residual_out = residual_mid + sum_heads_fwd(
        jnp.dot(hidden, contract, preferred_element_type=jnp.float32)
    )
    kept = (
        residual,
        normed,
        q_pre,
        k_pre,
        query_bf,
        keys_bf,
        values_bf,
        gate_pre,
        weights_blk,
        weighted_values,
        state_low,
        retained,
        gated_out,
        residual_mid,
        normed_b,
        gate_up,
        hidden,
    )
    return (residual_out, kept)


def layer_bwd(
    grad_out, kept, mixer, output, expand, contract, gain_a, gain_b, rate_value, cosines, sines
):
    (
        residual,
        normed,
        q_pre,
        k_pre,
        query_bf,
        keys_bf,
        values_bf,
        gate_pre,
        weights_blk,
        weighted_values,
        state_low,
        retained,
        gated_out,
        residual_mid,
        normed_b,
        gate_up,
        hidden,
    ) = kept
    span_len = residual.shape[0]
    within, tail_decay, lead_decay, block_decay = decay_tables(rate_value, span_len)
    grad_branch = grad_out.astype(jnp.bfloat16)
    grad_hidden = contract_dims(grad_branch, contract, 1, 1)
    grad_contract = contract_dims(hidden, grad_branch, 0, 0)
    width_ff = gate_up.shape[1] // 2
    _, gelu_back = jax.vjp(gelu_gate, gate_up[:, :width_ff], gate_up[:, width_ff:])
    grad_gate, grad_up = gelu_back(grad_hidden)
    grad_gate_up = jnp.concatenate([grad_gate, grad_up], axis=1).astype(jnp.bfloat16)
    grad_expand = contract_dims(normed_b, grad_gate_up, 0, 0)
    grad_normed_b = sum_heads_back(contract_dims(grad_gate_up, expand, 1, 1))
    _, norm_back_b = jax.vjp(layer_norm, residual_mid, gain_b)
    grad_mid, grad_gain_b = norm_back_b(grad_normed_b)
    grad_mid = grad_mid + grad_out
    grad_attn = grad_mid.astype(jnp.bfloat16)
    grad_gated = contract_dims(grad_attn, output, 1, 1)
    grad_output = contract_dims(gated_out, grad_attn, 0, 0)
    _, gate_back = jax.vjp(gate_norm, gate_pre, retained)
    grad_gate_pre, grad_ret = gate_back(grad_gated)
    grad_ret_low = grad_ret.astype(jnp.bfloat16)
    grad_cross = (lead_decay[:, None] * grad_ret).astype(jnp.bfloat16)
    grad_weights = contract_dims(grad_ret_low, values_bf, 1, 1)
    grad_scores = (grad_weights * within).astype(jnp.bfloat16)
    grad_query = jnp.dot(grad_scores, keys_bf, preferred_element_type=jnp.float32) + contract_dims(
        grad_cross, state_low, 1, 1
    )
    grad_keys = contract_dims(grad_scores, query_bf, 0, 0)
    grad_state = contract_dims(query_bf, grad_cross, 0, 0)
    grad_update = state_suffix(block_decay, grad_state).astype(jnp.bfloat16)
    grad_values = contract_dims(weights_blk, grad_ret_low, 0, 0) + contract_dims(
        weighted_values, grad_update, 1, 0
    )
    grad_weighted = contract_dims(values_bf, grad_update, 1, 1)
    grad_keys = grad_keys + grad_weighted * tail_decay[:, None]

    def rope_pair(first_pre, second_pre):
        return (
            rotate(first_pre, cosines, sines),
            rotate(second_pre, cosines, sines) * KD ** (-0.5),
        )

    _, rope_back = jax.vjp(rope_pair, q_pre, k_pre)
    grad_q_pre, grad_k_pre = rope_back((grad_query, grad_keys))
    grad_proj = jnp.concatenate(
        [grad_q_pre, grad_k_pre, grad_values, grad_gate_pre], axis=1
    ).astype(jnp.bfloat16)
    grad_mixer = contract_dims(normed, grad_proj, 0, 0)
    grad_normed = sum_heads_back(contract_dims(grad_proj, mixer, 1, 1))
    _, norm_back_a = jax.vjp(layer_norm, residual, gain_a)
    grad_residual, grad_gain_a = norm_back_a(grad_normed)
    grad_residual = grad_residual + grad_mid
    return (
        grad_residual,
        (grad_mixer, grad_output, grad_expand, grad_contract),
        grad_gain_a,
        grad_gain_b,
    )


def lamb_parts(weight, moment, second, grad):
    new_moment = BETA_ONE * moment + (1.0 - BETA_ONE) * grad
    new_second = BETA_TWO * second + (1.0 - BETA_TWO) * grad * grad
    moment_hat = new_moment / (1.0 - BETA_ONE**STEP)
    second_hat = new_second / (1.0 - BETA_TWO**STEP)
    ratio = moment_hat / (jnp.sqrt(second_hat) + ADAM_EPS) + DECAY_WT * weight
    return (new_moment, new_second, ratio)


def local(
    token_ids,
    completion,
    decay_rate,
    w_mixer,
    w_output,
    w_expand,
    w_contract,
    norm_gains,
    embedding,
    mom_mixer,
    var_mixer,
    mom_output,
    var_output,
    mom_expand,
    var_expand,
    mom_contract,
    var_contract,
    mom_gains,
    var_gains,
    mom_embed,
    var_embed,
):
    seq_index = lax.axis_index("seq")
    head_index = lax.axis_index("head")
    head_count = lax.axis_size("head")
    total_tokens = token_ids.shape[0]
    span_len = total_tokens // lax.axis_size("seq")
    spans_n = total_tokens // span_len
    vocab_part = embedding.shape[0]
    model_width = embedding.shape[1]
    quarter = model_width // head_count
    layer_count = w_mixer.shape[0]
    gathered = (
        lax.all_gather(w_mixer, "seq", axis=1, tiled=True),
        lax.all_gather(w_output, "seq", axis=2, tiled=True),
        lax.all_gather(w_expand, "seq", axis=1, tiled=True),
        lax.all_gather(w_contract, "seq", axis=2, tiled=True),
        lax.all_gather(norm_gains, "seq", axis=1, tiled=True),
    )
    mixer_all, output_all, expand_all, contract_all, gains_all = gathered
    gains_f = gains_all.astype(jnp.float32)
    token_start = seq_index * span_len
    vocab_start = seq_index * vocab_part
    cosines, sines = rotary_tables(token_start + jnp.arange(span_len), KD)
    chosen = token_ids - vocab_start
    inside = ((chosen >= 0) & (chosen < vocab_part)).astype(jnp.float32)
    table_rows = jnp.take(embedding, jnp.clip(chosen, 0, vocab_part - 1), axis=0).astype(
        jnp.float32
    )
    residual = lax.psum_scatter(
        (table_rows * inside[:, None]).astype(jnp.bfloat16), "seq", scatter_dimension=0, tiled=True
    ).astype(jnp.float32)
    layer_no = 0
    residual, kept = layer_fwd(
        residual,
        mixer_all[layer_no],
        output_all[layer_no],
        expand_all[layer_no],
        contract_all[layer_no],
        gains_f[2 * layer_no],
        gains_f[2 * layer_no + 1],
        decay_rate[layer_no, 0],
        cosines,
        sines,
    )
    kept_all = [kept]
    final_gain = gains_f[2 * layer_count]
    final_norm = layer_norm(residual, final_gain).astype(jnp.bfloat16)
    capacity = span_len // 2
    slot_quarter = capacity // head_count
    local_mask = lax.dynamic_slice_in_dim(completion, token_start, span_len)
    slot_of = jnp.where(local_mask == 1, jnp.cumsum(local_mask) - 1, -1)
    own_slots = head_index * slot_quarter + jnp.arange(slot_quarter)
    picker = (slot_of[None, :] == own_slots[:, None]).astype(jnp.bfloat16)
    chosen_own = jnp.dot(picker, final_norm, preferred_element_type=jnp.float32).astype(
        jnp.bfloat16
    )
    chosen_all = lax.all_gather(chosen_own, "seq", axis=0, tiled=True)
    mask_grid = completion.reshape(spans_n, span_len)
    next_ids = jnp.roll(token_ids, -1).reshape(spans_n, span_len)
    live = (completion * (jnp.arange(total_tokens) < total_tokens - 1)).reshape(spans_n, span_len)
    slot_grid = jnp.where(mask_grid == 1, jnp.cumsum(mask_grid, axis=1) - 1, -1)
    matches = slot_grid[:, None, :] == own_slots[None, :, None]
    targets = jnp.sum(jnp.where(matches, next_ids[:, None, :], 0), axis=-1).reshape(-1)
    weight_rows = (
        jnp.sum(jnp.where(matches, live[:, None, :], 0), axis=-1).reshape(-1).astype(jnp.float32)
    )
    count_live = jnp.sum(live).astype(jnp.float32)
    logits = contract_dims(chosen_all, embedding, 1, 1)
    local_target = targets - vocab_start
    target_hit = jnp.arange(vocab_part)[None, :] == local_target[:, None]
    target_logit = jnp.sum(jnp.where(target_hit, logits, 0.0), axis=-1)
    peak = jnp.max(logits, axis=-1)
    exp_total = jnp.sum(jnp.exp(logits - peak[:, None]), axis=-1)

    def stats_join(left_side, right_side):
        highest = jnp.maximum(left_side[0], right_side[0])
        summed = left_side[1] * jnp.exp(left_side[0] - highest) + right_side[1] * jnp.exp(
            right_side[0] - highest
        )
        return (highest, summed)

    peak_all, total_all = joined((peak, exp_total), "seq", stats_join)
    log_total = peak_all + jnp.log(total_all)
    scale_row = weight_rows / count_live
    sequence_single = (seq_index == 0).astype(jnp.float32)
    shard_loss = jnp.sum(scale_row * log_total) * sequence_single - jnp.sum(
        scale_row * target_logit
    )
    grad_logits = (
        (jnp.exp(logits - log_total[:, None]) - target_hit.astype(jnp.float32)) * scale_row[:, None]
    ).astype(jnp.bfloat16)
    grad_table = contract_dims(grad_logits, chosen_all, 0, 0)
    grad_own = lax.psum_scatter(
        jnp.dot(grad_logits, embedding, preferred_element_type=jnp.float32),
        "seq",
        scatter_dimension=0,
        tiled=True,
    )
    placed_slots = lax.dynamic_update_slice_in_dim(
        jnp.zeros((capacity, model_width), jnp.float32), grad_own, head_index * slot_quarter, 0
    )
    grad_slots = sum_heads_back(placed_slots)
    grad_final = jnp.where(
        (slot_of >= 0)[:, None],
        jnp.take(grad_slots, jnp.clip(slot_of, 0, capacity - 1), axis=0),
        0.0,
    )
    _, final_back = jax.vjp(layer_norm, residual, final_gain)
    grad_stream, grad_gain_final = final_back(grad_final)
    layer_grads = []
    gain_grads = [grad_gain_final] * (2 * layer_count + 1)
    for layer_no in reversed(range(layer_count)):
        grad_stream, weight_grad, grad_gain_a, grad_gain_b = layer_bwd(
            grad_stream,
            kept_all[layer_no],
            mixer_all[layer_no],
            output_all[layer_no],
            expand_all[layer_no],
            contract_all[layer_no],
            gains_f[2 * layer_no],
            gains_f[2 * layer_no + 1],
            decay_rate[layer_no, 0],
            cosines,
            sines,
        )
        layer_grads.insert(0, weight_grad)
        gain_grads[2 * layer_no] = grad_gain_a
        gain_grads[2 * layer_no + 1] = grad_gain_b
    rows_quarter = span_len // head_count
    own_rows = lax.dynamic_slice_in_dim(grad_stream, head_index * rows_quarter, rows_quarter, 0)
    piece_rows = lax.all_gather(own_rows, "seq", axis=0, tiled=True)
    index_in = jnp.arange(piece_rows.shape[0])
    token_at = (
        index_in // rows_quarter * span_len + head_index * rows_quarter + index_in % rows_quarter
    )
    local_id = jnp.take(token_ids, token_at) - vocab_start
    inside = ((local_id >= 0) & (local_id < vocab_part)).astype(jnp.float32)
    grad_table = grad_table + jax.ops.segment_sum(
        piece_rows * inside[:, None], jnp.clip(local_id, 0, vocab_part - 1), num_segments=vocab_part
    )
    grad_embed = lax.psum_scatter(grad_table, "head", scatter_dimension=1, tiled=True)
    stacked = (
        jnp.stack([group_entry[0] for group_entry in layer_grads]),
        jnp.stack([group_entry[1] for group_entry in layer_grads]),
        jnp.stack([group_entry[2] for group_entry in layer_grads]),
        jnp.stack([group_entry[3] for group_entry in layer_grads]),
        jnp.stack(gain_grads),
    )
    grad_mixer, grad_output, grad_expand, grad_contract, grad_gains = (
        lax.psum_scatter(stacked[0], "seq", scatter_dimension=1, tiled=True),
        lax.psum_scatter(stacked[1], "seq", scatter_dimension=2, tiled=True),
        lax.psum_scatter(stacked[2], "seq", scatter_dimension=1, tiled=True),
        lax.psum_scatter(stacked[3], "seq", scatter_dimension=2, tiled=True),
        lax.psum_scatter(stacked[4], "seq", scatter_dimension=1, tiled=True),
    )
    mixer_f = w_mixer.astype(jnp.float32)
    output_f = w_output.astype(jnp.float32)
    expand_f = w_expand.astype(jnp.float32)
    contract_f = w_contract.astype(jnp.float32)
    gains_own = norm_gains.astype(jnp.float32)
    table_own = lax.dynamic_slice_in_dim(embedding, head_index * quarter, quarter, 1).astype(
        jnp.float32
    )
    part_mixer = lamb_parts(mixer_f, mom_mixer, var_mixer, grad_mixer)
    part_output = lamb_parts(output_f, mom_output, var_output, grad_output)
    part_expand = lamb_parts(expand_f, mom_expand, var_expand, grad_expand)
    part_contract = lamb_parts(contract_f, mom_contract, var_contract, grad_contract)
    shard_gains = lamb_parts(gains_own, mom_gains, var_gains, grad_gains)
    shard_table = lamb_parts(table_own, mom_embed, var_embed, grad_embed)
    head_once = (head_index == 0).astype(jnp.float32)
    layered_w = (mixer_f, output_f, expand_f, contract_f)
    layered_ratio_rows = (part_mixer[2], part_output[2], part_expand[2], part_contract[2])
    wsq_layers = jnp.stack(
        [jnp.sum(group_entry * group_entry, axis=(1, 2)) for group_entry in layered_w], axis=1
    ).reshape(-1)
    layer_ratio_squares = jnp.stack(
        [jnp.sum(group_entry * group_entry, axis=(1, 2)) for group_entry in layered_ratio_rows],
        axis=1,
    ).reshape(-1)
    shard_weight_squares = jnp.concatenate(
        [
            wsq_layers,
            jnp.sum(table_own * table_own)[None],
            jnp.sum(gains_own * gains_own, axis=1) * head_once,
        ]
    )
    shard_ratio_squares = jnp.concatenate(
        [
            layer_ratio_squares,
            jnp.sum(shard_table[2] * shard_table[2])[None],
            jnp.sum(shard_gains[2] * shard_gains[2], axis=1) * head_once,
        ]
    )
    weight_squares, ratio_squares, scalar_loss = lax.psum(
        (shard_weight_squares, shard_ratio_squares, shard_loss), ("seq", "head")
    )
    trust_ratio = jnp.sqrt(weight_squares) * lax.rsqrt(ratio_squares + TRUST_EPSILON)
    trust_layers = trust_ratio[: 4 * layer_count].reshape(layer_count, 4)
    new_w_mixer = mixer_f - LEARN_RATE * trust_layers[:, 0][:, None, None] * part_mixer[2]
    new_w_output = output_f - LEARN_RATE * trust_layers[:, 1][:, None, None] * part_output[2]
    new_w_expand = expand_f - LEARN_RATE * trust_layers[:, 2][:, None, None] * part_expand[2]
    new_w_contract = contract_f - LEARN_RATE * trust_layers[:, 3][:, None, None] * part_contract[2]
    new_w_embed = table_own - LEARN_RATE * trust_ratio[4 * layer_count] * shard_table[2]
    new_w_gains = (
        gains_own - LEARN_RATE * trust_ratio[4 * layer_count + 1 :][:, None] * shard_gains[2]
    )
    trust_square_sums = jnp.stack([weight_squares, ratio_squares], axis=1)
    return (
        scalar_loss,
        trust_square_sums,
        part_mixer[0],
        part_mixer[1],
        new_w_mixer,
        part_output[0],
        part_output[1],
        new_w_output,
        part_expand[0],
        part_expand[1],
        new_w_expand,
        part_contract[0],
        part_contract[1],
        new_w_contract,
        shard_gains[0],
        shard_gains[1],
        new_w_gains,
        shard_table[0],
        shard_table[1],
        new_w_embed,
    )


def solution(mesh):
    placed = (
        P(),
        P(),
        P(None, "head"),
        P(None, "seq", "head"),
        P(None, "head", "seq"),
        P(None, "seq", "head"),
        P(None, "head", "seq"),
        P(None, "seq"),
        P("seq", None),
        P(None, "seq", "head"),
        P(None, "seq", "head"),
        P(None, "head", "seq"),
        P(None, "head", "seq"),
        P(None, "seq", "head"),
        P(None, "seq", "head"),
        P(None, "head", "seq"),
        P(None, "head", "seq"),
        P(None, "seq"),
        P(None, "seq"),
        P("seq", "head"),
        P("seq", "head"),
    )
    return jax.shard_map(
        local,
        mesh=mesh,
        in_specs=placed,
        out_specs=(
            P(),
            P(),
            P(None, "seq", "head"),
            P(None, "seq", "head"),
            P(None, "seq", "head"),
            P(None, "head", "seq"),
            P(None, "head", "seq"),
            P(None, "head", "seq"),
            P(None, "seq", "head"),
            P(None, "seq", "head"),
            P(None, "seq", "head"),
            P(None, "head", "seq"),
            P(None, "head", "seq"),
            P(None, "head", "seq"),
            P(None, "seq"),
            P(None, "seq"),
            P(None, "seq"),
            P("seq", "head"),
            P("seq", "head"),
            P("seq", "head"),
        ),
        check_vma=False,
    )
```

profile of v0, /device:TPU:0, one launch (start us, length us, event | category | flops | bytes accessed | tf_op | source)
XLA Modules:
  0.0 1756.6 jit_solution(16875427561192827058)
XLA Ops:
  8.8 35.2 %gather_fusion = bf16[6144,1024]{1,0:T(8,128)(2,1)} fusion(bf16[4000,1024]{1,0:T(8,128)(2,1)} %param.35, s32[6144]{0:T(1024)S(1)} %fusion.115), kind=kCustom, calls=%fused_computation | custom fusion | bytes 25190400 | tf_op jit(solution)/shard_map/jit(_take)/gather | solution.py:310
  43.9 11.5 multiply_convert_fusion
  56.9 10.4 all_gather.53
  67.4 83.2 %reduce-scatter.11.cloned.1.call-done = bf16[768,1024]{1,0:T(8,128)(2,1)} async-done(((bf16[6144,1024]{1,0:T(8,128)(2,1)}), bf16[768,1024]{1,0:T(8,128)(2,1)}) %reduce-scatter.11.cloned.1.call-update) | async-done | bytes 1572880 | tf_op jit(solution)/shard_map/reduce_scatter | solution.py:313
  154.4 30.3 %all-gather.15.cloned.1.call-done = bf16[1,1024,1536]{2,1,0:T(8,128)(2,1)} async-done(((bf16[1,128,1536]{2,1,0:T(8,128)(2,1)}), bf16[1,1024,1536]{2,1,0:T(8,128)(2,1)}) %all-gather.15.cloned.1.call-update) | async-done | bytes 3145744 | tf_op jit(solution)/shard_map/all_gather | solution.py:297
  195.0 13.5 all-reduce.4
  209.4 20.3 %all-gather.27.cloned.1.call-done = f32[2048,512]{1,0:T(8,128)} async-done(((f32[256,512]{1,0:T(8,128)}), f32[2048,512]{1,0:T(8,128)}) %all-gather.27.cloned.1.call-update) | async-done | bytes 4194320 | tf_op jit(solution)/shard_map/all_gather | solution.py:22
  229.7 17.9 %while.46 = (s32[]{:T(128)}, f32[256,512]{1,0:T(8,128)S(1)}, s32[]{:T(128)}, f32[8]{0:T(128)S(1)}, f32[8,256,512]{2,1,0:T(8,128)}, /*index=5*/s32[]{:T(128)}, s32[]{:T(128)}) while((s32[]{:T(128)}, f32[256,512]{1,0:T(8,128)S(1)}, s32[]{:T(128)}, f32[8]{0:T(128)S(1)}, f32[8,256,512]{2,1,0:T(8,128)}, /*index=5*/s32[]{:T(128)}, ...), condition=%wide.region_10.11_spmd.clone, body=%wide.region_9.10_spmd.clone.sunk | while | flops 524292 | bytes 1572989 | solution.py:34
  260.4 119.6 %all-reduce.12.cloned.1.call-done = f32[768,1024]{1,0:T(8,128)} async-done(((f32[768,1024]{1,0:T(8,128)}), f32[768,1024]{1,0:T(8,128)}) %all-reduce.12.cloned.1.call-update) | async-done | bytes 3145744 | tf_op jit(solution)/shard_map/psum | solution.py:88
  383.2 25.3 %all-gather.19.cloned.1.call-done = bf16[1,1024,1024]{2,1,0:T(8,128)(2,1)} async-done(((bf16[1,128,1024]{2,1,0:T(8,128)(2,1)}), bf16[1,1024,1024]{2,1,0:T(8,128)(2,1)}) %all-gather.19.cloned.1.call-update) | async-done | bytes 2097168 | tf_op jit(solution)/shard_map/all_gather | solution.py:299
  415.1 18.8 %all-gather.21.cloned.1.call-done = bf16[1,512,1024]{2,1,0:T(8,128)(2,1)} async-done(((bf16[1,512,128]{2,1,0:T(8,128)(2,1)}), bf16[1,512,1024]{2,1,0:T(8,128)(2,1)}) %all-gather.21.cloned.1.call-update) | async-done | bytes 1048592 | tf_op jit(solution)/shard_map/all_gather | solution.py:300
  440.0 119.3 %all-reduce.14.cloned.1.call-done = f32[768,1024]{1,0:T(8,128)} async-done(((f32[768,1024]{1,0:T(8,128)}), f32[768,1024]{1,0:T(8,128)}) %all-reduce.14.cloned.1.call-update) | async-done | bytes 3145744 | tf_op jit(solution)/shard_map/psum | solution.py:88
  572.4 17.0 all-gather.23.cloned.1.call-done
  589.4 9.6 fusion.163
  603.6 9.0 all-gather.5
  622.3 13.4 fusion.147
  635.8 46.2 %reduce-scatter.13.cloned.1.call-done = f32[96,1024]{1,0:T(8,128)} async-done(((f32[768,1024]{1,0:T(8,128)}), f32[96,1024]{1,0:T(8,128)}) %reduce-scatter.13.cloned.1.call-update) | async-done | bytes 393232 | tf_op jit(solution)/shard_map/reduce_scatter | solution.py:377
  685.2 69.0 %all-reduce.16.cloned.1.call-done = f32[384,1024]{1,0:T(8,128)} async-done(((f32[384,1024]{1,0:T(8,128)}), f32[384,1024]{1,0:T(8,128)}) %all-reduce.16.cloned.1.call-update) | async-done | bytes 1572880 | tf_op jit(solution)/shard_map/psum | solution.py:92
  774.1 120.1 %all-reduce.18.cloned.1.call-done = f32[768,1024]{1,0:T(8,128)} async-done(((f32[768,1024]{1,0:T(8,128)}), f32[768,1024]{1,0:T(8,128)}) %all-reduce.18.cloned.1.call-update) | async-done | bytes 3145744 | tf_op jit(solution)/shard_map/psum | solution.py:92
  914.6 29.3 %all-gather.29.cloned.1.call-done = f32[2048,512]{1,0:T(8,128)} async-done(((f32[256,512]{1,0:T(8,128)}), f32[2048,512]{1,0:T(8,128)}) %all-gather.29.cloned.1.call-update) | async-done | bytes 4194320 | tf_op jit(solution)/shard_map/all_gather | solution.py:22
  948.6 23.2 %while.47 = (s32[]{:T(128)}, f32[256,512]{1,0:T(8,128)}, s32[]{:T(128)}, f32[8]{0:T(128)S(1)}, f32[8,256,512]{2,1,0:T(8,128)}, /*index=5*/s32[]{:T(128)}, s32[]{:T(128)}) while((s32[]{:T(128)}, f32[256,512]{1,0:T(8,128)}, s32[]{:T(128)}, f32[8]{0:T(128)S(1)}, f32[8,256,512]{2,1,0:T(8,128)}, /*index=5*/s32[]{:T(128)}, ...), condition=%wide.region_43.44_spmd.clone, body=%wide.region_42.43_spmd.clone.sunk | while | flops 524292 | bytes 1572989 | solution.py:34
  984.2 120.9 %all-reduce.20.cloned.1.call-done = f32[768,1024]{1,0:T(8,128)} async-done(((f32[768,1024]{1,0:T(8,128)}), f32[768,1024]{1,0:T(8,128)}) %all-reduce.20.cloned.1.call-update) | async-done | bytes 3145744 | tf_op jit(solution)/shard_map/psum | solution.py:92
  1145.7 15.7 fusion.146
  1161.4 26.5 %scatter_custom_fusion = f32[4000,1024]{1,0:T(8,128)} fusion(f32[4000,1024]{1,0:T(8,128)} %fusion.146, s32[1536]{0:T(1024)S(1)} %clamp_reduce_fusion, f32[1536,1024]{1,0:T(8,128)} %all-gather.25.cloned.1.call-done, f32[1536]{0:T(1024)S(1)} %and_convert_fusion.1), kind=kCustom, calls=%fused_computation.16 | custom fusion | flops 3145728 | bytes 22683648 | tf_op jit(solution)/shard_map/scatter-add | solution.py:422
  1189.5 12.1 reduce-scatter.21.cloned.1.call-done
  1204.2 51.8 %reduce-scatter.19.cloned.1.call-done = f32[1,128,1024]{2,1,0:T(8,128)} async-done(((f32[1,1024,1024]{2,1,0:T(8,128)}), f32[1,128,1024]{2,1,0:T(8,128)}) %reduce-scatter.19.cloned.1.call-update) | async-done | bytes 524304 | tf_op jit(solution)/shard_map/reduce_scatter | solution.py:436
  1258.2 42.8 %reduce-scatter.17.cloned.1.call-done = f32[1,512,128]{2,1,0:T(8,128)} async-done(((f32[1,512,1024]{2,1,0:T(8,128)}), f32[1,512,128]{2,1,0:T(8,128)}) %reduce-scatter.17.cloned.1.call-update) | async-done | bytes 262160 | tf_op jit(solution)/shard_map/reduce_scatter | solution.py:435
  1303.6 35.1 %reduce-scatter.25.cloned.1.call-done = f32[128,3]{1,0:T(8,128)} async-done(((f32[1024,3]{1,0:T(8,128)}), f32[128,3]{1,0:T(8,128)}) %reduce-scatter.25.cloned.1.call-update) | async-done | bytes 1552
  1341.4 62.3 %reduce-scatter.15.cloned.1.call-done = f32[1,128,1536]{2,1,0:T(8,128)} async-done(((f32[1,1024,1536]{2,1,0:T(8,128)}), f32[1,128,1536]{2,1,0:T(8,128)}) %reduce-scatter.15.cloned.1.call-update) | async-done | bytes 786448 | tf_op jit(solution)/shard_map/reduce_scatter | solution.py:434
  1412.0 268.4 %reduce-scatter.23.cloned.1.call-done = f32[4000,256]{1,0:T(8,128)} async-done(((f32[4000,1024]{1,0:T(8,128)}), f32[4000,256]{1,0:T(8,128)}) %reduce-scatter.23.cloned.1.call-update) | async-done | bytes 4096016 | tf_op jit(solution)/shard_map/reduce_scatter | solution.py:425
  1680.4 10.3 multiply_reduce_fusion
  1693.1 41.0 %all-reduce.5 = (f32[]{:T(128)}, f32[8]{0:T(128)S(1)}, f32[8]{0:T(128)S(1)}) all-reduce(f32[]{:T(128)S(6)} %sub.225, f32[8]{0:T(128)} %pad_maximum_fusion.10, f32[8]{0:T(128)} %pad_maximum_fusion.9), channel_id=1, replica_groups=mesh['seq'=8,'head'=4] {'seq','head'}, use_global_device_ids=true, to_apply=%region_26.27 | all-reduce | flops 17 | bytes 136 | tf_op jit(solution)/shard_map/psum | solution.py:478
  (412 shorter events, 246.6 us)
Async XLA Ops:
  7.2 143.4 %reduce-scatter.11.cloned.1.call-start = ((), (), s32[]{:S(2)}) async-start(), calls=%async_computation.8 | async-start | bytes 14155776 | tf_op jit(solution)/shard_map/reduce_scatter | solution.py:313
  55.5 129.3 %all-gather.15.cloned.1.call-start = ((), (), s32[]{:S(2)}) async-start(), calls=%async_computation.9 | async-start | bytes 3538944 | tf_op jit(solution)/shard_map/all_gather | solution.py:297
  56.2 173.4 %all-gather.27.cloned.1.call-start = ((), (), s32[]{:S(2)}) async-start(), calls=%async_computation.26 | async-start | bytes 4718592 | tf_op jit(solution)/shard_map/all_gather | solution.py:22
  67.4 122.0 %copy-start.72 = (f32[128]{0:T(128)}, f32[128]{0:T(128)S(1)}, u32[]{:S(2)}) copy-start(f32[128]{0:T(128)S(1)} %multiply_exponential_fusion.2) | copy-start | bytes 1540
  67.4 341.2 %copy-start.61 = (f32[1,1024]{1,0:T(1,128)}, f32[1,1024]{1,0:T(1,128)S(1)}, u32[]{:S(2)}) copy-start(f32[1,1024]{1,0:T(1,128)S(1)} %get-tuple-element.485) | copy-start | bytes 12292
  192.9 62.0 %all-gather.17.cloned.1.call-start = ((), (), s32[]{:S(2)}) async-start(), calls=%async_computation.10 | async-start | bytes 1179648 | tf_op jit(solution)/shard_map/all_gather | solution.py:298
  193.5 186.5 %all-reduce.12.cloned.1.call-start = ((), (), s32[]{:S(2)}) async-start(), calls=%async_computation.11 | async-start | bytes 6291456 | tf_op jit(solution)/shard_map/psum | solution.py:88
  258.8 149.8 %all-gather.19.cloned.1.call-start = ((), (), s32[]{:S(2)}) async-start(), calls=%async_computation.12 | async-start | bytes 2359296 | tf_op jit(solution)/shard_map/all_gather | solution.py:299
  259.4 174.6 %all-gather.21.cloned.1.call-start = ((), (), s32[]{:S(2)}) async-start(), calls=%async_computation.13 | async-start | bytes 1179648 | tf_op jit(solution)/shard_map/all_gather | solution.py:300
  260.1 299.1 %all-reduce.14.cloned.1.call-start = ((), (), s32[]{:S(2)}) async-start(), calls=%async_computation.14 | async-start | bytes 6291456 | tf_op jit(solution)/shard_map/psum | solution.py:88
  438.1 151.4 %all-gather.23.cloned.1.call-start = ((), (), s32[]{:S(2)}) async-start(), calls=%async_computation.15 | async-start | bytes 1769472 | tf_op jit(solution)/shard_map/all_gather | solution.py:341
  439.3 122.9 %copy-start.74 = (s32[96]{0:T(128)}, s32[96]{0:T(128)S(1)}, u32[]{:S(2)}) copy-start(s32[96]{0:T(128)S(1)} %iota_add_fusion) | copy-start | bytes 1156
  564.7 117.3 %reduce-scatter.13.cloned.1.call-start = ((), (), s32[]{:S(2)}) async-start(), calls=%async_computation.16 | async-start | bytes 3538944 | tf_op jit(solution)/shard_map/reduce_scatter | solution.py:377
  635.7 118.5 %all-reduce.16.cloned.1.call-start = ((), (), s32[]{:S(2)}) async-start(), calls=%async_computation.17 | async-start | bytes 3145728 | tf_op jit(solution)/shard_map/psum | solution.py:92
  685.1 209.2 %all-reduce.18.cloned.1.call-start = ((), (), s32[]{:S(2)}) async-start(), calls=%async_computation.18 | async-start | bytes 6291456 | tf_op jit(solution)/shard_map/psum | solution.py:92
  773.9 170.0 %all-gather.29.cloned.1.call-start = ((), (), s32[]{:S(2)}) async-start(), calls=%async_computation.27 | async-start | bytes 4718592 | tf_op jit(solution)/shard_map/all_gather | solution.py:22
  908.2 196.9 %all-reduce.20.cloned.1.call-start = ((), (), s32[]{:S(2)}) async-start(), calls=%async_computation.23 | async-start | bytes 6291456 | tf_op jit(solution)/shard_map/psum | solution.py:92
  984.0 177.5 %all-gather.25.cloned.1.call-start = ((), (), s32[]{:S(2)}) async-start(), calls=%async_computation.24 | async-start | bytes 7077888 | tf_op jit(solution)/shard_map/all_gather | solution.py:415
  1112.2 89.4 %reduce-scatter.21.cloned.1.call-start = ((), (), s32[]{:S(2)}) async-start(), calls=%async_computation.22 | async-start | bytes 2359296 | tf_op jit(solution)/shard_map/reduce_scatter | solution.py:437
  1116.8 139.2 %reduce-scatter.19.cloned.1.call-start = ((), (), s32[]{:S(2)}) async-start(), calls=%async_computation.21 | async-start | bytes 4718592 | tf_op jit(solution)/shard_map/reduce_scatter | solution.py:436
  1122.5 178.4 %reduce-scatter.17.cloned.1.call-start = ((), (), s32[]{:S(2)}) async-start(), calls=%async_computation.20 | async-start | bytes 2359296 | tf_op jit(solution)/shard_map/reduce_scatter | solution.py:435
  1127.9 210.9 %reduce-scatter.25.cloned.1.call-start = ((), (), s32[]{:S(2)}) async-start(), calls=%async_computation.28 | async-start | bytes 589824
  1129.0 274.8 %reduce-scatter.15.cloned.1.call-start = ((), (), s32[]{:S(2)}) async-start(), calls=%async_computation.19 | async-start | bytes 7077888 | tf_op jit(solution)/shard_map/reduce_scatter | solution.py:434
  1136.8 543.5 %reduce-scatter.23.cloned.1.call-start = ((), (), s32[]{:S(2)}) async-start(), calls=%async_computation.25 | async-start | bytes 20480000 | tf_op jit(solution)/shard_map/reduce_scatter | solution.py:425
  1188.0 151.6 %copy-start.67 = (bf16[3,128]{1,0:T(4,128)(2,1)S(1)}, bf16[3,128]{1,0:T(4,128)(2,1)}, u32[]{:S(2)}) copy-start(bf16[3,128]{1,0:T(4,128)(2,1)} %param.34) | copy-start | bytes 2308
  1188.1 151.6 %copy-start.70 = (f32[3,128]{1,0:T(4,128)S(1)}, f32[3,128]{1,0:T(4,128)}, u32[]{:S(2)}) copy-start(f32[3,128]{1,0:T(4,128)} %param.44) | copy-start | bytes 4612
  1188.1 151.6 %copy-start.71 = (f32[3,128]{1,0:T(4,128)S(1)}, f32[3,128]{1,0:T(4,128)}, u32[]{:S(2)}) copy-start(f32[3,128]{1,0:T(4,128)} %param.45) | copy-start | bytes 4612
  1188.1 215.7 %copy-start.26 = (bf16[1,128,1536]{2,1,0:T(8,128)(2,1)S(1)}, bf16[1,128,1536]{2,1,0:T(8,128)(2,1)}, u32[]{:S(2)}) copy-start(bf16[1,128,1536]{2,1,0:T(8,128)(2,1)} %param.30) | copy-start | bytes 1179652
  1258.1 488.7 %copy-start.33 = (f32[1,128,1024]{2,1,0:T(8,128)}, f32[1,128,1024]{2,1,0:T(8,128)S(1)}, u32[]{:S(2)}) copy-start(f32[1,128,1024]{2,1,0:T(8,128)S(1)} %get-tuple-element.440) | copy-start | bytes 1572868
  1258.2 488.7 %copy-start.34 = (f32[1,128,1024]{2,1,0:T(8,128)}, f32[1,128,1024]{2,1,0:T(8,128)S(1)}, u32[]{:S(2)}) copy-start(f32[1,128,1024]{2,1,0:T(8,128)S(1)} %get-tuple-element.441) | copy-start | bytes 1572868
  1406.6 341.3 %copy-start.27 = (f32[1,128,1536]{2,1,0:T(8,128)}, f32[1,128,1536]{2,1,0:T(8,128)S(1)}, u32[]{:S(2)}) copy-start(f32[1,128,1536]{2,1,0:T(8,128)S(1)} %get-tuple-element.436) | copy-start | bytes 2359300
  1406.6 341.3 %copy-start.28 = (f32[1,128,1536]{2,1,0:T(8,128)}, f32[1,128,1536]{2,1,0:T(8,128)S(1)}, u32[]{:S(2)}) copy-start(f32[1,128,1536]{2,1,0:T(8,128)S(1)} %get-tuple-element.437) | copy-start | bytes 2359300
  (76 other events, 1086.1 us)
Sparse Core Ops, SparseCore 0:
  55.6 94.9 reduce-scatter.10
  152.5 32.1 all-gather.14
  193.0 36.6 all-gather.26
  231.4 23.4 all-gather.16
  258.9 121.0 all-reduce.11
  381.7 26.7 all-gather.18
  410.4 23.4 all-gather.20
  438.2 121.0 all-reduce.13
  564.8 24.5 all-gather.22
  635.9 46.0 reduce-scatter.12
  685.2 68.9 all-reduce.15
  774.0 120.2 all-reduce.17
  908.3 35.5 all-gather.28
  984.1 121.0 all-reduce.19
  1112.3 44.3 all-gather.24
  1160.5 41.1 reduce-scatter.20
  1204.8 51.1 reduce-scatter.18
  1259.8 41.1 reduce-scatter.16
  1304.6 34.1 reduce-scatter.24
  1342.0 61.7 reduce-scatter.14
  1406.1 274.1 reduce-scatter.22
where the time goes:
time: 1770 us; the launch traced here: 1760 us
  waiting for transfers between devices  1300 us (73%)
  other arithmetic  161 us (9%)
  matrix products  106 us (6%)
  local copies, waits for them, and re-layouts  87.1 us (5%)
  blocking collectives  82.5 us (5%)
  between operations  22 us (1%)
    psum x3, waiting for transfers between devices, sum_heads_back(): return lax.psum(values, 'head')  310 us
    reduce_scatter x1, waiting for transfers between devices, local(): lax.psum_scatter(grad_table, 'head', scatter_dimension=1, tiled=True)  268 us
    psum x2, waiting for transfers between devices, sum_heads_fwd(): return lax.psum(values, 'head')  239 us
    reduce_scatter x1, waiting for transfers between devices, local(): lax.psum_scatter((table_rows * inside[:, None]).astype(jnp.bfloat16), 'se...  83.2 us
    dot_general x19, matrix products, contract_dims(): lax.dot_general(left_side, right_side, (((left_dim,), (right_dim,)), ((),...  71.7 us
    reduce_scatter x1, waiting for transfers between devices, local(): lax.psum_scatter(stacked[0], 'seq', scatter_dimension=1, tiled=True)  62.3 us
    reduce_scatter x1, waiting for transfers between devices, local(): lax.psum_scatter(stacked[2], 'seq', scatter_dimension=1, tiled=True)  51.8 us
    all_gather x2, waiting for transfers between devices, prefix(): pieces = jax.tree.map(lambda part: lax.all_gather(part, axis), value)  49.6 us
  transfers between devices with their start and end apart: 21, of which 20 were waited for; matrix products, arithmetic and copies ran while one was open for 8% of the time, Pallas kernels for 0%

commit v1 on v0

v1 whole, which is shorter than its diff:
```python
import functools
import jax
import jax.numpy as jnp
from jax import lax
from jax.experimental import pallas as pl
from jax.experimental.pallas import tpu as pltpu
from jax.sharding import PartitionSpec as P

MESH = pl.DeviceIdType.MESH
ANY = pl.BlockSpec(memory_space=pl.ANY)
WHOLE = pl.BlockSpec(memory_space=pltpu.VMEM)


def greet(targets):
    barrier = pltpu.get_barrier_semaphore()
    for target in targets:
        pl.semaphore_signal(barrier, inc=1, device_id=target, device_id_type=MESH)
    pl.semaphore_wait(barrier, len(targets))


def push(src, dst, sends, recvs, at, target):
    copy = pltpu.make_async_remote_copy(
        src_ref=src,
        dst_ref=dst,
        send_sem=sends.at[at],
        recv_sem=recvs.at[at],
        device_id=target,
        device_id_type=MESH,
    )
    copy.start()
    return copy


def call(body, outs, in_specs, out_specs, scratch, cid, args, sent=0, name=None):
    return pl.pallas_call(
        body,
        out_shape=outs,
        in_specs=in_specs,
        out_specs=out_specs,
        scratch_shapes=scratch,
        compiler_params=pltpu.CompilerParams(
            collective_id=cid, has_side_effects=True, vmem_limit_bytes=48 * 2**20
        ),
        cost_estimate=pl.CostEstimate(flops=0, bytes_accessed=sent * 40 + 2**20, transcendentals=0),
        name=name,
    )(*args)


def z_ag(x, H, cid):
    def body(x_ref, o_ref, sends, recvs, own):
        h = lax.axis_index("head")
        peers = [{"head": lax.rem(h + k, H)} for k in range(1, H)]
        mine = pltpu.make_async_copy(x_ref, o_ref.at[h], own)
        mine.start()
        greet(peers)
        copies = [push(x_ref, o_ref.at[h], sends, recvs, k, peers[k]) for k in range(H - 1)]
        for copy in copies:
            copy.wait()
        mine.wait()

    return call(
        body,
        jax.ShapeDtypeStruct((H,) + x.shape, x.dtype),
        [ANY],
        ANY,
        [pltpu.SemaphoreType.DMA((H - 1,)), pltpu.SemaphoreType.DMA((H - 1,)), pltpu.SemaphoreType.DMA],
        cid,
        (x,),
        sent=x.size * 2 * (H - 1),
        name="z_ag",
    )


def z_rs(x, H, cid):
    R, C = x.shape[1:]

    def body(x_ref, o_ref, held, sends, recvs, own):
        h = lax.axis_index("head")
        peers = [{"head": lax.rem(h + k, H)} for k in range(1, H)]
        mine = pltpu.make_async_copy(x_ref.at[h], held.at[0], own)
        mine.start()
        greet(peers)
        copies = [
            push(x_ref.at[lax.rem(h + k, H)], held.at[k], sends, recvs, k - 1, peers[k - 1])
            for k in range(1, H)
        ]
        mine.wait()
        for copy in copies:
            copy.wait()
        step = min(R, 32)

        def rows(i, carry):
            at = pl.ds(pl.multiple_of(i * step, step), step)
            total = held[0, at, :].astype(jnp.float32)
            for k in range(1, H):
                total = total + held[k, at, :].astype(jnp.float32)
            o_ref[at, :] = total
            return carry

        lax.fori_loop(0, R // step, rows, 0)

    return call(
        body,
        jax.ShapeDtypeStruct((R, C), jnp.float32),
        [ANY],
        WHOLE,
        [
            pltpu.VMEM((H, R, C), x.dtype),
            pltpu.SemaphoreType.DMA((H - 1,)),
            pltpu.SemaphoreType.DMA((H - 1,)),
            pltpu.SemaphoreType.DMA,
        ],
        cid,
        (x,),
        sent=R * C * 2 * (H - 1),
        name="z_rs",
    )


def p_ag(x, S, cid):
    N = S // 2

    def body(x_ref, o_ref, sends, recvs, fsends, frecvs, own):
        s = lax.axis_index("seq")
        sib = {"seq": s + 1 - 2 * lax.rem(s, 2)}
        peers = [{"seq": lax.rem(s + 2 * k, S)} for k in range(1, N)]
        mine = pltpu.make_async_copy(x_ref, o_ref.at[s], own)
        mine.start()
        greet(peers + [sib])
        copies = [push(x_ref, o_ref.at[s], sends, recvs, k, peers[k]) for k in range(N - 1)]
        copies.append(push(x_ref, o_ref.at[s], sends, recvs, N - 1, sib))
        passed = []
        for k in range(1, N):
            copies[k - 1].wait_recv()
            source = lax.rem(s - 2 * k + 2 * S, S)
            passed.append(push(o_ref.at[source], o_ref.at[source], fsends, frecvs, k - 1, sib))
        copies[N - 1].wait_recv()
        for copy in copies:
            copy.wait_send()
        for copy in passed:
            copy.wait()
        mine.wait()

    return call(
        body,
        jax.ShapeDtypeStruct((S,) + x.shape, x.dtype),
        [ANY],
        ANY,
        [
            pltpu.SemaphoreType.DMA((N,)),
            pltpu.SemaphoreType.DMA((N,)),
            pltpu.SemaphoreType.DMA((N - 1,)),
            pltpu.SemaphoreType.DMA((N - 1,)),
            pltpu.SemaphoreType.DMA,
        ],
        cid,
        (x,),
        sent=x.size * 2 * N,
        name="p_ag",
    )


def p_rs(x, S, cid):
    N = S // 2
    R, C = x.shape[1:]
    step = min(R, 32)

    def body(x_ref, o_ref, sib_held, own_held, out_held, held, sends, recvs, csends, crecvs, own):
        s = lax.axis_index("seq")
        parity = lax.rem(s, 2)
        sib = {"seq": s + 1 - 2 * parity}
        peers = [{"seq": lax.rem(s + 2 * k, S)} for k in range(1, N)]
        mine = []
        for k in range(N):
            owner = lax.rem(s + 2 * k, S)
            mine.append(pltpu.make_async_copy(x_ref.at[owner], own_held.at[k], own.at[k]))
            mine[-1].start()
        greet(peers + [sib])
        order = list(range(1, N)) + [0]
        swaps = {}
        for k in order:
            owner = lax.rem(s + 2 * k, S) + 1 - 2 * parity
            swaps[k] = push(x_ref.at[owner], sib_held.at[k], csends, crecvs, k, sib)
        copies = []
        for k in order:
            mine[k].wait()
            swaps[k].wait_recv()

            def rows(i, carry, k=k):
                at = pl.ds(pl.multiple_of(i * step, step), step)
                total = own_held[k, at, :].astype(jnp.float32) + sib_held[k, at, :].astype(jnp.float32)
                if k == 0:
                    o_ref[at, :] = total
                else:
                    out_held[k - 1, at, :] = total.astype(x.dtype)
                return carry

            lax.fori_loop(0, R // step, rows, 0)
            if k > 0:
                copies.append(push(out_held.at[k - 1], held.at[k - 1], sends, recvs, k - 1, peers[k - 1]))
        for copy in copies:
            copy.wait()
        for k in order:
            swaps[k].wait_send()

        def total_rows(i, carry):
            at = pl.ds(pl.multiple_of(i * step, step), step)
            total = o_ref[at, :]
            for k in range(N - 1):
                total = total + held[k, at, :].astype(jnp.float32)
            o_ref[at, :] = total
            return carry

        lax.fori_loop(0, R // step, total_rows, 0)

    return call(
        body,
        jax.ShapeDtypeStruct((R, C), jnp.float32),
        [ANY],
        WHOLE,
        [
            pltpu.VMEM((N, R, C), x.dtype),
            pltpu.VMEM((N, R, C), x.dtype),
            pltpu.VMEM((N - 1, R, C), x.dtype),
            pltpu.VMEM((N - 1, R, C), x.dtype),
            pltpu.SemaphoreType.DMA((N - 1,)),
            pltpu.SemaphoreType.DMA((N - 1,)),
            pltpu.SemaphoreType.DMA((N,)),
            pltpu.SemaphoreType.DMA((N,)),
            pltpu.SemaphoreType.DMA((N,)),
        ],
        cid,
        (x,),
        sent=R * C * 2 * N,
        name="p_rs",
    )


def all_sum(x, S, H, cid):
    def body(x_ref, o_ref, first, middle, second, sends, recvs, zsends, zrecvs):
        s, h = lax.axis_index("seq"), lax.axis_index("head")
        peers = [{"seq": lax.rem(s + k, S)} for k in range(1, S)]
        heads = [{"head": lax.rem(h + k, H)} for k in range(1, H)]
        greet(peers + heads)
        copies = [push(x_ref, first.at[s], sends, recvs, k, peers[k]) for k in range(S - 1)]
        first[s] = x_ref[...]
        for copy in copies:
            copy.wait()
        total = first[0]
        for k in range(1, S):
            total = total + first[k]
        middle[...] = total
        copies = [push(middle, second.at[h], zsends, zrecvs, k, heads[k]) for k in range(H - 1)]
        second[h] = total
        for copy in copies:
            copy.wait()
        total = second[0]
        for k in range(1, H):
            total = total + second[k]
        o_ref[...] = total

    return call(
        body,
        jax.ShapeDtypeStruct(x.shape, x.dtype),
        [WHOLE],
        WHOLE,
        [
            pltpu.VMEM((S,) + x.shape, x.dtype),
            pltpu.VMEM(x.shape, x.dtype),
            pltpu.VMEM((H,) + x.shape, x.dtype),
            pltpu.SemaphoreType.DMA((S - 1,)),
            pltpu.SemaphoreType.DMA((S - 1,)),
            pltpu.SemaphoreType.DMA((H - 1,)),
            pltpu.SemaphoreType.DMA((H - 1,)),
        ],
        cid,
        (x,),
        sent=x.size * 4 * (S + H),
        name="all_sum",
    )


KD = 256
VD = 512
STEP = 10

NORM_EPS = 1e-05
BETA_ONE = 0.9
BETA_TWO = 0.999
ADAM_EPS = 1e-08
DECAY_WT = 0.01
LEARN_RATE = 0.2
TRUST_EPSILON = 1e-06


def contract_dims(left_side, right_side, left_dim, right_dim):
    return lax.dot_general(
        left_side,
        right_side,
        (((left_dim,), (right_dim,)), ((), ())),
        preferred_element_type=jnp.float32,
    )


def matmul(left_side, right_side):
    return jnp.dot(left_side, right_side, preferred_element_type=jnp.float32)


def centre(values):
    centred = values - jnp.mean(values, axis=-1, keepdims=True)
    return centred * lax.rsqrt(jnp.mean(centred * centred, axis=-1, keepdims=True) + NORM_EPS)


def row_scale(values):
    centred = values - jnp.mean(values, axis=-1, keepdims=True)
    return lax.rsqrt(jnp.mean(centred * centred, axis=-1, keepdims=True) + NORM_EPS)


def norm_back(values, gain_row, grad):
    hat, scale = centre(values), row_scale(values)
    scaled = grad * gain_row
    mean_one = jnp.mean(scaled, axis=-1, keepdims=True)
    mean_two = jnp.mean(scaled * hat, axis=-1, keepdims=True)
    return scale * (scaled - mean_one - hat * mean_two), jnp.sum(grad * hat, axis=0)


def rotary_tables(positions):
    halfway = KD // 2
    frequency = jnp.exp(-jnp.log(10000.0) * jnp.arange(halfway).astype(jnp.float32) / halfway)
    phases = positions.astype(jnp.float32)[:, None] * frequency[None, :]
    return (jnp.cos(phases), jnp.sin(phases))


def rotate(values, cosines, sines):
    halfway = values.shape[-1] // 2
    leading = values[..., :halfway]
    trailing = values[..., halfway:]
    return jnp.concatenate(
        [leading * cosines - trailing * sines, leading * sines + trailing * cosines], axis=-1
    )


def rotate_back(grads, cosines, sines):
    return rotate(grads, cosines, -sines)


def gate_norm(gate_pre, retained):
    scaled = retained * lax.rsqrt(jnp.mean(retained * retained, axis=-1, keepdims=True) + NORM_EPS)
    return gate_pre * jax.nn.sigmoid(gate_pre) * scaled


def gelu_gate(gate_part, up_part):
    return jax.nn.gelu(gate_part) * up_part


def lamb_parts(weight, moment, second, grad):
    new_moment = BETA_ONE * moment + (1.0 - BETA_ONE) * grad
    new_second = BETA_TWO * second + (1.0 - BETA_TWO) * grad * grad
    moment_hat = new_moment / (1.0 - BETA_ONE**STEP)
    second_hat = new_second / (1.0 - BETA_TWO**STEP)
    ratio = moment_hat / (jnp.sqrt(second_hat) + ADAM_EPS) + DECAY_WT * weight
    return (new_moment, new_second, ratio)


def shift(value, axis, by):
    count = lax.axis_size(axis)
    return lax.ppermute(value, axis, [(i, (i + by) % count) for i in range(count)])


def head_gather(value):
    return [value] + [shift(value, "head", k) for k in range(1, lax.axis_size("head"))]


def head_sum(pieces_of):
    count, mine = lax.axis_size("head"), lax.axis_index("head")
    total = pieces_of(mine).astype(jnp.float32)
    for k in range(1, count):
        piece = pieces_of(lax.rem(mine + k, count)).astype(jnp.bfloat16)
        total = total + shift(piece, "head", k).astype(jnp.float32)
    return total


def in_order(pieces):
    count, mine = len(pieces), lax.axis_index("head")
    rows = pieces[0].shape[0]
    whole = jnp.zeros((count * rows,) + pieces[0].shape[1:], pieces[0].dtype)
    for k, piece in enumerate(pieces):
        at = lax.rem(mine - k + count, count) * rows
        whole = lax.dynamic_update_slice_in_dim(whole, piece, at, 0)
    return whole


def local(
    token_ids,
    completion,
    decay_rate,
    w_mixer,
    w_output,
    w_expand,
    w_contract,
    norm_gains,
    embedding,
    mom_mixer,
    var_mixer,
    mom_output,
    var_output,
    mom_expand,
    var_expand,
    mom_contract,
    var_contract,
    mom_gains,
    var_gains,
    mom_embed,
    var_embed,
):
    bf, f32 = jnp.bfloat16, jnp.float32
    s, h = lax.axis_index("seq"), lax.axis_index("head")
    S, H = lax.axis_size("seq"), lax.axis_size("head")
    total_tokens = token_ids.shape[0]
    span = total_tokens // S
    vocab_part, width = embedding.shape
    quarter = width // H
    cap = span // 2
    own = cap // H
    rows_own = span // H
    assert w_mixer.shape[0] == 1
    token_start = s * span
    vocab_start = s * vocab_part

    mixer = lax.all_gather(w_mixer[0], "seq", axis=0, tiled=True)
    output = lax.all_gather(w_output[0], "seq", axis=1, tiled=True)
    expand = lax.all_gather(w_expand[0], "seq", axis=0, tiled=True)
    contract = lax.all_gather(w_contract[0], "seq", axis=1, tiled=True)
    small = jnp.concatenate([norm_gains.astype(f32), mom_gains, var_gains], axis=0)
    small = jnp.concatenate([small, jnp.zeros((16 - small.shape[0], small.shape[1]), f32)], axis=0)
    small_all = p_ag(small, S, 1).transpose(1, 0, 2).reshape(16, width)
    gains, mom_gains_all, var_gains_all = small_all[:3], small_all[3:6], small_all[6:9]

    ids_grid = token_ids.reshape(S, H, rows_own)
    ids_own = lax.dynamic_index_in_dim(ids_grid, h, 1, keepdims=False)
    chosen = ids_own.reshape(-1) - vocab_start
    inside = (chosen >= 0) & (chosen < vocab_part)
    found = jnp.take(embedding, jnp.clip(chosen, 0, vocab_part - 1), axis=0)
    found = jnp.where(inside[:, None], found, jnp.zeros((), bf))
    rows = p_rs(found.reshape(S, rows_own, width), S, 2).astype(bf)
    x0 = in_order(head_gather(rows))

    mask_own = lax.dynamic_slice_in_dim(completion, token_start, span)
    slot_of = jnp.where(mask_own == 1, jnp.cumsum(mask_own) - 1, -1)
    picker = (slot_of[None, :] == jnp.arange(cap)[:, None]).astype(bf)
    place = jnp.sum(
        jnp.where(slot_of[None, :] == jnp.arange(cap)[:, None], jnp.arange(span)[None, :], 0), axis=1
    )
    mask_grid = completion.reshape(S, span)
    next_ids = jnp.roll(token_ids, -1).reshape(S, span)
    live = (completion * (jnp.arange(total_tokens) < total_tokens - 1)).reshape(S, span)
    slot_grid = jnp.where(mask_grid == 1, jnp.cumsum(mask_grid, axis=1) - 1, -1)
    matches = slot_grid[:, None, :] == jnp.arange(cap)[None, :, None]
    targets = jnp.sum(jnp.where(matches, next_ids[:, None, :], 0), axis=-1)
    row_weights = jnp.sum(jnp.where(matches, live[:, None, :], 0), axis=-1).astype(f32)
    count_live = jnp.sum(live).astype(f32)

    def of_quarter(grid, head):
        return lax.dynamic_index_in_dim(grid.reshape(S, H, own), head, 1, keepdims=False).reshape(-1)

    rate = decay_rate[0, 0]
    steps_in = jnp.arange(span).astype(f32)
    offsets = place[:, None].astype(f32) - steps_in[None, :]
    within = jnp.where(offsets >= 0, jnp.exp(-rate * jnp.maximum(offsets, 0.0)), 0.0)
    tail_decay = jnp.exp(-rate * (span - 1.0 - steps_in))[:, None]
    lead_decay = jnp.exp(-rate * (place.astype(f32) + 1.0))[:, None]
    cosines, sines = rotary_tables(token_start + jnp.arange(span))
    cosines_q, sines_q = rotary_tables(token_start + place)

    def state_sum(update, cid, backward):
        everyone = p_ag(update.astype(bf), S, cid)
        position = jnp.arange(S)
        gap = position - s - 1 if backward else s - 1 - position
        factor = jnp.where(gap >= 0, jnp.exp(-rate * span * jnp.maximum(gap, 0).astype(f32)), 0.0)
        return jnp.sum(everyone.astype(f32) * factor[:, None, None], axis=0).astype(bf)

    hat0 = centre(x0.astype(f32))
    normed = (hat0 * gains[0]).astype(bf)
    proj_kv = matmul(normed, mixer[:, KD : 2 * KD + VD])
    keys = (rotate(proj_kv[:, :KD], cosines, sines) * KD ** (-0.5)).astype(bf)
    values = proj_kv[:, KD:].astype(bf)
    weighted = (keys.astype(f32) * tail_decay).astype(bf)
    update = contract_dims(weighted, values, 0, 0)
    state = state_sum(update, 3, False)
    normed_q = matmul(picker, normed).astype(bf)
    query = rotate(matmul(normed_q, mixer[:, :KD]), cosines_q, sines_q).astype(bf)
    gate_pre = matmul(normed_q, mixer[:, 2 * KD + VD :])
    scores = contract_dims(query, keys, 1, 1)
    weights_blk = (scores * within).astype(bf)
    inner_part = matmul(weights_blk, values)
    retained = inner_part + lead_decay * matmul(query, state)
    gated = gate_norm(gate_pre, retained).astype(bf)

    def own_rows(value):
        return lambda head: lax.dynamic_slice_in_dim(value, head * own, own, 0)

    picker_own = own_rows(picker)(h)
    x0_own = matmul(picker_own, x0)
    x1 = x0_own + head_sum(own_rows(matmul(gated, output)))
    normed_b_own = (centre(x1) * gains[1]).astype(bf)
    normed_b = in_order(head_gather(normed_b_own))
    gate_up = matmul(normed_b, expand)
    width_ff = gate_up.shape[1] // 2
    hidden = gelu_gate(gate_up[:, :width_ff], gate_up[:, width_ff:]).astype(bf)
    x2 = x1 + head_sum(own_rows(matmul(hidden, contract)))
    final_own = (centre(x2) * gains[2]).astype(bf)

    final_rows = p_ag(final_own, S, 4).reshape(S * own, width)
    logits = contract_dims(final_rows, embedding, 1, 1)
    peak = jnp.max(logits, axis=-1)
    exp_total = jnp.sum(jnp.exp(logits - peak[:, None]), axis=-1)
    stats = p_ag(jnp.stack([peak, exp_total]).reshape(-1, 128), S, 5).reshape(S, 2, S * own)
    peak_all = jnp.max(stats[:, 0], axis=0)
    total_all = jnp.sum(stats[:, 1] * jnp.exp(stats[:, 0] - peak_all), axis=0)
    log_total = peak_all + jnp.log(total_all)

    def logits_grad(logits, log_total, head):
        scale = of_quarter(row_weights, head) / count_live
        local_target = of_quarter(targets, head) - vocab_start
        hit = jnp.arange(vocab_part)[None, :] == local_target[:, None]
        grads = jnp.exp(logits - log_total[:, None]) - hit.astype(f32)
        return (grads * scale[:, None]).astype(bf), hit, scale

    grad_logits, hit, scale_row = logits_grad(logits, log_total, h)
    target_logit = jnp.sum(jnp.where(hit, logits, 0.0), axis=-1)
    shard_loss = jnp.sum(scale_row * log_total) * (s == 0).astype(f32) - jnp.sum(
        scale_row * target_logit
    )
    grad_final = p_rs(matmul(grad_logits, embedding).astype(bf).reshape(S, own, width), S, 6)
    grad_x2, grad_gain_final = norm_back(x2, gains[2], grad_final)

    row_pieces = head_gather(final_rows)
    log_pieces = head_gather(log_total.reshape(-1, 128))

    def own_columns(value):
        return lax.dynamic_slice_in_dim(value, h * quarter, quarter, 1)

    grad_table = contract_dims(grad_logits, own_columns(final_rows), 0, 0)
    for k in range(1, H):
        there = lax.rem(h - k + H, H)
        logits_k = contract_dims(row_pieces[k], embedding, 1, 1)
        grads_k = logits_grad(logits_k, log_pieces[k].reshape(-1), there)[0]
        grad_table = grad_table + contract_dims(grads_k, own_columns(row_pieces[k]), 0, 0)

    grad_branch = in_order(head_gather(grad_x2.astype(bf)))
    grad_hidden = contract_dims(grad_branch, contract, 1, 1)
    grad_contract = contract_dims(hidden, grad_branch, 0, 0)
    _, gelu_back = jax.vjp(gelu_gate, gate_up[:, :width_ff], gate_up[:, width_ff:])
    grad_gate_up = jnp.concatenate(gelu_back(grad_hidden), axis=1).astype(bf)
    grad_expand = contract_dims(normed_b, grad_gate_up, 0, 0)
    grad_normed_b = head_sum(own_rows(contract_dims(grad_gate_up, expand, 1, 1)))
    grad_x1, grad_gain_b = norm_back(x1, gains[1], grad_normed_b)
    grad_x1 = grad_x1 + grad_x2
    grad_attn = in_order(head_gather(grad_x1.astype(bf)))
    grad_gated = contract_dims(grad_attn, output, 1, 1)
    grad_output = contract_dims(gated, grad_attn, 0, 0)
    _, gate_back = jax.vjp(gate_norm, gate_pre, retained)
    grad_gate_pre, grad_ret = gate_back(grad_gated)
    grad_cross = (lead_decay * grad_ret).astype(bf)
    grad_ret = grad_ret.astype(bf)
    grad_state = contract_dims(query, grad_cross, 0, 0)
    grad_update = state_sum(grad_state, 7, True)
    grad_weights = contract_dims(grad_ret, values, 1, 1)
    grad_scores = (grad_weights * within).astype(bf)
    grad_query = matmul(grad_scores, keys) + contract_dims(grad_cross, state, 1, 1)
    grad_keys = contract_dims(grad_scores, query, 0, 0)
    grad_values = contract_dims(weights_blk, grad_ret, 0, 0) + matmul(weighted, grad_update)
    grad_keys = grad_keys + contract_dims(values, grad_update, 1, 1) * tail_decay
    grad_q_pre = rotate_back(grad_query, cosines_q, sines_q).astype(bf)
    grad_k_pre = rotate_back(grad_keys * KD ** (-0.5), cosines, sines).astype(bf)
    grad_qg = contract_dims(
        picker, jnp.concatenate([grad_q_pre, grad_gate_pre.astype(bf)], axis=1), 0, 0
    ).astype(bf)
    grad_proj = jnp.concatenate(
        [grad_qg[:, :KD], grad_k_pre, grad_values.astype(bf), grad_qg[:, KD:]], axis=1
    )
    grad_normed = contract_dims(grad_proj, mixer, 1, 1)
    grad_mixer = contract_dims(normed, grad_proj, 0, 0)

    scaled = grad_normed * gains[0]
    row_sums = jnp.stack([jnp.sum(scaled, axis=1), jnp.sum(scaled * hat0, axis=1)]).reshape(-1, 128)
    row_sums = sum(head_gather(row_sums)).reshape(2, span, 1) / width
    columns = head_sum(lambda head: lax.dynamic_slice_in_dim(grad_normed, head * quarter, quarter, 1))
    hat_cols = own_columns(hat0)
    gain_cols = lax.dynamic_slice_in_dim(gains[0], h * quarter, quarter, 0)
    grad_gain_a = jnp.sum(columns * hat_cols, axis=0)
    grad_in = row_scale(x0.astype(f32)) * (columns * gain_cols - row_sums[0] - hat_cols * row_sums[1])
    grad_in = grad_in + contract_dims(picker, own_columns(grad_attn), 0, 0)
    piece_rows = p_ag(grad_in.astype(bf), S, 8).reshape(total_tokens, quarter)
    local_id = token_ids - vocab_start
    one_hot = (jnp.arange(vocab_part)[:, None] == local_id[None, :]).astype(bf)
    grad_table = grad_table + matmul(one_hot, piece_rows)

    def scattered(value, dim):
        return lax.psum_scatter(value.astype(bf), "seq", scatter_dimension=dim, tiled=True).astype(f32)[None]

    grad_contract = scattered(grad_contract, 1)
    grad_expand = scattered(grad_expand, 0)
    grad_output = scattered(grad_output, 1)
    grad_mixer = scattered(grad_mixer, 0)
    grad_gains = jnp.stack(
        [lax.dynamic_update_slice_in_dim(jnp.zeros((width,), f32), grad_gain_a, h * quarter, 0), grad_gain_b, grad_gain_final]
    )

    mixer_f = w_mixer.astype(f32)
    output_f = w_output.astype(f32)
    expand_f = w_expand.astype(f32)
    contract_f = w_contract.astype(f32)
    table_own = own_columns(embedding).astype(f32)
    parts = [
        lamb_parts(mixer_f, mom_mixer, var_mixer, grad_mixer),
        lamb_parts(output_f, mom_output, var_output, grad_output),
        lamb_parts(expand_f, mom_expand, var_expand, grad_expand),
        lamb_parts(contract_f, mom_contract, var_contract, grad_contract),
        lamb_parts(table_own, mom_embed, var_embed, grad_table),
    ]
    held = [mixer_f, output_f, expand_f, contract_f, table_own]
    sums = jnp.stack(
        [jnp.sum(w * w) for w in held] + [jnp.sum(p[2] * p[2]) for p in parts] + [shard_loss]
    )
    packed = jnp.concatenate([jnp.pad(sums, (0, 1024 - sums.shape[0])).reshape(8, 128), grad_gains.reshape(-1, 128)])
    packed = all_sum(packed, S, H, 9)
    sums = packed[0]
    grad_gains = packed[8:].reshape(3, width)
    part_gains = lamb_parts(gains, mom_gains_all, var_gains_all, grad_gains)
    weight_squares = jnp.concatenate([sums[:5], jnp.sum(gains * gains, axis=1)])
    ratio_squares = jnp.concatenate([sums[5:10], jnp.sum(part_gains[2] * part_gains[2], axis=1)])
    trust = jnp.sqrt(weight_squares) * lax.rsqrt(ratio_squares + TRUST_EPSILON)
    new_w = [w - LEARN_RATE * trust[i] * parts[i][2] for i, w in enumerate(held)]
    new_gains = gains - LEARN_RATE * trust[5:][:, None] * part_gains[2]

    def own_gains(value):
        return lax.dynamic_slice_in_dim(value, s * (width // S), width // S, 1)

    return (
        sums[10],
        jnp.stack([weight_squares, ratio_squares], axis=1),
        parts[0][0],
        parts[0][1],
        new_w[0],
        parts[1][0],
        parts[1][1],
        new_w[1],
        parts[2][0],
        parts[2][1],
        new_w[2],
        parts[3][0],
        parts[3][1],
        new_w[3],
        own_gains(part_gains[0]),
        own_gains(part_gains[1]),
        own_gains(new_gains),
        parts[4][0],
        parts[4][1],
        new_w[4],
    )


def solution(mesh):
    placed = (
        P(),
        P(),
        P(None, "head"),
        P(None, "seq", "head"),
        P(None, "head", "seq"),
        P(None, "seq", "head"),
        P(None, "head", "seq"),
        P(None, "seq"),
        P("seq", None),
        P(None, "seq", "head"),
        P(None, "seq", "head"),
        P(None, "head", "seq"),
        P(None, "head", "seq"),
        P(None, "seq", "head"),
        P(None, "seq", "head"),
        P(None, "head", "seq"),
        P(None, "head", "seq"),
        P(None, "seq"),
        P(None, "seq"),
        P("seq", "head"),
        P("seq", "head"),
    )
    return jax.shard_map(
        local,
        mesh=mesh,
        in_specs=placed,
        out_specs=(P(), P()) + placed[3:4] * 3 + placed[4:5] * 3 + placed[3:4] * 3 + placed[4:5] * 3 + placed[7:8] * 3 + placed[19:20] * 3,
        check_vma=False,
    )
```

time: 1770 us -> 608 us (0.34)
  waiting for transfers between devices: 1300 us -> 99.5 us
  Pallas kernels: 0 us -> 145 us
  other arithmetic: 161 us -> 56.4 us
  blocking collectives: 82.5 us -> 0 us
  starting transfers between devices: 1.71 us -> 81.1 us
  matrix products: 106 us -> 148 us
  local copies, waits for them, and re-layouts: 87.1 us -> 57.4 us
    reduce_scatter x7 -> x2, waiting for transfers between devices: 567 us -> 0.01 us  [scattered(): lax.psum_scatter(value.astype(bf), 'seq', scatter_dimension=dim, tiled=True)]
    psum x5 -> x0, waiting for transfers between devices: 549 us -> none  [the longest x3 310 us: sum_heads_back(): return lax.psum(values, 'head')]
    pallas_call x0 -> x9, Pallas kernels: none -> 145 us  [call(): pl.pallas_call(body, out_shape=outs, in_specs=in_specs, out_specs=out_spe...]
    all_gather x8 -> x4, waiting for transfers between devices: 143 us -> 0.07 us  [the longest x1 0.02 us: local(): mixer = lax.all_gather(w_mixer[0], 'seq', axis=0, tiled=True)]
    ppermute x0 -> x33, waiting for transfers between devices: none -> 97.2 us  [shift(): lax.ppermute(value, axis, [(i, (i + by) % count) for i in range(count)])]
    ppermute x0 -> x33, starting transfers between devices: none -> 80.2 us  [shift(): lax.ppermute(value, axis, [(i, (i + by) % count) for i in range(count)])]
    psum x1 -> x0, blocking collectives: 41 us -> none  [local(): lax.psum((shard_weight_squares, shard_ratio_squares, shard_loss), ('seq',...]
    gather x3 -> x1, local copies, waits for them, and re-layouts: 49.6 us -> 11.5 us  [local(): found = jnp.take(embedding, jnp.clip(chosen, 0, vocab_part - 1), axis=0)]
  transfers between devices with their start and end apart: 21 -> 41, of which waited for: 20 -> 14; matrix products, arithmetic and copies ran while one was open for 8% -> 32% of each run, Pallas kernels for 0% -> 17%
where the time goes in v1:
time: 608 us; the launch traced here: 609 us
  matrix products  148 us (24%)
  Pallas kernels  145 us (24%)
  waiting for transfers between devices  99.5 us (16%)
  starting transfers between devices  81.1 us (13%)
  local copies, waits for them, and re-layouts  57.4 us (9%)
  other arithmetic  56.4 us (9%)
  between operations  22 us (4%)
    pallas_call x9, Pallas kernels, call(): pl.pallas_call(body, out_shape=outs, in_specs=in_specs, out_specs=out_spe...  145 us
    dot_general x23, matrix products, contract_dims(): lax.dot_general(left_side, right_side, (((left_dim,), (right_dim,)), ((),...  102 us
    ppermute x33, waiting for transfers between devices, shift(): lax.ppermute(value, axis, [(i, (i + by) % count) for i in range(count)])  97.2 us
    ppermute x33, starting transfers between devices, shift(): lax.ppermute(value, axis, [(i, (i + by) % count) for i in range(count)])  80.2 us
    dot_general x14, matrix products, matmul(): return jnp.dot(left_side, right_side, preferred_element_type=jnp.float32)  45.9 us
    unnamed x198, local copies, waits for them, and re-layouts  17.9 us
  transfers between devices with their start and end apart: 41, of which 14 were waited for; matrix products, arithmetic and copies ran while one was open for 32% of the time, Pallas kernels for 17%

profile of v1, /device:TPU:0, one launch (start us, length us, event | category | flops | bytes accessed | tf_op | source)
XLA Modules:
  0.0 609.1 jit_solution(2077780751258688175)
XLA Ops:
  10.5 11.5 %gather_fusion = bf16[1536,1024]{1,0:T(8,128)(2,1)S(1)} fusion(bf16[4000,1024]{1,0:T(8,128)(2,1)} %param.29, s32[2048]{0:T(1024)S(1)} %pad_clamp_fusion), kind=kCustom, calls=%fused_computation | custom fusion | bytes 6297600 | tf_op jit(solution)/shard_map/jit(_take)/gather | solution.py:443
  22.7 33.4 %p_rs.2 = f32[192,1024]{1,0:T(8,128)S(1)} custom-call(bf16[8,192,1024]{2,1,0:T(8,128)(2,1)S(1)} %select_select_fusion.x_ref), custom_call_target="tpu_custom_call" | custom-call | bytes 63963136 | tf_op jit(solution)/shard_map/p_rs/pallas_call | solution.py:35
  70.5 5.5 p_ag.6
  96.9 21.6 %p_ag.7 = bf16[8,256,512]{2,1,0:T(8,128)(2,1)S(1)} custom-call(bf16[256,512]{1,0:T(8,128)(2,1)S(1)} %convolution_convert_fusion.8.x_ref), custom_call_target="tpu_custom_call" | custom-call | bytes 42991616 | tf_op jit(solution)/shard_map/p_ag/pallas_call | solution.py:35
  124.2 9.3 %collective-permute-start.5 = (bf16[96,1024]{1,0:T(8,128)(2,1)S(1)}, bf16[96,1024]{1,0:T(8,128)(2,1)S(1)}, u32[]{:S(2)}, u32[]{:S(2)}) collective-permute-start(bf16[96,1024]{1,0:T(8,128)(2,1)S(1)} %get-tuple-element.97), channel_id=1, source_target_pairs={{0,3},{1,0},{2,1},{3,2},{4,7},{5,4},{6,5},{7,6},{8,11},{9,8},{10,9... | collective-permute-start | bytes 589832 | tf_op jit(solution)/shard_map/ppermute | solution.py:367
  138.9 11.9 %collective-permute-done.4 = bf16[96,1024]{1,0:T(8,128)(2,1)S(1)} collective-permute-done((bf16[96,1024]{1,0:T(8,128)(2,1)S(1)}, bf16[96,1024]{1,0:T(8,128)(2,1)S(1)}, u32[]{:S(2)}, u32[]{:S(2)}) %collective-permute-start.4) | collective-permute-done | bytes 196640 | tf_op jit(solution)/shard_map/ppermute | solution.py:367
  152.1 12.5 %collective-permute-start.6 = (bf16[96,1024]{1,0:T(8,128)(2,1)S(1)}, bf16[96,1024]{1,0:T(8,128)(2,1)S(1)}, u32[]{:S(2)}, u32[]{:S(2)}) collective-permute-start(bf16[96,1024]{1,0:T(8,128)(2,1)S(1)} %get-tuple-element.74), channel_id=1, source_target_pairs={{0,1},{1,2},{2,3},{3,0},{4,5},{5,6},{6,7},{7,4},{8,9},{9,10},{10,1... | collective-permute-start | bytes 589832 | tf_op jit(solution)/shard_map/ppermute | solution.py:367
  174.7 7.4 %collective-permute-done.7 = bf16[96,1024]{1,0:T(8,128)(2,1)S(1)} collective-permute-done((bf16[96,1024]{1,0:T(8,128)(2,1)S(1)}, bf16[96,1024]{1,0:T(8,128)(2,1)S(1)}, u32[]{:S(2)}, u32[]{:S(2)}) %collective-permute-start.7) | collective-permute-done | bytes 196640 | tf_op jit(solution)/shard_map/ppermute | solution.py:367
  189.1 5.6 collective-permute-start.11
  200.1 10.7 %collective-permute-done.10 = bf16[96,1024]{1,0:T(8,128)(2,1)S(1)} collective-permute-done((bf16[96,1024]{1,0:T(8,128)(2,1)S(1)}, bf16[96,1024]{1,0:T(8,128)(2,1)S(1)}, u32[]{:S(2)}, u32[]{:S(2)}) %collective-permute-start.10) | collective-permute-done | bytes 196640 | tf_op jit(solution)/shard_map/ppermute | solution.py:367
  211.4 12.6 %p_ag.8 = bf16[8,96,1024]{2,1,0:T(8,128)(2,1)S(1)} custom-call(bf16[96,1024]{1,0:T(8,128)(2,1)S(1)} %multiply_convert_fusion.10.x_ref), custom_call_target="tpu_custom_call" | custom-call | bytes 32505856 | tf_op jit(solution)/shard_map/p_ag/pallas_call | solution.py:35
  223.9 9.0 %fusion.194 = (f32[768]{0:T(1024)S(1)}, f32[768,4000]{0,1:T(8,128)S(1)}) fusion(bf16[768,1024]{1,0:T(8,128)(2,1)S(1)} %bitcast.199, bf16[4000,1024]{1,0:T(8,128)(2,1)} %param.29), kind=kOutput, calls=%fused_computation.413 | convolution fusion | flops 6294526976 | bytes 22055936 | tf_op jit(solution)/shard_map/dot_general | solution.py:297
  237.5 5.6 p_ag.9
  244.1 12.3 %convolution_convert_fusion.2 = bf16[768,1024]{1,0:T(8,128)(2,1)S(1)} fusion(bf16[4000,1024]{1,0:T(8,128)(2,1)} %param.29, f32[768,4000]{0,1:T(8,128)} %copy-done.6, f32[768]{0:T(1024)S(1)} %div.220, s32[768]{0:T(1024)S(1)} %sub.361, f32[768]{0:T(1024)S(1)} %log_add_fusion), kind=kOutput, calls=%fused_computation.52 | convolution fusion | flops 6310674432 | bytes 22062080 | tf_op jit(solution)/shard_map/dot_general | solution.py:306
  256.4 15.0 %p_rs.3 = f32[96,1024]{1,0:T(8,128)S(1)} custom-call(bf16[8,96,1024]{2,1,0:T(8,128)(2,1)S(1)} %bitcast.204), custom_call_target="tpu_custom_call" | custom-call | bytes 32505856 | tf_op jit(solution)/shard_map/p_rs/pallas_call | solution.py:35
  282.9 7.5 %collective-permute-done.13 = bf16[96,1024]{1,0:T(8,128)(2,1)S(1)} collective-permute-done((bf16[96,1024]{1,0:T(8,128)(2,1)S(1)}, bf16[96,1024]{1,0:T(8,128)(2,1)S(1)}, u32[]{:S(2)}, u32[]{:S(2)}) %collective-permute-start.13) | collective-permute-done | bytes 196640 | tf_op jit(solution)/shard_map/ppermute | solution.py:367
  295.4 6.7 %collective-permute-start.17 = (bf16[96,1024]{1,0:T(8,128)(2,1)}, bf16[96,1024]{1,0:T(8,128)(2,1)}, u32[]{:S(2)}, u32[]{:S(2)}) collective-permute-start(bf16[96,1024]{1,0:T(8,128)(2,1)} %get-tuple-element.91), channel_id=1, source_target_pairs={{0,3},{1,0},{2,1},{3,2},{4,7},{5,4},{6,5},{7,6},{8,11},{9,8},{10,9... | collective-permute-start | bytes 589832 | tf_op jit(solution)/shard_map/ppermute | solution.py:367
  307.8 11.5 %collective-permute-done.16 = bf16[96,1024]{1,0:T(8,128)(2,1)} collective-permute-done((bf16[96,1024]{1,0:T(8,128)(2,1)}, bf16[96,1024]{1,0:T(8,128)(2,1)}, u32[]{:S(2)}, u32[]{:S(2)}) %collective-permute-start.16) | collective-permute-done | bytes 196640 | tf_op jit(solution)/shard_map/ppermute | solution.py:367
  353.4 10.5 %fusion.92 = f32[4000,256]{1,0:T(8,128)} fusion(bf16[768,1024]{1,0:T(8,128)(2,1)S(1)} %bitcast.202, s32[]{:T(128)S(6)} %select_n.169, f32[768,4000]{0,1:T(8,128)} %copy-done.6, f32[768]{0:T(1024)S(1)} %copy-done.83, s32[768]{0:T(1024)S(1)} %copy-done.67, f32[768]{0:T(1024)S(1)} %copy-done.69), kind=kOutput, calls=%fused_computation.182 | convolution fusion | flops 1591296000 | bytes 16789508 | tf_op jit(solution)/shard_map/dot_general | solution.py:297
  374.0 16.7 %p_ag.10 = bf16[8,256,512]{2,1,0:T(8,128)(2,1)S(1)} custom-call(bf16[256,512]{1,0:T(8,128)(2,1)S(1)} %convolution_convert_fusion.7.x_ref), custom_call_target="tpu_custom_call" | custom-call | bytes 42991616 | tf_op jit(solution)/shard_map/p_ag/pallas_call | solution.py:35
  398.7 5.4 multiply_reduce_fusion.4
  408.7 6.3 %convolution_convert_fusion = bf16[1024,1536]{1,0:T(8,128)(2,1)} fusion(bf16[768,1536]{0,1:T(8,128)(2,1)} %copy-done.54, f32[1024]{0:T(1024)S(1)} %bitcast.235, f32[768]{0:T(1024)S(1)} %copy-done.81, f32[768]{0:T(1024)S(1)} %copy-done.65, bf16[768,1024]{1,0:T(8,128)(2,1)S(1)} %constant_dynamic-update-slice_fusion.13), kind=kOutput, calls=%fused_computation.37 | convolution fusion | flops 2421424128 | bytes 7088128 | tf_op jit(solution)/shard_map/dot_general | solution.py:297
  423.3 8.9 %collective-permute-done.29 = bf16[768,256]{1,0:T(8,128)(2,1)S(1)} collective-permute-done((bf16[768,256]{1,0:T(8,128)(2,1)S(1)}, bf16[768,256]{1,0:T(8,128)(2,1)S(1)}, u32[]{:S(2)}, u32[]{:S(2)}) %collective-permute-start.29) | collective-permute-done | bytes 393248 | tf_op jit(solution)/shard_map/ppermute | solution.py:367
  436.5 19.2 %collective-permute-done.28 = bf16[768,256]{1,0:T(8,128)(2,1)S(1)} collective-permute-done((bf16[768,256]{1,0:T(8,128)(2,1)S(1)}, bf16[768,256]{1,0:T(8,128)(2,1)S(1)}, u32[]{:S(2)}, u32[]{:S(2)}) %collective-permute-start.28) | collective-permute-done | bytes 393248 | tf_op jit(solution)/shard_map/ppermute | solution.py:367
  459.3 25.6 %p_ag.11 = bf16[8,768,256]{2,1,0:T(8,128)(2,1)S(1)} custom-call(bf16[768,256]{1,0:T(8,128)(2,1)S(1)} %fusion.26.x_ref), custom_call_target="tpu_custom_call" | custom-call | bytes 63963136 | tf_op jit(solution)/shard_map/p_ag/pallas_call | solution.py:35
  486.6 18.8 %fusion = f32[4000,256]{1,0:T(8,128)} fusion(bf16[6144,256]{1,0:T(8,128)(2,1)S(1)} %bitcast.198, s32[6144]{0:T(1024)S(1)} %broadcast_subtract_fusion), kind=kOutput, calls=%fused_computation.2 | convolution fusion | flops 12607488000 | bytes 7266304 | tf_op jit(solution)/shard_map/dot_general | solution.py:306
  507.9 13.9 %fusion.8 = f32[4000,256]{1,0:T(8,128)} fusion(f32[4000,256]{1,0:T(8,128)} %fusion.92, bf16[768,1024]{1,0:T(8,128)(2,1)} %collective-permute-done.21, bf16[4000,1024]{1,0:T(8,128)(2,1)} %param.29, f32[768]{0:T(1024)S(1)} %div.244, s32[768]{0:T(1024)S(1)} %sub.380, f32[768]{0:T(1024)S(1)} %bitcast.241, s32[]{:T(128)S(6)} %select_n.169), kind=kOutput, calls=%fused_computation.27 | convolution fusion | flops 7883776000 | bytes 18359300 | tf_op jit(solution)/shard_map/dot_general | solution.py:297
  521.8 13.6 %fusion.4 = f32[4000,256]{1,0:T(8,128)} fusion(bf16[768,1024]{1,0:T(8,128)(2,1)} %collective-permute-done.25, bf16[4000,1024]{1,0:T(8,128)(2,1)} %param.29, f32[768]{0:T(1024)S(1)} %div.248, s32[768]{0:T(1024)S(1)} %sub.392, f32[768]{0:T(1024)S(1)} %bitcast.240, s32[]{:T(128)S(6)} %select_n.169), kind=kOutput, calls=%fused_computation.23 | convolution fusion | flops 7882752000 | bytes 14263300 | tf_op jit(solution)/shard_map/dot_general | solution.py:297
  535.5 24.1 %multiply_reduce_fusion.2 = (f32[]{:T(128)}, f32[4000,256]{1,0:T(8,128)}, f32[4000,256]{1,0:T(8,128)}, f32[4000,256]{1,0:T(8,128)}, f32[]{:T(128)}) fusion(bf16[4000,1024]{1,0:T(8,128)(2,1)} %param.29, s32[]{:T(128)S(6)} %select_n.169, f32[4000,256]{1,0:T(8,128)} %param.40, f32[4000,256]{1,0:T(8,128)} %param.41, f32[4000,256]{1,0:T(8,128)} %fusion, ...), kind=kOutput, calls=%fused_computation.33 | convolution fusion | flops 7904256000 | bytes 44984328 | tf_op jit(solution)/shard_map/dot_general | solution.py:297
  570.4 6.5 %stack.92 = f32[11]{0:T(128)S(1)} concatenate(f32[1]{0:T(128)} %bitcast, f32[1]{0:T(128)} %bitcast.1, f32[1]{0:T(128)} %bitcast.2, f32[1]{0:T(128)} %bitcast.3, f32[1]{0:T(128)} %bitcast.4, f32[1]{0:T(128)} %bitcast.24, f32[1]{0:T(128)} %bitcast.27, f32[1]{0:T(128)} %bitcast.30, f32[1]{0:T(128)} %bitcast.33, f32[1]{0:T(128)} %bitcast.41, f32[1]{0:T(128)} %bitcast.42), dimensions={0} | concatenate | bytes 88 | tf_op jit(solution)/shard_map/stack | solution.py:623
  576.8 9.1 %all_sum.1 = f32[32,128]{1,0:T(8,128)S(1)} custom-call(f32[32,128]{1,0:T(8,128)S(1)} %pad_maximum_fusion.5.x_ref), custom_call_target="tpu_custom_call" | custom-call | bytes 8912896 | tf_op jit(solution)/shard_map/all_sum/pallas_call | solution.py:35
  592.0 5.2 convert_subtract_fusion
  (468 shorter events, 193.5 us)
Async XLA Ops:
  7.2 81.6 %all-gather.9.cloned.1.call-start = ((), (), s32[]{:S(2)}) async-start(), calls=%async_computation.6 | async-start | bytes 3538944 | tf_op jit(solution)/shard_map/all_gather | solution.py:430
  7.9 114.2 %all-gather.11.cloned.1.call-start = ((), (), s32[]{:S(2)}) async-start(), calls=%async_computation.7 | async-start | bytes 1179648 | tf_op jit(solution)/shard_map/all_gather | solution.py:431
  8.7 173.5 %all-gather.13.cloned.1.call-start = ((), (), s32[]{:S(2)}) async-start(), calls=%async_computation.8 | async-start | bytes 2359296 | tf_op jit(solution)/shard_map/all_gather | solution.py:432
  9.4 177.7 %all-gather.15.cloned.1.call-start = ((), (), s32[]{:S(2)}) async-start(), calls=%async_computation.9 | async-start | bytes 1179648 | tf_op jit(solution)/shard_map/all_gather | solution.py:433
  56.5 29.3 %collective-permute-start = (bf16[192,1024]{1,0:T(8,128)(2,1)S(1)}, bf16[192,1024]{1,0:T(8,128)(2,1)S(1)}, u32[]{:S(2)}, u32[]{:S(2)}) collective-permute-start(bf16[192,1024]{1,0:T(8,128)(2,1)S(1)} %get-tuple-element.76), channel_id=1, source_target_pairs={{0,1},{1,2},{2,3},{3,0},{4,5},{5,6},{6,7},{7,4},{8,9},{9,10},{10,1... | collective-permute-start | bytes 1179656 | tf_op jit(solution)/shard_map/ppermute | solution.py:367
  58.1 28.6 %collective-permute-start.1 = (bf16[192,1024]{1,0:T(8,128)(2,1)S(1)}, bf16[192,1024]{1,0:T(8,128)(2,1)S(1)}, u32[]{:S(2)}, u32[]{:S(2)}) collective-permute-start(bf16[192,1024]{1,0:T(8,128)(2,1)S(1)} %get-tuple-element.76), channel_id=1, source_target_pairs={{0,2},{1,3},{2,0},{3,1},{4,6},{5,7},{6,4},{7,5},{8,10},{9,11},{10,... | collective-permute-start | bytes 1179656 | tf_op jit(solution)/shard_map/ppermute | solution.py:367
  60.7 26.0 %collective-permute-start.2 = (bf16[192,1024]{1,0:T(8,128)(2,1)S(1)}, bf16[192,1024]{1,0:T(8,128)(2,1)S(1)}, u32[]{:S(2)}, u32[]{:S(2)}) collective-permute-start(bf16[192,1024]{1,0:T(8,128)(2,1)S(1)} %get-tuple-element.76), channel_id=1, source_target_pairs={{0,3},{1,0},{2,1},{3,2},{4,7},{5,4},{6,5},{7,6},{8,11},{9,8},{10,9... | collective-permute-start | bytes 1179656 | tf_op jit(solution)/shard_map/ppermute | solution.py:367
  62.1 497.6 %reduce-scatter.15.cloned.1.call-start = ((), (), s32[]{:S(2)}) async-start(), calls=%async_computation.11 | async-start | bytes 1179648
  124.2 14.7 %collective-permute-start.5 = (bf16[96,1024]{1,0:T(8,128)(2,1)S(1)}, bf16[96,1024]{1,0:T(8,128)(2,1)S(1)}, u32[]{:S(2)}, u32[]{:S(2)}) collective-permute-start(bf16[96,1024]{1,0:T(8,128)(2,1)S(1)} %get-tuple-element.97), channel_id=1, source_target_pairs={{0,3},{1,0},{2,1},{3,2},{4,7},{5,4},{6,5},{7,6},{8,11},{9,8},{10,9... | collective-permute-start | bytes 589832 | tf_op jit(solution)/shard_map/ppermute | solution.py:367
  133.5 17.3 %collective-permute-start.4 = (bf16[96,1024]{1,0:T(8,128)(2,1)S(1)}, bf16[96,1024]{1,0:T(8,128)(2,1)S(1)}, u32[]{:S(2)}, u32[]{:S(2)}) collective-permute-start(bf16[96,1024]{1,0:T(8,128)(2,1)S(1)} %get-tuple-element.98), channel_id=1, source_target_pairs={{0,2},{1,3},{2,0},{3,1},{4,6},{5,7},{6,4},{7,5},{8,10},{9,11},{10,... | collective-permute-start | bytes 589832 | tf_op jit(solution)/shard_map/ppermute | solution.py:367
  133.6 17.3 %collective-permute-start.3 = (bf16[96,1024]{1,0:T(8,128)(2,1)S(1)}, bf16[96,1024]{1,0:T(8,128)(2,1)S(1)}, u32[]{:S(2)}, u32[]{:S(2)}) collective-permute-start(bf16[96,1024]{1,0:T(8,128)(2,1)S(1)} %get-tuple-element.96), channel_id=1, source_target_pairs={{0,1},{1,2},{2,3},{3,0},{4,5},{5,6},{6,7},{7,4},{8,9},{9,10},{10,1... | collective-permute-start | bytes 589832 | tf_op jit(solution)/shard_map/ppermute | solution.py:367
  152.1 22.5 %collective-permute-start.6 = (bf16[96,1024]{1,0:T(8,128)(2,1)S(1)}, bf16[96,1024]{1,0:T(8,128)(2,1)S(1)}, u32[]{:S(2)}, u32[]{:S(2)}) collective-permute-start(bf16[96,1024]{1,0:T(8,128)(2,1)S(1)} %get-tuple-element.74), channel_id=1, source_target_pairs={{0,1},{1,2},{2,3},{3,0},{4,5},{5,6},{6,7},{7,4},{8,9},{9,10},{10,1... | collective-permute-start | bytes 589832 | tf_op jit(solution)/shard_map/ppermute | solution.py:367
  194.7 16.1 %collective-permute-start.10 = (bf16[96,1024]{1,0:T(8,128)(2,1)S(1)}, bf16[96,1024]{1,0:T(8,128)(2,1)S(1)}, u32[]{:S(2)}, u32[]{:S(2)}) collective-permute-start(bf16[96,1024]{1,0:T(8,128)(2,1)S(1)} %get-tuple-element.95), channel_id=1, source_target_pairs={{0,2},{1,3},{2,0},{3,1},{4,6},{5,7},{6,4},{7,5},{8,10},{9,11},{10,... | collective-permute-start | bytes 589832 | tf_op jit(solution)/shard_map/ppermute | solution.py:367
  194.7 16.1 %collective-permute-start.9 = (bf16[96,1024]{1,0:T(8,128)(2,1)S(1)}, bf16[96,1024]{1,0:T(8,128)(2,1)S(1)}, u32[]{:S(2)}, u32[]{:S(2)}) collective-permute-start(bf16[96,1024]{1,0:T(8,128)(2,1)S(1)} %get-tuple-element.93), channel_id=1, source_target_pairs={{0,1},{1,2},{2,3},{3,0},{4,5},{5,6},{6,7},{7,4},{8,9},{9,10},{10,1... | collective-permute-start | bytes 589832 | tf_op jit(solution)/shard_map/ppermute | solution.py:367
  274.8 15.6 %collective-permute-start.13 = (bf16[96,1024]{1,0:T(8,128)(2,1)S(1)}, bf16[96,1024]{1,0:T(8,128)(2,1)S(1)}, u32[]{:S(2)}, u32[]{:S(2)}) collective-permute-start(bf16[96,1024]{1,0:T(8,128)(2,1)S(1)} %get-tuple-element.69), channel_id=1, source_target_pairs={{0,2},{1,3},{2,0},{3,1},{4,6},{5,7},{6,4},{7,5},{8,10},{9,11},{10,... | collective-permute-start | bytes 589832 | tf_op jit(solution)/shard_map/ppermute | solution.py:367
  302.1 17.1 %collective-permute-start.16 = (bf16[96,1024]{1,0:T(8,128)(2,1)}, bf16[96,1024]{1,0:T(8,128)(2,1)}, u32[]{:S(2)}, u32[]{:S(2)}) collective-permute-start(bf16[96,1024]{1,0:T(8,128)(2,1)} %get-tuple-element.92), channel_id=1, source_target_pairs={{0,2},{1,3},{2,0},{3,1},{4,6},{5,7},{6,4},{7,5},{8,10},{9,11},{10,... | collective-permute-start | bytes 589832 | tf_op jit(solution)/shard_map/ppermute | solution.py:367
  302.1 17.1 %collective-permute-start.15 = (bf16[96,1024]{1,0:T(8,128)(2,1)}, bf16[96,1024]{1,0:T(8,128)(2,1)}, u32[]{:S(2)}, u32[]{:S(2)}) collective-permute-start(bf16[96,1024]{1,0:T(8,128)(2,1)} %get-tuple-element.90), channel_id=1, source_target_pairs={{0,1},{1,2},{2,3},{3,0},{4,5},{5,6},{6,7},{7,4},{8,9},{9,10},{10,1... | collective-permute-start | bytes 589832 | tf_op jit(solution)/shard_map/ppermute | solution.py:367
  307.1 255.3 %reduce-scatter.13.cloned.1.call-start = ((), (), s32[]{:S(2)}) async-start(), calls=%async_computation.10 | async-start | bytes 1179648
  323.8 16.5 %collective-permute-start.19 = (bf16[96,1024]{1,0:T(8,128)(2,1)}, bf16[96,1024]{1,0:T(8,128)(2,1)S(1)}, u32[]{:S(2)}, u32[]{:S(2)}) collective-permute-start(bf16[96,1024]{1,0:T(8,128)(2,1)} %get-tuple-element.66), channel_id=1, source_target_pairs={{0,2},{1,3},{2,0},{3,1},{4,6},{5,7},{6,4},{7,5},{8,10},{9,11},{10,... | collective-permute-start | bytes 589832 | tf_op jit(solution)/shard_map/ppermute | solution.py:367
  346.9 218.2 %reduce-scatter.11.cloned.1.call-start = ((), (), s32[]{:S(2)}) async-start(), calls=%async_computation.5 | async-start | bytes 2359296 | tf_op jit(solution)/shard_map/reduce_scatter | solution.py:600
  347.0 174.8 %collective-permute-start.25 = (bf16[768,1024]{1,0:T(8,128)(2,1)S(1)}, bf16[768,1024]{1,0:T(8,128)(2,1)}, u32[]{:S(2)}, u32[]{:S(2)}) collective-permute-start(bf16[768,1024]{1,0:T(8,128)(2,1)S(1)} %bitcast.200), channel_id=1, source_target_pairs={{0,3},{1,0},{2,1},{3,2},{4,7},{5,4},{6,5},{7,6},{8,11},{9,8},{10,9... | collective-permute-start | bytes 4718600 | tf_op jit(solution)/shard_map/ppermute | solution.py:367
  352.2 155.7 %collective-permute-start.21 = (bf16[768,1024]{1,0:T(8,128)(2,1)S(1)}, bf16[768,1024]{1,0:T(8,128)(2,1)}, u32[]{:S(2)}, u32[]{:S(2)}) collective-permute-start(bf16[768,1024]{1,0:T(8,128)(2,1)S(1)} %bitcast.201), channel_id=1, source_target_pairs={{0,1},{1,2},{2,3},{3,0},{4,5},{5,6},{6,7},{7,4},{8,9},{9,10},{10,1... | collective-permute-start | bytes 4718600 | tf_op jit(solution)/shard_map/ppermute | solution.py:367
  366.6 200.6 %reduce-scatter.9.cloned.1.call-start = ((), (), s32[]{:S(2)}) async-start(), calls=%async_computation.4 | async-start | bytes 3538944 | tf_op jit(solution)/shard_map/reduce_scatter | solution.py:600
  404.1 15.0 %collective-permute-start.32 = (f32[12,128]{1,0:T(8,128)S(1)}, f32[12,128]{1,0:T(8,128)S(1)}, u32[]{:S(2)}, u32[]{:S(2)}) collective-permute-start(f32[12,128]{1,0:T(8,128)S(1)} %reshape.514), channel_id=1, source_target_pairs={{0,3},{1,0},{2,1},{3,2},{4,7},{5,4},{6,5},{7,6},{8,11},{9,8},{10,9... | collective-permute-start | bytes 18440 | tf_op jit(solution)/shard_map/ppermute | solution.py:367
  408.0 14.6 %collective-permute-start.31 = (f32[12,128]{1,0:T(8,128)S(1)}, f32[12,128]{1,0:T(8,128)S(1)}, u32[]{:S(2)}, u32[]{:S(2)}) collective-permute-start(f32[12,128]{1,0:T(8,128)S(1)} %reshape.514), channel_id=1, source_target_pairs={{0,2},{1,3},{2,0},{3,1},{4,6},{5,7},{6,4},{7,5},{8,10},{9,11},{10,... | collective-permute-start | bytes 18440 | tf_op jit(solution)/shard_map/ppermute | solution.py:367
  408.0 14.6 %collective-permute-start.30 = (f32[12,128]{1,0:T(8,128)S(1)}, f32[12,128]{1,0:T(8,128)S(1)}, u32[]{:S(2)}, u32[]{:S(2)}) collective-permute-start(f32[12,128]{1,0:T(8,128)S(1)} %reshape.514), channel_id=1, source_target_pairs={{0,1},{1,2},{2,3},{3,0},{4,5},{5,6},{6,7},{7,4},{8,9},{9,10},{10,1... | collective-permute-start | bytes 18440 | tf_op jit(solution)/shard_map/ppermute | solution.py:367
  422.7 33.0 %collective-permute-start.28 = (bf16[768,256]{1,0:T(8,128)(2,1)S(1)}, bf16[768,256]{1,0:T(8,128)(2,1)S(1)}, u32[]{:S(2)}, u32[]{:S(2)}) collective-permute-start(bf16[768,256]{1,0:T(8,128)(2,1)S(1)} %get-tuple-element.82), channel_id=1, source_target_pairs={{0,2},{1,3},{2,0},{3,1},{4,6},{5,7},{6,4},{7,5},{8,10},{9,11},{10,... | collective-permute-start | bytes 1179656 | tf_op jit(solution)/shard_map/ppermute | solution.py:367
  422.7 33.0 %collective-permute-start.27 = (bf16[768,256]{1,0:T(8,128)(2,1)S(1)}, bf16[768,256]{1,0:T(8,128)(2,1)S(1)}, u32[]{:S(2)}, u32[]{:S(2)}) collective-permute-start(bf16[768,256]{1,0:T(8,128)(2,1)S(1)} %get-tuple-element.80), channel_id=1, source_target_pairs={{0,1},{1,2},{2,3},{3,0},{4,5},{5,6},{6,7},{7,4},{8,9},{9,10},{10,1... | collective-permute-start | bytes 1179656 | tf_op jit(solution)/shard_map/ppermute | solution.py:367
  432.2 89.6 %collective-permute-start.26 = (f32[6,128]{1,0:T(8,128)S(1)}, f32[6,128]{1,0:T(8,128)S(1)}, u32[]{:S(2)}, u32[]{:S(2)}) collective-permute-start(f32[6,128]{1,0:T(8,128)S(1)} %bitcast.221), channel_id=1, source_target_pairs={{0,3},{1,0},{2,1},{3,2},{4,7},{5,4},{6,5},{7,6},{8,11},{9,8},{10,9... | collective-permute-start | bytes 9224 | tf_op jit(solution)/shard_map/ppermute | solution.py:367
  455.7 49.7 %collective-permute-start.22 = (f32[6,128]{1,0:T(8,128)S(1)}, f32[6,128]{1,0:T(8,128)S(1)}, u32[]{:S(2)}, u32[]{:S(2)}) collective-permute-start(f32[6,128]{1,0:T(8,128)S(1)} %bitcast.222), channel_id=1, source_target_pairs={{0,1},{1,2},{2,3},{3,0},{4,5},{5,6},{6,7},{7,4},{8,9},{9,10},{10,1... | collective-permute-start | bytes 9224 | tf_op jit(solution)/shard_map/ppermute | solution.py:367
  455.7 79.7 %collective-permute-start.23 = (bf16[768,1024]{1,0:T(8,128)(2,1)S(1)}, bf16[768,1024]{1,0:T(8,128)(2,1)}, u32[]{:S(2)}, u32[]{:S(2)}) collective-permute-start(bf16[768,1024]{1,0:T(8,128)(2,1)S(1)} %bitcast.203), channel_id=1, source_target_pairs={{0,2},{1,3},{2,0},{3,1},{4,6},{5,7},{6,4},{7,5},{8,10},{9,11},{10,... | collective-permute-start | bytes 4718600 | tf_op jit(solution)/shard_map/ppermute | solution.py:367
  505.4 30.0 %collective-permute-start.24 = (f32[6,128]{1,0:T(8,128)S(1)}, f32[6,128]{1,0:T(8,128)S(1)}, u32[]{:S(2)}, u32[]{:S(2)}) collective-permute-start(f32[6,128]{1,0:T(8,128)S(1)} %bitcast.223), channel_id=1, source_target_pairs={{0,2},{1,3},{2,0},{3,1},{4,6},{5,7},{6,4},{7,5},{8,10},{9,11},{10,... | collective-permute-start | bytes 9224 | tf_op jit(solution)/shard_map/ppermute | solution.py:367
  (105 other events, 1357.4 us)
Sparse Core Ops, SparseCore 0:
  9.9 47.6 all-gather.8
  59.5 23.6 all-gather.10
  85.1 33.2 all-gather.12
  120.2 28.0 all-gather.14
  307.2 35.8 reduce-scatter.14
  347.0 39.7 reduce-scatter.12
  390.2 40.4 reduce-scatter.10
  434.0 57.9 reduce-scatter.8

commit v2 on v1

v2 whole, which is shorter than its diff:
```python
import jax
import jax.numpy as jnp
from jax import lax
from jax.experimental import pallas as pl
from jax.experimental.pallas import tpu as pltpu
from jax.sharding import PartitionSpec as P

MESH = pl.DeviceIdType.MESH
ANY = pl.BlockSpec(memory_space=pl.ANY)
WHOLE = pl.BlockSpec(memory_space=pltpu.VMEM)
DMA = pltpu.SemaphoreType.DMA


def push(src, dst, sends, recvs, at, target):
    copy = pltpu.make_async_remote_copy(
        src_ref=src,
        dst_ref=dst,
        send_sem=sends.at[at],
        recv_sem=recvs.at[at],
        device_id=target,
        device_id_type=MESH,
    )
    copy.start()
    return copy


def fetch(src, dst, sems, at):
    copy = pltpu.make_async_copy(src, dst, sems.at[at])
    copy.start()
    return copy


def by_rows(count, step, body):
    def one(i, carry):
        body(pl.ds(pl.multiple_of(i * step, step), step))
        return carry

    lax.fori_loop(0, count // step, one, 0)


def row_step(rows):
    return 32 if rows % 32 == 0 else 16


class Here:
    def __init__(self, S, H):
        self.S, self.H, self.N = S, H, S // 2
        self.s, self.h = lax.axis_index("seq"), lax.axis_index("head")
        self.parity = lax.rem(self.s, 2)

    def head(self, k):
        return lax.rem(self.h + k, self.H)

    def seq(self, k):
        return lax.rem(self.s + 2 * k, self.S)

    def heads(self):
        return [{"head": self.head(k)} for k in range(1, self.H)]

    def chips(self):
        return [{"seq": self.seq(k)} for k in range(1, self.N)]

    def other(self):
        return {"seq": self.s + 1 - 2 * self.parity}


class Task:
    def __init__(self, axis, operands, outs, scratch, run):
        self.axis, self.operands, self.outs, self.scratch, self.run = axis, operands, outs, scratch, run


def fused(cid, S, H, tasks, name):
    operands, outs, specs, scratch = [], [], [], []
    for task in tasks:
        operands += task.operands
        for shape, dtype, spec in task.outs:
            outs.append(jax.ShapeDtypeStruct(shape, dtype))
            specs.append(spec)
        scratch += task.scratch

    def body(*refs):
        here = Here(S, H)
        ins, rest = refs[: len(operands)], refs[len(operands) :]
        results, held = rest[: len(outs)], rest[len(outs) :]
        live = []
        for task in tasks:
            live.append(
                task.run(here, ins[: len(task.operands)], results[: len(task.outs)], held[: len(task.scratch)])
            )
            ins, results, held = ins[len(task.operands) :], results[len(task.outs) :], held[len(task.scratch) :]
        axes = {task.axis for task in tasks}
        targets = []
        if axes & {"head", "both"}:
            targets += here.heads()
        if axes & {"seq", "both"}:
            targets += here.chips() + [here.other()]
        barrier = pltpu.get_barrier_semaphore()
        for target in targets:
            pl.semaphore_signal(barrier, inc=1, device_id=target, device_id_type=MESH)
        for run in live:
            next(run)
        pl.semaphore_wait(barrier, len(targets))
        while live:
            live = [run for run in live if next(run, "end") != "end"]

    got = pl.pallas_call(
        body,
        out_shape=outs,
        in_specs=[ANY] * len(operands),
        out_specs=specs,
        scratch_shapes=scratch,
        compiler_params=pltpu.CompilerParams(
            collective_id=cid, has_side_effects=True, vmem_limit_bytes=56 * 2**20
        ),
        cost_estimate=pl.CostEstimate(flops=0, bytes_accessed=2**25, transcendentals=0),
        name=name,
    )(*operands)
    split = []
    for task in tasks:
        split.append(got[: len(task.outs)])
        got = got[len(task.outs) :]
    return split


def gather_head(x, H):
    def run(here, ins, outs, held):
        (src,), (dst,), (sends, recvs, own) = ins, outs, held
        mine = fetch(src, dst.at[here.h], own, 0)
        yield
        copies = [push(src, dst.at[here.h], sends, recvs, k, to) for k, to in enumerate(here.heads())]
        yield
        for copy in copies:
            copy.wait()
        mine.wait()

    return Task("head", [x], [((H,) + x.shape, x.dtype, ANY)], [DMA((H - 1,)), DMA((H - 1,)), DMA((1,))], run)


def sum_head(x, H, columns=False):
    R, C = (x.shape[0], x.shape[1] // H) if columns else x.shape[1:]

    def run(here, ins, outs, held):
        (src,), (dst,), (got, sends, recvs, own) = ins, outs, held

        def block(i):
            return src.at[:, pl.ds(pl.multiple_of(i * C, C), C)] if columns else src.at[i]

        mine = fetch(block(here.h), got.at[0], own, 0)
        yield
        copies = [
            push(block(here.head(k)), got.at[k], sends, recvs, k - 1, {"head": here.head(k)}) for k in range(1, H)
        ]
        yield
        mine.wait()
        for copy in copies:
            copy.wait()

        def add(rows):
            total = got[0, rows, :].astype(jnp.float32)
            for k in range(1, H):
                total = total + got[k, rows, :].astype(jnp.float32)
            dst[rows, :] = total

        by_rows(R, row_step(R), add)

    return Task(
        "head",
        [x],
        [((R, C), jnp.float32, WHOLE)],
        [pltpu.VMEM((H, R, C), x.dtype), DMA((H - 1,)), DMA((H - 1,)), DMA((1,))],
        run,
    )


def gather_seq(x, S, columns=False, ahead=None):
    N = S // 2
    R, C = x.shape[-2:]

    def run(here, ins, outs, held):
        (src,), (dst,), (sends, recvs, fsends, frecvs, own) = ins, outs, held
        if ahead is not None:
            src = src.at[here.head(ahead)]

        def block(i):
            return dst.at[:, pl.ds(pl.multiple_of(i * C, C), C)] if columns else dst.at[i]

        mine = fetch(src, block(here.s), own, 0)
        yield
        copies = [push(src, block(here.s), sends, recvs, k, to) for k, to in enumerate(here.chips() + [here.other()])]
        passed = []
        for k in range(1, N):
            yield
            copies[k - 1].wait_recv()
            source = lax.rem(here.s - 2 * k + 2 * S, S)
            passed.append(push(block(source), block(source), fsends, frecvs, k - 1, here.other()))
        yield
        copies[N - 1].wait_recv()
        for copy in copies:
            copy.wait_send()
        for copy in passed:
            copy.wait()
        mine.wait()

    shape = (R, S * C) if columns else (S, R, C)
    return Task(
        "seq", [x], [(shape, x.dtype, ANY)], [DMA((N,)), DMA((N,)), DMA((N - 1,)), DMA((N - 1,)), DMA((1,))], run
    )


def sum_seq(x, S, columns=False):
    N = S // 2
    R, C = (x.shape[0], x.shape[1] // S) if columns else x.shape[1:]
    order = list(range(1, N)) + [0]

    def run(here, ins, outs, held):
        (src,), (dst,) = ins, outs
        theirs, ours, out, got, sends, recvs, csends, crecvs, own = held

        def block(i):
            return src.at[:, pl.ds(pl.multiple_of(i * C, C), C)] if columns else src.at[i]

        mine = {k: fetch(block(here.seq(k)), ours.at[k], own, k) for k in order}
        yield
        swaps = {
            k: push(block(here.seq(k) + 1 - 2 * here.parity), theirs.at[k], csends, crecvs, k, here.other())
            for k in order
        }
        copies = []
        for k in order:
            yield
            mine[k].wait()
            swaps[k].wait_recv()

            def add(rows, k=k):
                total = ours[k, rows, :].astype(jnp.float32) + theirs[k, rows, :].astype(jnp.float32)
                if k == 0:
                    dst[rows, :] = total
                else:
                    out[k - 1, rows, :] = total.astype(x.dtype)

            by_rows(R, row_step(R), add)
            if k > 0:
                copies.append(push(out.at[k - 1], got.at[k - 1], sends, recvs, k - 1, {"seq": here.seq(k)}))
        yield
        for copy in copies:
            copy.wait()
        for k in order:
            swaps[k].wait_send()

        def total(rows):
            value = dst[rows, :]
            for k in range(N - 1):
                value = value + got[k, rows, :].astype(jnp.float32)
            dst[rows, :] = value

        by_rows(R, row_step(R), total)

    blocks = lambda count: pltpu.VMEM((count, R, C), x.dtype)
    return Task(
        "seq",
        [x],
        [((R, C), jnp.float32, WHOLE)],
        [blocks(N), blocks(N), blocks(N - 1), blocks(N - 1)]
        + [DMA((N - 1,)), DMA((N - 1,)), DMA((N,)), DMA((N,)), DMA((N,))],
        run,
    )


def lookup(x, S, H, parts):
    N = S // 2
    R, C = x.shape[1:]
    piece = R // parts
    order = list(range(1, N)) + [0]

    def run(here, ins, outs, held):
        (src,), (dst,) = ins, outs
        theirs, ours, out, got, sends, recvs, csends, crecvs, zsends, zrecvs, own, left = held
        mine, swaps, copies, spread, kept = {}, {}, {}, [], []
        for q in range(parts):
            rows = pl.ds(q * piece, piece)
            for k in order:
                mine[q, k] = fetch(src.at[here.seq(k), rows], ours.at[k, rows], own, q * N + k)
        yield
        for q in range(parts):
            rows = pl.ds(q * piece, piece)
            for k in order:
                swaps[q, k] = push(
                    src.at[here.seq(k) + 1 - 2 * here.parity, rows],
                    theirs.at[k, rows],
                    csends,
                    crecvs,
                    q * N + k,
                    here.other(),
                )

        def first(q):
            for k in order:
                mine[q, k].wait()
                swaps[q, k].wait_recv()
                for at in range(q * piece, (q + 1) * piece, 16):
                    rows = pl.ds(at, 16)
                    total = ours[k, rows, :] + theirs[k, rows, :]
                    if k == 0:
                        ours[k, rows, :] = total
                    else:
                        out[k - 1, rows, :] = total
                if k > 0:
                    rows = pl.ds(q * piece, piece)
                    copies[q, k] = push(
                        out.at[k - 1, rows],
                        got.at[k - 1, rows],
                        sends,
                        recvs,
                        q * (N - 1) + k - 1,
                        {"seq": here.seq(k)},
                    )

        def second(q):
            for k in range(1, N):
                copies[q, k].wait_recv()
            for at in range(q * piece, (q + 1) * piece, 16):
                rows = pl.ds(at, 16)
                total = ours[0, rows, :]
                for k in range(1, N):
                    total = total + got[k - 1, rows, :]
                ours[0, rows, :] = total
            rows = pl.ds(q * piece, piece)
            kept.append(fetch(ours.at[0, rows], dst.at[here.h, rows], left, q))
            for k in range(1, H):
                spread.append(
                    push(
                        ours.at[0, rows],
                        dst.at[here.h, rows],
                        zsends,
                        zrecvs,
                        q * (H - 1) + k - 1,
                        {"head": here.head(k)},
                    )
                )

        for q in range(parts):
            first(q)
            yield
            if q > 0:
                second(q - 1)
        second(parts - 1)
        yield
        for copy in spread:
            copy.wait()
        for copy in kept:
            copy.wait()
        for q in range(parts):
            for k in order:
                swaps[q, k].wait_send()
                if k > 0:
                    copies[q, k].wait_send()

    blocks = lambda count: pltpu.VMEM((count, R, C), x.dtype)
    return Task(
        "both",
        [x],
        [((H, R, C), x.dtype, ANY)],
        [blocks(N), blocks(N), blocks(N - 1), blocks(N - 1)]
        + [DMA((parts * (N - 1),)), DMA((parts * (N - 1),)), DMA((parts * N,)), DMA((parts * N,))]
        + [DMA((parts * (H - 1),)), DMA((parts * (H - 1),)), DMA((parts * N,)), DMA((parts,))],
        run,
    )


def all_sum(x, S, H, cid):
    def body(x_ref, o_ref, first, middle, second, sends, recvs, zsends, zrecvs):
        s, h = lax.axis_index("seq"), lax.axis_index("head")
        peers = [{"seq": lax.rem(s + k, S)} for k in range(1, S)]
        heads = [{"head": lax.rem(h + k, H)} for k in range(1, H)]
        barrier = pltpu.get_barrier_semaphore()
        for target in peers + heads:
            pl.semaphore_signal(barrier, inc=1, device_id=target, device_id_type=MESH)
        pl.semaphore_wait(barrier, S + H - 2)
        copies = [push(x_ref, first.at[s], sends, recvs, k, peers[k]) for k in range(S - 1)]
        first[s] = x_ref[...]
        for copy in copies:
            copy.wait()
        total = first[0]
        for k in range(1, S):
            total = total + first[k]
        middle[...] = total
        copies = [push(middle, second.at[h], zsends, zrecvs, k, heads[k]) for k in range(H - 1)]
        second[h] = total
        for copy in copies:
            copy.wait()
        total = second[0]
        for k in range(1, H):
            total = total + second[k]
        o_ref[...] = total

    return pl.pallas_call(
        body,
        out_shape=jax.ShapeDtypeStruct(x.shape, x.dtype),
        in_specs=[WHOLE],
        out_specs=WHOLE,
        scratch_shapes=[
            pltpu.VMEM((S,) + x.shape, x.dtype),
            pltpu.VMEM(x.shape, x.dtype),
            pltpu.VMEM((H,) + x.shape, x.dtype),
            DMA((S - 1,)),
            DMA((S - 1,)),
            DMA((H - 1,)),
            DMA((H - 1,)),
        ],
        compiler_params=pltpu.CompilerParams(collective_id=cid, has_side_effects=True),
        name="all_sum",
    )(x)


KD = 256
VD = 512
STEP = 10

NORM_EPS = 1e-05
BETA_ONE = 0.9
BETA_TWO = 0.999
ADAM_EPS = 1e-08
DECAY_WT = 0.01
LEARN_RATE = 0.2
TRUST_EPSILON = 1e-06


def contract_dims(left_side, right_side, left_dim, right_dim):
    return lax.dot_general(
        left_side,
        right_side,
        (((left_dim,), (right_dim,)), ((), ())),
        preferred_element_type=jnp.float32,
    )


def matmul(left_side, right_side):
    return jnp.dot(left_side, right_side, preferred_element_type=jnp.float32)


def centre(values):
    centred = values - jnp.mean(values, axis=-1, keepdims=True)
    return centred * lax.rsqrt(jnp.mean(centred * centred, axis=-1, keepdims=True) + NORM_EPS)


def row_scale(values):
    centred = values - jnp.mean(values, axis=-1, keepdims=True)
    return lax.rsqrt(jnp.mean(centred * centred, axis=-1, keepdims=True) + NORM_EPS)


def norm_back(values, gain_row, grad):
    hat, scale = centre(values), row_scale(values)
    scaled = grad * gain_row
    mean_one = jnp.mean(scaled, axis=-1, keepdims=True)
    mean_two = jnp.mean(scaled * hat, axis=-1, keepdims=True)
    return scale * (scaled - mean_one - hat * mean_two), jnp.sum(grad * hat, axis=0)


def rotary_tables(positions):
    halfway = KD // 2
    frequency = jnp.exp(-jnp.log(10000.0) * jnp.arange(halfway).astype(jnp.float32) / halfway)
    phases = positions.astype(jnp.float32)[:, None] * frequency[None, :]
    return (jnp.cos(phases), jnp.sin(phases))


def rotate(values, cosines, sines):
    halfway = values.shape[-1] // 2
    leading = values[..., :halfway]
    trailing = values[..., halfway:]
    return jnp.concatenate(
        [leading * cosines - trailing * sines, leading * sines + trailing * cosines], axis=-1
    )


def rotate_back(grads, cosines, sines):
    return rotate(grads, cosines, -sines)


def gate_norm(gate_pre, retained):
    scaled = retained * lax.rsqrt(jnp.mean(retained * retained, axis=-1, keepdims=True) + NORM_EPS)
    return gate_pre * jax.nn.sigmoid(gate_pre) * scaled


def gelu_gate(gate_part, up_part):
    return jax.nn.gelu(gate_part) * up_part


def lamb_parts(weight, moment, second, grad):
    new_moment = BETA_ONE * moment + (1.0 - BETA_ONE) * grad
    new_second = BETA_TWO * second + (1.0 - BETA_TWO) * grad * grad
    moment_hat = new_moment / (1.0 - BETA_ONE**STEP)
    second_hat = new_second / (1.0 - BETA_TWO**STEP)
    ratio = moment_hat / (jnp.sqrt(second_hat) + ADAM_EPS) + DECAY_WT * weight
    return (new_moment, new_second, ratio)


def local(
    token_ids,
    completion,
    decay_rate,
    w_mixer,
    w_output,
    w_expand,
    w_contract,
    norm_gains,
    embedding,
    mom_mixer,
    var_mixer,
    mom_output,
    var_output,
    mom_expand,
    var_expand,
    mom_contract,
    var_contract,
    mom_gains,
    var_gains,
    mom_embed,
    var_embed,
):
    bf, f32 = jnp.bfloat16, jnp.float32
    s, h = lax.axis_index("seq"), lax.axis_index("head")
    S, H = lax.axis_size("seq"), lax.axis_size("head")
    total_tokens = token_ids.shape[0]
    span = total_tokens // S
    vocab_part, width = embedding.shape
    quarter = width // H
    cap = span // 2
    own = cap // H
    rows_own = span // H
    assert w_mixer.shape[0] == 1
    token_start = s * span
    vocab_start = s * vocab_part

    aligned = w_output.shape[2] % 128 == 0

    def run(cid, name, *tasks):
        return [results[0] for results in fused(cid, S, H, tasks, name)]

    def flat(blocks):
        return blocks.reshape((-1,) + blocks.shape[2:])

    def gather_columns(weight):
        return gather_seq(weight, S, columns=aligned)

    def joined(gathered):
        if aligned:
            return gathered
        return gathered.transpose(1, 0, 2).reshape(gathered.shape[1], -1)

    def sum_columns(grad):
        grad = grad.astype(bf)
        if not aligned:
            grad = grad.reshape(grad.shape[0], S, -1).transpose(1, 0, 2)
        return sum_seq(grad, S, columns=aligned)

    small = jnp.concatenate([norm_gains.astype(f32), mom_gains, var_gains], axis=0)
    small = jnp.concatenate([small, jnp.zeros((16 - small.shape[0], small.shape[1]), f32)], axis=0)

    ids_grid = token_ids.reshape(S, H, rows_own)
    ids_own = lax.dynamic_index_in_dim(ids_grid, h, 1, keepdims=False)
    chosen = ids_own.reshape(-1) - vocab_start
    inside = (chosen >= 0) & (chosen < vocab_part)
    found = jnp.take(embedding, jnp.clip(chosen, 0, vocab_part - 1), axis=0)
    found = jnp.where(inside[:, None], found, jnp.zeros((), bf))
    rows, mixer, small_all = run(
        1,
        "enter",
        lookup(found.reshape(S, rows_own, width), S, H, 4 if S <= 8 else 1),
        gather_seq(w_mixer[0], S),
        gather_seq(small, S),
    )
    x0, mixer = flat(rows), flat(mixer)
    small_all = small_all.transpose(1, 0, 2).reshape(16, width)
    gains, mom_gains_all, var_gains_all = small_all[:3], small_all[3:6], small_all[6:9]

    mask_own = lax.dynamic_slice_in_dim(completion, token_start, span)
    slot_of = jnp.where(mask_own == 1, jnp.cumsum(mask_own) - 1, -1)
    picker = (slot_of[None, :] == jnp.arange(cap)[:, None]).astype(bf)
    place = jnp.sum(
        jnp.where(slot_of[None, :] == jnp.arange(cap)[:, None], jnp.arange(span)[None, :], 0), axis=1
    )
    mask_grid = completion.reshape(S, span)
    next_ids = jnp.roll(token_ids, -1).reshape(S, span)
    live = (completion * (jnp.arange(total_tokens) < total_tokens - 1)).reshape(S, span)
    slot_grid = jnp.where(mask_grid == 1, jnp.cumsum(mask_grid, axis=1) - 1, -1)
    matches = slot_grid[:, None, :] == jnp.arange(cap)[None, :, None]
    targets = jnp.sum(jnp.where(matches, next_ids[:, None, :], 0), axis=-1)
    row_weights = jnp.sum(jnp.where(matches, live[:, None, :], 0), axis=-1).astype(f32)
    count_live = jnp.sum(live).astype(f32)

    def of_quarter(grid, head):
        return lax.dynamic_index_in_dim(grid.reshape(S, H, own), head, 1, keepdims=False).reshape(-1)

    rate = decay_rate[0, 0]
    steps_in = jnp.arange(span).astype(f32)
    offsets = place[:, None].astype(f32) - steps_in[None, :]
    within = jnp.where(offsets >= 0, jnp.exp(-rate * jnp.maximum(offsets, 0.0)), 0.0)
    tail_decay = jnp.exp(-rate * (span - 1.0 - steps_in))[:, None]
    lead_decay = jnp.exp(-rate * (place.astype(f32) + 1.0))[:, None]
    cosines, sines = rotary_tables(token_start + jnp.arange(span))
    cosines_q, sines_q = rotary_tables(token_start + place)

    def state_sum(everyone, backward):
        position = jnp.arange(S)
        gap = position - s - 1 if backward else s - 1 - position
        factor = jnp.where(gap >= 0, jnp.exp(-rate * span * jnp.maximum(gap, 0).astype(f32)), 0.0)
        return jnp.sum(everyone.astype(f32) * factor[:, None, None], axis=0).astype(bf)

    hat0 = centre(x0.astype(f32))
    normed = (hat0 * gains[0]).astype(bf)
    proj_kv = matmul(normed, mixer[:, KD : 2 * KD + VD])
    keys = (rotate(proj_kv[:, :KD], cosines, sines) * KD ** (-0.5)).astype(bf)
    values = proj_kv[:, KD:].astype(bf)
    weighted = (keys.astype(f32) * tail_decay).astype(bf)
    update = contract_dims(weighted, values, 0, 0)
    everyone, output = run(2, "states", gather_seq(update.astype(bf), S), gather_columns(w_output[0]))
    output = joined(output)
    state = state_sum(everyone, False)
    normed_q = matmul(picker, normed).astype(bf)
    query = rotate(matmul(normed_q, mixer[:, :KD]), cosines_q, sines_q).astype(bf)
    gate_pre = matmul(normed_q, mixer[:, 2 * KD + VD :])
    scores = contract_dims(query, keys, 1, 1)
    weights_blk = (scores * within).astype(bf)
    inner_part = matmul(weights_blk, values)
    retained = inner_part + lead_decay * matmul(query, state)
    gated = gate_norm(gate_pre, retained).astype(bf)

    def by_head(value):
        return sum_head(value.astype(bf).reshape(H, own, width), H)

    x0_own = matmul(lax.dynamic_slice_in_dim(picker, h * own, own, 0), x0)
    branch, expand, contract = run(
        3, "mid", by_head(matmul(gated, output)), gather_seq(w_expand[0], S), gather_columns(w_contract[0])
    )
    expand, contract = flat(expand), joined(contract)
    x1 = x0_own + branch
    normed_b_own = (centre(x1) * gains[1]).astype(bf)
    normed_b = flat(run(4, "normed", gather_head(normed_b_own, H))[0])
    gate_up = matmul(normed_b, expand)
    width_ff = gate_up.shape[1] // 2
    hidden = gelu_gate(gate_up[:, :width_ff], gate_up[:, width_ff:]).astype(bf)
    x2 = x1 + run(5, "feed", by_head(matmul(hidden, contract)))[0]
    final_own = (centre(x2) * gains[2]).astype(bf)

    final_rows = flat(run(6, "final", gather_seq(final_own, S))[0])
    logits = contract_dims(final_rows, embedding, 1, 1)
    peak = jnp.max(logits, axis=-1)
    exp_total = jnp.sum(jnp.exp(logits - peak[:, None]), axis=-1)
    stats = run(7, "stats", gather_seq(jnp.stack([peak, exp_total]).reshape(-1, 128), S))[0].reshape(S, 2, S * own)
    peak_all = jnp.max(stats[:, 0], axis=0)
    total_all = jnp.sum(stats[:, 1] * jnp.exp(stats[:, 0] - peak_all), axis=0)
    log_total = peak_all + jnp.log(total_all)

    def logits_grad(logits, log_total, head):
        scale = of_quarter(row_weights, head) / count_live
        local_target = of_quarter(targets, head) - vocab_start
        hit = jnp.arange(vocab_part)[None, :] == local_target[:, None]
        grads = jnp.exp(logits - log_total[:, None]) - hit.astype(f32)
        return (grads * scale[:, None]).astype(bf), hit, scale

    grad_logits, hit, scale_row = logits_grad(logits, log_total, h)
    target_logit = jnp.sum(jnp.where(hit, logits, 0.0), axis=-1)
    shard_loss = jnp.sum(scale_row * log_total) * (s == 0).astype(f32) - jnp.sum(
        scale_row * target_logit
    )
    grad_final, finals, logs = run(
        8,
        "logits_back",
        sum_seq(matmul(grad_logits, embedding).astype(bf).reshape(S, own, width), S),
        gather_head(final_own, H),
        gather_head(log_total.reshape(-1, 128), H),
    )
    grad_x2, grad_gain_final = norm_back(x2, gains[2], grad_final)

    pieces = {}
    grad_branch, pieces[1], pieces[2] = run(
        9,
        "branch_back",
        gather_head(grad_x2.astype(bf), H),
        gather_seq(finals, S, ahead=1),
        gather_seq(finals, S, ahead=2),
    )
    grad_branch = flat(grad_branch)
    grad_hidden = contract_dims(grad_branch, contract, 1, 1)
    grad_contract = contract_dims(hidden, grad_branch, 0, 0)
    _, gelu_back = jax.vjp(gelu_gate, gate_up[:, :width_ff], gate_up[:, width_ff:])
    grad_gate_up = jnp.concatenate(gelu_back(grad_hidden), axis=1).astype(bf)
    grad_expand = contract_dims(normed_b, grad_gate_up, 0, 0)
    grad_normed_b, pieces[3], grad_contract = run(
        10,
        "expand_back",
        by_head(contract_dims(grad_gate_up, expand, 1, 1)),
        gather_seq(finals, S, ahead=3),
        sum_columns(grad_contract),
    )
    grad_x1, grad_gain_b = norm_back(x1, gains[1], grad_normed_b)
    grad_x1 = grad_x1 + grad_x2
    grad_attn, grad_expand = run(
        11,
        "attn_back",
        gather_head(grad_x1.astype(bf), H),
        sum_seq(grad_expand.astype(bf).reshape(S, -1, grad_expand.shape[1]), S),
    )
    grad_attn = flat(grad_attn)
    grad_gated = contract_dims(grad_attn, output, 1, 1)
    grad_output = contract_dims(gated, grad_attn, 0, 0)
    _, gate_back = jax.vjp(gate_norm, gate_pre, retained)
    grad_gate_pre, grad_ret = gate_back(grad_gated)
    grad_cross = (lead_decay * grad_ret).astype(bf)
    grad_ret = grad_ret.astype(bf)
    grad_state = contract_dims(query, grad_cross, 0, 0)
    everyone, grad_output = run(12, "states_back", gather_seq(grad_state.astype(bf), S), sum_columns(grad_output))
    grad_update = state_sum(everyone, True)
    grad_weights = contract_dims(grad_ret, values, 1, 1)
    grad_scores = (grad_weights * within).astype(bf)
    grad_query = matmul(grad_scores, keys) + contract_dims(grad_cross, state, 1, 1)
    grad_keys = contract_dims(grad_scores, query, 0, 0)
    grad_values = contract_dims(weights_blk, grad_ret, 0, 0) + matmul(weighted, grad_update)
    grad_keys = grad_keys + contract_dims(values, grad_update, 1, 1) * tail_decay
    grad_q_pre = rotate_back(grad_query, cosines_q, sines_q).astype(bf)
    grad_k_pre = rotate_back(grad_keys * KD ** (-0.5), cosines, sines).astype(bf)
    grad_qg = contract_dims(
        picker, jnp.concatenate([grad_q_pre, grad_gate_pre.astype(bf)], axis=1), 0, 0
    ).astype(bf)
    grad_proj = jnp.concatenate(
        [grad_qg[:, :KD], grad_k_pre, grad_values.astype(bf), grad_qg[:, KD:]], axis=1
    )
    grad_normed = contract_dims(grad_proj, mixer, 1, 1)
    grad_mixer = contract_dims(normed, grad_proj, 0, 0)

    def own_columns(value):
        return lax.dynamic_slice_in_dim(value, h * quarter, quarter, 1)

    scaled = grad_normed * gains[0]
    row_sums = jnp.stack([jnp.sum(scaled, axis=1), jnp.sum(scaled * hat0, axis=1)]).reshape(-1, 128)
    columns, row_sums, grad_mixer = run(
        13,
        "mixer_back",
        sum_head(grad_normed.astype(bf), H, columns=True),
        gather_head(row_sums, H),
        sum_seq(grad_mixer.astype(bf).reshape(S, -1, grad_mixer.shape[1]), S),
    )
    row_sums = jnp.sum(row_sums, axis=0).reshape(2, span, 1) / width
    hat_cols = own_columns(hat0)
    gain_cols = lax.dynamic_slice_in_dim(gains[0], h * quarter, quarter, 0)
    grad_gain_a = jnp.sum(columns * hat_cols, axis=0)
    grad_in = row_scale(x0.astype(f32)) * (columns * gain_cols - row_sums[0] - hat_cols * row_sums[1])
    grad_in = grad_in + contract_dims(picker, own_columns(grad_attn), 0, 0)
    piece_rows = flat(run(14, "rows", gather_seq(grad_in.astype(bf), S))[0])
    grad_table = contract_dims(grad_logits, own_columns(final_rows), 0, 0)
    for k in range(1, H):
        there = lax.rem(h + k, H)
        rows_k = flat(pieces[k])
        logits_k = contract_dims(rows_k, embedding, 1, 1)
        log_k = lax.dynamic_index_in_dim(logs, there, 0, keepdims=False).reshape(-1)
        grads_k = logits_grad(logits_k, log_k, there)[0]
        grad_table = grad_table + contract_dims(grads_k, own_columns(rows_k), 0, 0)

    local_id = token_ids - vocab_start
    one_hot = (jnp.arange(vocab_part)[:, None] == local_id[None, :]).astype(bf)
    grad_table = grad_table + matmul(one_hot, piece_rows)

    grad_mixer, grad_output, grad_expand, grad_contract = (
        grad_mixer[None],
        grad_output[None],
        grad_expand[None],
        grad_contract[None],
    )
    grad_gains = jnp.stack(
        [lax.dynamic_update_slice_in_dim(jnp.zeros((width,), f32), grad_gain_a, h * quarter, 0), grad_gain_b, grad_gain_final]
    )

    mixer_f = w_mixer.astype(f32)
    output_f = w_output.astype(f32)
    expand_f = w_expand.astype(f32)
    contract_f = w_contract.astype(f32)
    table_own = own_columns(embedding).astype(f32)
    parts = [
        lamb_parts(mixer_f, mom_mixer, var_mixer, grad_mixer),
        lamb_parts(output_f, mom_output, var_output, grad_output),
        lamb_parts(expand_f, mom_expand, var_expand, grad_expand),
        lamb_parts(contract_f, mom_contract, var_contract, grad_contract),
        lamb_parts(table_own, mom_embed, var_embed, grad_table),
    ]
    held = [mixer_f, output_f, expand_f, contract_f, table_own]
    sums = jnp.stack(
        [jnp.sum(w * w) for w in held] + [jnp.sum(p[2] * p[2]) for p in parts] + [shard_loss]
    )
    packed = jnp.concatenate([jnp.pad(sums, (0, 1024 - sums.shape[0])).reshape(8, 128), grad_gains.reshape(-1, 128)])
    packed = all_sum(packed, S, H, 15)
    sums = packed[0]
    grad_gains = packed[8:].reshape(3, width)
    part_gains = lamb_parts(gains, mom_gains_all, var_gains_all, grad_gains)
    weight_squares = jnp.concatenate([sums[:5], jnp.sum(gains * gains, axis=1)])
    ratio_squares = jnp.concatenate([sums[5:10], jnp.sum(part_gains[2] * part_gains[2], axis=1)])
    trust = jnp.sqrt(weight_squares) * lax.rsqrt(ratio_squares + TRUST_EPSILON)
    new_w = [w - LEARN_RATE * trust[i] * parts[i][2] for i, w in enumerate(held)]
    new_gains = gains - LEARN_RATE * trust[5:][:, None] * part_gains[2]

    def own_gains(value):
        return lax.dynamic_slice_in_dim(value, s * (width // S), width // S, 1)

    return (
        sums[10],
        jnp.stack([weight_squares, ratio_squares], axis=1),
        parts[0][0],
        parts[0][1],
        new_w[0],
        parts[1][0],
        parts[1][1],
        new_w[1],
        parts[2][0],
        parts[2][1],
        new_w[2],
        parts[3][0],
        parts[3][1],
        new_w[3],
        own_gains(part_gains[0]),
        own_gains(part_gains[1]),
        own_gains(new_gains),
        parts[4][0],
        parts[4][1],
        new_w[4],
    )


def solution(mesh):
    placed = (
        P(),
        P(),
        P(None, "head"),
        P(None, "seq", "head"),
        P(None, "head", "seq"),
        P(None, "seq", "head"),
        P(None, "head", "seq"),
        P(None, "seq"),
        P("seq", None),
        P(None, "seq", "head"),
        P(None, "seq", "head"),
        P(None, "head", "seq"),
        P(None, "head", "seq"),
        P(None, "seq", "head"),
        P(None, "seq", "head"),
        P(None, "head", "seq"),
        P(None, "head", "seq"),
        P(None, "seq"),
        P(None, "seq"),
        P("seq", "head"),
        P("seq", "head"),
    )
    return jax.shard_map(
        local,
        mesh=mesh,
        in_specs=placed,
        out_specs=(P(), P()) + placed[3:4] * 3 + placed[4:5] * 3 + placed[3:4] * 3 + placed[4:5] * 3 + placed[7:8] * 3 + placed[19:20] * 3,
        check_vma=False,
    )
```

time: 608 us -> 698 us (1.15); the launches traced: 609 us -> 691 us
  Pallas kernels: 145 us -> 404 us
  waiting for transfers between devices: 99.5 us -> 0 us
  starting transfers between devices: 81.1 us -> 0 us
  other arithmetic: 56.4 us -> 79.8 us
  between operations: 22 us -> 8.59 us
  local copies, waits for them, and re-layouts: 57.4 us -> 45.8 us
    pallas_call x9 -> x15, Pallas kernels: 145 us -> 404 us  [the longest x14 393 us: fused(): pl.pallas_call(body, out_shape=outs, in_specs=[ANY] * len(operands), out_...]
    ppermute x33 -> x0, waiting for transfers between devices: 97.2 us -> none  [shift(): lax.ppermute(value, axis, [(i, (i + by) % count) for i in range(count)])]
    ppermute x33 -> x0, starting transfers between devices: 80.2 us -> none  [shift(): lax.ppermute(value, axis, [(i, (i + by) % count) for i in range(count)])]
    dot_general x14, matrix products: 45.9 us -> 57.3 us  [matmul(): return jnp.dot(left_side, right_side, preferred_element_type=jnp.float32)]
    unnamed x198 -> x262, local copies, waits for them, and re-layouts: 17.9 us -> 8.3 us
  transfers between devices with their start and end apart: 41 -> 0, of which waited for: 14 -> 0; matrix products, arithmetic and copies ran while one was open for 32% -> 0% of each run, Pallas kernels for 17% -> 0%
where the time goes in v2:
time: 698 us; the launch traced here: 691 us
  Pallas kernels  404 us (58%)
  matrix products  152 us (22%)
  other arithmetic  79.8 us (11%)
  local copies, waits for them, and re-layouts  45.8 us (7%)
  between operations  8.59 us (1%)
    pallas_call x14, Pallas kernels, fused(): pl.pallas_call(body, out_shape=outs, in_specs=[ANY] * len(operands), out_...  393 us
    dot_general x23, matrix products, contract_dims(): lax.dot_general(left_side, right_side, (((left_dim,), (right_dim,)), ((),...  94.8 us
    dot_general x14, matrix products, matmul(): return jnp.dot(left_side, right_side, preferred_element_type=jnp.float32)  57.3 us

profile of v2, /device:TPU:0, one launch (start us, length us, event | category | flops | bytes accessed | tf_op | source)
XLA Modules:
  0.0 690.6 jit_solution(5204211715040124371)
XLA Ops:
  1.7 11.5 %gather_fusion = bf16[1536,1024]{1,0:T(8,128)(2,1)S(1)} fusion(bf16[4000,1024]{1,0:T(8,128)(2,1)} %param.29, s32[2048]{0:T(1024)S(1)} %pad_clamp_fusion), kind=kCustom, calls=%fused_computation | custom fusion | bytes 6297600 | tf_op jit(solution)/shard_map/jit(_take)/gather | solution.py:563
  16.0 65.3 %enter.1 = (bf16[4,192,1024]{2,1,0:T(8,128)(2,1)}, bf16[8,128,1536]{2,1,0:T(8,128)(2,1)}, f32[8,16,128]{2,1,0:T(8,128)}) custom-call(bf16[8,192,1024]{2,1,0:T(8,128)(2,1)} %select_select_fusion.refs_0_, bf16[128,1536]{1,0:T(8,128)(2,1)} %bitcast.202, f32[16,128]{1,0:T(8,128)} %maximum_maximum_fusion.refs_2_), custom_call_target="tpu_custom_call" | custom-call | bytes 33554432 | tf_op jit(solution)/shard_map/enter/pallas_call | solution.py:106
  92.0 3.1 fusion.70
  108.7 22.3 %states.1 = (bf16[8,256,512]{2,1,0:T(8,128)(2,1)}, bf16[512,1024]{1,0:T(8,128)(2,1)}) custom-call(bf16[256,512]{1,0:T(8,128)(2,1)} %convolution_convert_fusion.11.refs_0_, bf16[512,128]{1,0:T(8,128)(2,1)} %bitcast.210), custom_call_target="tpu_custom_call" | custom-call | bytes 33554432 | tf_op jit(solution)/shard_map/states/pallas_call | solution.py:106
  138.7 26.5 %mid.1 = (f32[96,1024]{1,0:T(8,128)}, bf16[8,128,1024]{2,1,0:T(8,128)(2,1)}, bf16[512,1024]{1,0:T(8,128)(2,1)}) custom-call(bf16[4,96,1024]{2,1,0:T(8,128)(2,1)} %bitcast.217, bf16[128,1024]{1,0:T(8,128)(2,1)} %bitcast.205, bf16[512,128]{1,0:T(8,128)(2,1)} %bitcast.211), custom_call_target="tpu_custom_call" | custom-call | bytes 33554432 | tf_op jit(solution)/shard_map/mid/pallas_call | solution.py:106
  168.4 17.9 %normed.1 = bf16[4,96,1024]{2,1,0:T(8,128)(2,1)} custom-call(bf16[96,1024]{1,0:T(8,128)(2,1)} %multiply_convert_fusion.11.refs_0_), custom_call_target="tpu_custom_call" | custom-call | bytes 33554432 | tf_op jit(solution)/shard_map/normed/pallas_call | solution.py:106
  192.9 20.9 %feed.1 = f32[96,1024]{1,0:T(8,128)} custom-call(bf16[4,96,1024]{2,1,0:T(8,128)(2,1)} %bitcast.218), custom_call_target="tpu_custom_call" | custom-call | bytes 33554432 | tf_op jit(solution)/shard_map/feed/pallas_call | solution.py:106
  216.7 12.9 %final.1 = bf16[8,96,1024]{2,1,0:T(8,128)(2,1)} custom-call(bf16[96,1024]{1,0:T(8,128)(2,1)} %multiply_convert_fusion.10.refs_0_.refs_1_), custom_call_target="tpu_custom_call" | custom-call | bytes 33554432 | tf_op jit(solution)/shard_map/final/pallas_call | solution.py:106
  229.7 11.0 %fusion.170 = (f32[768]{0:T(1024)}, f32[768,4000]{0,1:T(8,128)}) fusion(bf16[768,1024]{1,0:T(8,128)(2,1)} %bitcast.207, bf16[4000,1024]{1,0:T(8,128)(2,1)S(1)} %bitcast.199), kind=kOutput, calls=%fused_computation.369 | convolution fusion | flops 6294526976 | bytes 22055936 | tf_op jit(solution)/shard_map/dot_general | solution.py:429
  245.2 2.9 select_reduce_fusion.2
  248.9 7.2 %select_reduce_fusion = (f32[768]{0:T(1024)S(1)}, f32[768]{0:T(1024)S(1)}) fusion(f32[768,4000]{0,1:T(8,128)} %get-tuple-element.173, s32[768]{0:T(1024)S(1)} %sub.353, f32[768]{0:T(1024)} %get-tuple-element.172), kind=kLoop, calls=%fused_computation.4 | loop fusion | flops 15358464 | bytes 12300288 | tf_op jit(solution)/shard_map/reduce_sum | solution.py:662
  256.8 6.2 stats.1
  266.2 13.2 %convolution_convert_fusion.2 = bf16[768,1024]{1,0:T(8,128)(2,1)} fusion(bf16[4000,1024]{1,0:T(8,128)(2,1)} %param.29, f32[768,4000]{0,1:T(8,128)} %get-tuple-element.173, f32[768]{0:T(1024)S(1)} %div.223, s32[768]{0:T(1024)S(1)} %sub.353, f32[768]{0:T(1024)S(1)} %log_add_fusion), kind=kOutput, calls=%fused_computation.48 | convolution fusion | flops 6310674432 | bytes 22062080 | tf_op jit(solution)/shard_map/dot_general | solution.py:438
  279.4 32.2 %logits_back.1 = (f32[96,1024]{1,0:T(8,128)}, bf16[4,96,1024]{2,1,0:T(8,128)(2,1)}, f32[4,6,128]{2,1,0:T(8,128)}) custom-call(bf16[8,96,1024]{2,1,0:T(8,128)(2,1)} %bitcast.209, bf16[96,1024]{1,0:T(8,128)(2,1)} %multiply_convert_fusion.10.refs_0_.refs_1_, f32[6,128]{1,0:T(8,128)} %bitcast.231), custom_call_target="tpu_custom_call" | custom-call | bytes 33554432 | tf_op jit(solution)/shard_map/logits_back/pallas_call | solution.py:106
  315.2 27.2 %branch_back.1 = (bf16[4,96,1024]{2,1,0:T(8,128)(2,1)}, bf16[8,96,1024]{2,1,0:T(8,128)(2,1)}, bf16[8,96,1024]{2,1,0:T(8,128)(2,1)}) custom-call(bf16[96,1024]{1,0:T(8,128)(2,1)} %get-tuple-element.113.refs_0_, bf16[4,96,1024]{2,1,0:T(8,128)(2,1)} %get-tuple-element.53.refs_1_.refs_2_, bf16[4,96,1024]{2,1,0:T(8,128)(2,1)} %get-tuple-element.53.refs_1_.refs_2_), custom_call_target="tpu_custom_call" | custom-call | bytes 33554432 | tf_op jit(solution)/shard_map/branch_back/pallas_call | solution.py:106
  348.5 26.3 %expand_back.1 = (f32[96,1024]{1,0:T(8,128)}, bf16[8,96,1024]{2,1,0:T(8,128)(2,1)}, f32[512,128]{1,0:T(8,128)}) custom-call(bf16[4,96,1024]{2,1,0:T(8,128)(2,1)} %bitcast.221, bf16[4,96,1024]{2,1,0:T(8,128)(2,1)} %get-tuple-element.53.refs_1_.refs_2_, bf16[512,1024]{1,0:T(8,128)(2,1)} %convolution_convert_fusion.5.refs_2_), custom_call_target="tpu_custom_call" | custom-call | bytes 33554432 | tf_op jit(solution)/shard_map/expand_back/pallas_call | solution.py:106
  381.1 32.1 %attn_back.1 = (bf16[4,96,1024]{2,1,0:T(8,128)(2,1)}, f32[128,1024]{1,0:T(8,128)}) custom-call(bf16[96,1024]{1,0:T(8,128)(2,1)} %add_convert_fusion.1.refs_0_, bf16[8,128,1024]{2,1,0:T(8,128)(2,1)} %bitcast.206), custom_call_target="tpu_custom_call" | custom-call | bytes 33554432 | tf_op jit(solution)/shard_map/attn_back/pallas_call | solution.py:106
  423.5 21.5 %states_back.1 = (bf16[8,256,512]{2,1,0:T(8,128)(2,1)}, f32[512,128]{1,0:T(8,128)}) custom-call(bf16[256,512]{1,0:T(8,128)(2,1)} %convolution_convert_fusion.10.refs_0_, bf16[512,1024]{1,0:T(8,128)(2,1)} %convolution_convert_fusion.4.refs_1_), custom_call_target="tpu_custom_call" | custom-call | bytes 33554432 | tf_op jit(solution)/shard_map/states_back/pallas_call | solution.py:106
  454.3 4.9 multiply_reduce_fusion.4
  459.8 5.7 convolution_convert_fusion
  465.6 58.8 %mixer_back.1 = (f32[768,256]{1,0:T(8,128)}, f32[4,12,128]{2,1,0:T(8,128)}, f32[128,1536]{1,0:T(8,128)}) custom-call(bf16[768,1024]{1,0:T(8,128)(2,1)} %get-tuple-element.120.refs_0_, f32[12,128]{1,0:T(8,128)} %reshape.589.refs_1_, bf16[8,128,1536]{2,1,0:T(8,128)(2,1)} %bitcast.204), custom_call_target="tpu_custom_call" | custom-call | bytes 33554432 | tf_op jit(solution)/shard_map/mixer_back/pallas_call | solution.py:106
  527.1 4.2 multiply_reduce_fusion.6
  536.7 10.2 %fusion.75 = f32[4000,256]{1,0:T(8,128)} fusion(bf16[768,1024]{1,0:T(8,128)(2,1)} %bitcast.208, s32[]{:T(128)S(6)} %select_n.119, f32[768,4000]{0,1:T(8,128)} %get-tuple-element.173, f32[768]{0:T(1024)S(1)} %copy-done.111, s32[768]{0:T(1024)S(1)} %copy-done.82, f32[768]{0:T(1024)S(1)} %copy-done.65), kind=kOutput, calls=%fused_computation.165 | convolution fusion | flops 1591296000 | bytes 16786436 | tf_op jit(solution)/shard_map/dot_general | solution.py:429
  549.5 13.9 %fusion.8 = f32[4000,256]{1,0:T(8,128)} fusion(f32[4000,256]{1,0:T(8,128)} %fusion.75, bf16[768,1024]{1,0:T(8,128)(2,1)} %bitcast.253, bf16[4000,1024]{1,0:T(8,128)(2,1)} %param.29, f32[768]{0:T(1024)} %div.247, s32[768]{0:T(1024)} %sub.372, f32[768]{0:T(1024)S(1)} %get-tuple-element.149, s32[]{:T(128)S(6)} %select_n.119), kind=kOutput, calls=%fused_computation.27 | convolution fusion | flops 7883776000 | bytes 18361348 | tf_op jit(solution)/shard_map/dot_general | solution.py:429
  565.4 14.4 %fusion.7 = f32[4000,256]{1,0:T(8,128)} fusion(f32[4000,256]{1,0:T(8,128)} %fusion.8, bf16[768,1024]{1,0:T(8,128)(2,1)} %bitcast.251, bf16[4000,1024]{1,0:T(8,128)(2,1)} %param.29, f32[768]{0:T(1024)S(1)} %div.249, s32[768]{0:T(1024)} %sub.378, f32[768]{0:T(1024)} %get-tuple-element.148, s32[]{:T(128)S(6)} %select_n.119), kind=kOutput, calls=%fused_computation.26 | convolution fusion | flops 7883776000 | bytes 18361348 | tf_op jit(solution)/shard_map/dot_general | solution.py:429
  580.5 13.9 %fusion.6 = f32[4000,256]{1,0:T(8,128)} fusion(f32[4000,256]{1,0:T(8,128)} %fusion.7, bf16[768,1024]{1,0:T(8,128)(2,1)} %bitcast.252, bf16[4000,1024]{1,0:T(8,128)(2,1)} %param.29, f32[768]{0:T(1024)S(1)} %div.251, s32[768]{0:T(1024)} %sub.384, f32[768]{0:T(1024)S(1)} %copy-done.107, s32[]{:T(128)S(6)} %select_n.119), kind=kOutput, calls=%fused_computation.25 | convolution fusion | flops 7883776000 | bytes 18360324 | tf_op jit(solution)/shard_map/dot_general | solution.py:429
  596.1 2.9 fusion.21.refs_0_
  599.1 22.8 %rows.1 = bf16[8,768,256]{2,1,0:T(8,128)(2,1)} custom-call(bf16[768,256]{1,0:T(8,128)(2,1)} %fusion.21.refs_0_), custom_call_target="tpu_custom_call" | custom-call | bytes 33554432 | tf_op jit(solution)/shard_map/rows/pallas_call | solution.py:106
  621.9 27.0 %multiply_reduce_fusion.2 = (f32[]{:T(128)}, f32[4000,256]{1,0:T(8,128)}, f32[4000,256]{1,0:T(8,128)}, f32[4000,256]{1,0:T(8,128)}, f32[]{:T(128)}) fusion(bf16[4000,1024]{1,0:T(8,128)(2,1)} %param.29, s32[]{:T(128)S(6)} %select_n.119, f32[4000,256]{1,0:T(8,128)S(1)} %copy-done.118, f32[4000,256]{1,0:T(8,128)} %param.41, f32[4000,256]{1,0:T(8,128)} %fusion.6, ...), kind=kOutput, calls=%fused_computation.33 | convolution fusion | flops 12626944000 | bytes 29794316 | tf_op jit(solution)/shard_map/dot_general | solution.py:438
  650.2 6.6 stack.92
  657.5 11.4 %all_sum.1 = f32[32,128]{1,0:T(8,128)} custom-call(f32[32,128]{1,0:T(8,128)} %pad_maximum_fusion.5.x_ref), custom_call_target="tpu_custom_call" | custom-call | tf_op jit(solution)/shard_map/all_sum/pallas_call | solution.py:396
  685.2 5.2 convert_subtract_fusion
  (432 shorter events, 120.0 us)
Async XLA Ops:
  86.3 80.8 %copy-start.57 = (f32[1,8,128]{2,0,1:T(1,128)}, f32[1,8,128]{2,0,1:T(1,128)S(1)}, u32[]{:S(2)}) copy-start(f32[1,8,128]{2,0,1:T(1,128)S(1)} %get-tuple-element.136) | copy-start | bytes 12292
  86.3 129.1 %copy-start.59 = (f32[1,8,128]{2,0,1:T(1,128)}, f32[1,8,128]{2,0,1:T(1,128)S(1)}, u32[]{:S(2)}) copy-start(f32[1,8,128]{2,0,1:T(1,128)S(1)} %get-tuple-element.135) | copy-start | bytes 12292
  106.5 27.1 %copy-start.24 = (bf16[384,128]{1,0:T(8,128)(2,1)}, bf16[384,128]{1,0:T(8,128)(2,1)S(1)}, u32[]{:S(2)}) copy-start(bf16[384,128]{1,0:T(8,128)(2,1)S(1)} %get-tuple-element.132) | copy-start | bytes 294916
  137.2 28.0 %copy-start.45 = (bf16[384,512]{1,0:T(8,128)(2,1)}, bf16[384,512]{1,0:T(8,128)(2,1)S(1)}, u32[]{:S(2)}) copy-start(bf16[384,512]{1,0:T(8,128)(2,1)S(1)} %get-tuple-element.168) | copy-start | bytes 1179652
  137.2 28.0 %copy-start.67 = (s32[768]{0:T(1024)S(1)}, s32[768]{0:T(1024)}, u32[]{:S(2)}) copy-start(s32[768]{0:T(1024)} %copy-done.66) | copy-start | bytes 9220
  167.6 62.0 %slice-start = ((s8[8192000]{0:T(1024)(128)(4,1)}), s8[4194304]{0:T(1024)(128)(4,1)S(1)}, s32[]{:S(2)}) async-start(s8[8192000]{0:T(1024)(128)(4,1)} %bitcast.198), calls=%async_computation | async-start | bytes 8388608
  190.4 39.2 %slice-start.1 = ((s8[8192000]{0:T(1024)(128)(4,1)}), s8[3997696]{0:T(1024)(128)(4,1)S(1)}, s32[]{:S(2)}) async-start(s8[8192000]{0:T(1024)(128)(4,1)} %bitcast.198), calls=%async_computation.1 | async-start | bytes 7995392
  266.1 45.5 %copy-start.7 = (f32[96,1024]{1,0:T(8,128)S(1)}, f32[96,1024]{1,0:T(8,128)}, u32[]{:S(2)}) copy-start(f32[96,1024]{1,0:T(8,128)} %copy-done.6) | copy-start | bytes 1179652
  266.1 45.5 %copy-start.60 = (f32[1,8,128]{2,0,1:T(1,128)S(1)}, f32[1,8,128]{2,0,1:T(1,128)}, u32[]{:S(2)}) copy-start(f32[1,8,128]{2,0,1:T(1,128)} %copy-done.59) | copy-start | bytes 12292
  266.2 45.5 %copy-start.100 = (f32[96]{0:T(128)S(1)}, f32[96]{0:T(128)}, u32[]{:S(2)}) copy-start(f32[96]{0:T(128)} %copy-done.99) | copy-start | bytes 1156
  266.2 45.5 %copy-start.106 = (f32[96]{0:T(128)S(1)}, f32[96]{0:T(128)}, u32[]{:S(2)}) copy-start(f32[96]{0:T(128)} %copy-done.105) | copy-start | bytes 1156
  279.4 63.1 %copy-start.29 = (f32[384,1024]{1,0:T(8,128)S(1)}, f32[384,1024]{1,0:T(8,128)}, u32[]{:S(2)}) copy-start(f32[384,1024]{1,0:T(8,128)} %copy-done.28) | copy-start | bytes 4718596
  279.4 63.1 %copy-start.125 = (bf16[512,1024]{1,0:T(8,128)(2,1)S(1)}, bf16[512,1024]{1,0:T(8,128)(2,1)}, u32[]{:S(2)}) copy-start(bf16[512,1024]{1,0:T(8,128)(2,1)} %get-tuple-element.51) | copy-start | bytes 3145732
  346.8 28.1 %copy-start.3 = (f32[96,1024]{1,0:T(8,128)S(1)}, f32[96,1024]{1,0:T(8,128)}, u32[]{:S(2)}) copy-start(f32[96,1024]{1,0:T(8,128)} %copy-done.2) | copy-start | bytes 1179652
  346.8 28.1 %copy-start.58 = (f32[1,8,128]{2,0,1:T(1,128)S(1)}, f32[1,8,128]{2,0,1:T(1,128)}, u32[]{:S(2)}) copy-start(f32[1,8,128]{2,0,1:T(1,128)} %copy-done.57) | copy-start | bytes 12292
  346.8 28.1 %copy-start.98 = (f32[96]{0:T(128)S(1)}, f32[96]{0:T(128)}, u32[]{:S(2)}) copy-start(f32[96]{0:T(128)} %copy-done.97) | copy-start | bytes 1156
  346.8 28.1 %copy-start.104 = (f32[96]{0:T(128)S(1)}, f32[96]{0:T(128)}, u32[]{:S(2)}) copy-start(f32[96]{0:T(128)} %copy-done.103) | copy-start | bytes 1156
  346.8 31.7 %copy-start.41 = (bf16[4,96,1024]{2,1,0:T(8,128)(2,1)S(1)}, bf16[4,96,1024]{2,1,0:T(8,128)(2,1)}, u32[]{:S(2)}) copy-start(bf16[4,96,1024]{2,1,0:T(8,128)(2,1)} %normed.1) | copy-start | bytes 2359300
  378.5 34.8 %copy-start.15 = (f32[384,512]{1,0:T(8,128)S(1)}, f32[384,512]{1,0:T(8,128)}, u32[]{:S(2)}) copy-start(f32[384,512]{1,0:T(8,128)} %copy-done.14) | copy-start | bytes 2359300
  378.5 34.8 %copy-start.40 = (f32[384,512]{1,0:T(8,128)S(1)}, f32[384,512]{1,0:T(8,128)}, u32[]{:S(2)}) copy-start(f32[384,512]{1,0:T(8,128)} %get-tuple-element.169) | copy-start | bytes 2359300
  378.5 34.8 %copy-start.123 = (bf16[512,1024]{1,0:T(8,128)(2,1)S(1)}, bf16[512,1024]{1,0:T(8,128)(2,1)}, u32[]{:S(2)}) copy-start(bf16[512,1024]{1,0:T(8,128)(2,1)} %get-tuple-element.48) | copy-start | bytes 3145732
  465.6 58.8 %copy-start.10 = (f32[768,1024]{1,0:T(8,128)S(1)}, f32[768,1024]{1,0:T(8,128)}, u32[]{:S(2)}) copy-start(f32[768,1024]{1,0:T(8,128)} %get-tuple-element.127) | copy-start | bytes 9437188
  465.6 61.5 %copy-start.11 = (bf16[1,128,1536]{2,1,0:T(8,128)(2,1)S(1)}, bf16[1,128,1536]{2,1,0:T(8,128)(2,1)}, u32[]{:S(2)}) copy-start(bf16[1,128,1536]{2,1,0:T(8,128)(2,1)} %param.24) | copy-start | bytes 1179652
  595.2 26.7 %copy-start.118 = (f32[4000,256]{1,0:T(8,128)S(1)}, f32[4000,256]{1,0:T(8,128)}, u32[]{:S(2)}) copy-start(f32[4000,256]{1,0:T(8,128)} %param.40) | copy-start | bytes 12288004
  621.9 35.0 %copy-start.63 = (f32[24,128]{1,0:T(8,128)S(1)}, f32[24,128]{1,0:T(8,128)}, u32[]{:S(2)}) copy-start(f32[24,128]{1,0:T(8,128)} %reshape.596) | copy-start | bytes 36868
  621.9 53.5 %copy-start.12 = (f32[1,128,1536]{2,1,0:T(8,128)S(1)}, f32[1,128,1536]{2,1,0:T(8,128)}, u32[]{:S(2)}) copy-start(f32[1,128,1536]{2,1,0:T(8,128)} %get-tuple-element.111) | copy-start | bytes 2359300
  621.9 53.5 %copy-start.13 = (f32[1,128,1536]{2,1,0:T(8,128)S(1)}, f32[1,128,1536]{2,1,0:T(8,128)}, u32[]{:S(2)}) copy-start(f32[1,128,1536]{2,1,0:T(8,128)} %get-tuple-element.112) | copy-start | bytes 2359300
  621.9 55.5 %copy-start.33 = (bf16[1,512,128]{2,1,0:T(8,128)(2,1)S(1)}, bf16[1,512,128]{2,1,0:T(8,128)(2,1)}, u32[]{:S(2)}) copy-start(bf16[1,512,128]{2,1,0:T(8,128)(2,1)} %param.25) | copy-start | bytes 393220
  648.9 31.0 %copy-start.21 = (bf16[1,128,1024]{2,1,0:T(8,128)(2,1)S(1)}, bf16[1,128,1024]{2,1,0:T(8,128)(2,1)}, u32[]{:S(2)}) copy-start(bf16[1,128,1024]{2,1,0:T(8,128)(2,1)} %param.26) | copy-start | bytes 786436
  648.9 31.0 %copy-start.22 = (f32[1,128,1024]{2,1,0:T(8,128)S(1)}, f32[1,128,1024]{2,1,0:T(8,128)}, u32[]{:S(2)}) copy-start(f32[1,128,1024]{2,1,0:T(8,128)} %get-tuple-element.107) | copy-start | bytes 1572868
  648.9 31.0 %copy-start.23 = (f32[1,128,1024]{2,1,0:T(8,128)S(1)}, f32[1,128,1024]{2,1,0:T(8,128)}, u32[]{:S(2)}) copy-start(f32[1,128,1024]{2,1,0:T(8,128)} %get-tuple-element.108) | copy-start | bytes 1572868
  648.9 32.8 %copy-start.35 = (bf16[1,512,128]{2,1,0:T(8,128)(2,1)S(1)}, bf16[1,512,128]{2,1,0:T(8,128)(2,1)}, u32[]{:S(2)}) copy-start(bf16[1,512,128]{2,1,0:T(8,128)(2,1)} %param.27) | copy-start | bytes 393220
  (98 other events, 625.5 us)

commit v3 on v2

--- a/solution.py
+++ b/solution.py
@@ -412,6 +412,77 @@
     )(x)
 
 
+def late(task, turns):
+    before = task.run
+
+    def run(here, ins, outs, held):
+        live = before(here, ins, outs, held)
+        next(live)
+        for _ in range(turns + 1):
+            yield
+        yield from live
+
+    task.run = run
+    return task
+
+
+def tile_of(count, most):
+    fits = [d for d in range(16, most + 1, 16) if count % d == 0]
+    return max(fits) if fits else count
+
+
+def table_grad(embedding, finals, logs, targets, scales, head, H, most=400, slots=768, unroll=1):
+    V, D = embedding.shape
+    R = finals[0].shape[0]
+    Q = D // H
+    tile = tile_of(V, most)
+    count = R // slots
+
+    def body(head_ref, e_ref, *refs):
+        rows, columns = refs[:H], refs[H : 2 * H]
+        log_ref, target_ref, scale_ref, o_ref = refs[2 * H :]
+        table = e_ref[...]
+        first = pl.program_id(0) * tile
+        ids = first + lax.broadcasted_iota(jnp.int32, (tile, slots), 0)
+        o_ref[...] = jnp.zeros((tile, Q), jnp.float32)
+        for k in range(H):
+
+            def chunk(i, carry, k=k):
+                at = pl.ds(pl.multiple_of(i * slots, slots), slots)
+                logits = lax.dot_general(
+                    table, rows[k][at, :], (((1,), (1,)), ((), ())), preferred_element_type=jnp.float32
+                )
+                place = k * count + i
+                grads = jnp.exp(logits - log_ref[place]) - (ids == target_ref[place]).astype(jnp.float32)
+                grads = (grads * scale_ref[place]).astype(jnp.bfloat16)
+                o_ref[...] += jnp.dot(grads, columns[k][at, :], preferred_element_type=jnp.float32)
+                return carry
+
+            lax.fori_loop(0, count, chunk, 0, unroll=unroll)
+
+    fixed = pl.Buffered(1)
+    whole = lambda shape: pl.BlockSpec(shape, lambda t, head_ref: (0,) * len(shape), pipeline_mode=fixed)
+    shaped = lambda value: value.reshape(H * count, 1, slots)
+    return pl.pallas_call(
+        body,
+        out_shape=jax.ShapeDtypeStruct((V, Q), jnp.float32),
+        grid_spec=pltpu.PrefetchScalarGridSpec(
+            num_scalar_prefetch=1,
+            grid=(V // tile,),
+            in_specs=[pl.BlockSpec((tile, D), lambda t, head_ref: (t, 0))]
+            + [whole((R, D))] * H
+            + [pl.BlockSpec((R, Q), lambda t, head_ref: (0, head_ref[0]), pipeline_mode=fixed)] * H
+            + [whole((H * count, 1, slots))] * 3,
+            out_specs=pl.BlockSpec((tile, Q), lambda t, head_ref: (t, 0)),
+        ),
+        compiler_params=pltpu.CompilerParams(vmem_limit_bytes=56 * 2**20),
+        cost_estimate=pl.CostEstimate(
+            flops=2 * V * H * R * (D + Q), bytes_accessed=V * D * 2 + V * Q * 4 + H * R * D * 2, transcendentals=V * H * R
+        ),
+        name="table_grad",
+    )(head.reshape(1), embedding, *finals, *finals, shaped(logs), shaped(targets), shaped(scales))
+
+
 KD = 256
 VD = 512
 STEP = 10
@@ -492,6 +563,11 @@
     second_hat = new_second / (1.0 - BETA_TWO**STEP)
     ratio = moment_hat / (jnp.sqrt(second_hat) + ADAM_EPS) + DECAY_WT * weight
     return (new_moment, new_second, ratio)
+
+
+def shift(value, axis, by):
+    count = lax.axis_size(axis)
+    return lax.ppermute(value, axis, [(i, (i + by) % count) for i in range(count)])
 
 
 def local(
@@ -531,28 +607,16 @@
     token_start = s * span
     vocab_start = s * vocab_part
 
-    aligned = w_output.shape[2] % 128 == 0
-
     def run(cid, name, *tasks):
         return [results[0] for results in fused(cid, S, H, tasks, name)]
 
     def flat(blocks):
         return blocks.reshape((-1,) + blocks.shape[2:])
 
-    def gather_columns(weight):
-        return gather_seq(weight, S, columns=aligned)
-
-    def joined(gathered):
-        if aligned:
-            return gathered
-        return gathered.transpose(1, 0, 2).reshape(gathered.shape[1], -1)
-
-    def sum_columns(grad):
-        grad = grad.astype(bf)
-        if not aligned:
-            grad = grad.reshape(grad.shape[0], S, -1).transpose(1, 0, 2)
-        return sum_seq(grad, S, columns=aligned)
-
+    mixer = lax.all_gather(w_mixer[0], "seq", axis=0, tiled=True)
+    output = lax.all_gather(w_output[0], "seq", axis=1, tiled=True)
+    expand = lax.all_gather(w_expand[0], "seq", axis=0, tiled=True)
+    contract = lax.all_gather(w_contract[0], "seq", axis=1, tiled=True)
     small = jnp.concatenate([norm_gains.astype(f32), mom_gains, var_gains], axis=0)
     small = jnp.concatenate([small, jnp.zeros((16 - small.shape[0], small.shape[1]), f32)], axis=0)
 
@@ -562,14 +626,13 @@
     inside = (chosen >= 0) & (chosen < vocab_part)
     found = jnp.take(embedding, jnp.clip(chosen, 0, vocab_part - 1), axis=0)
     found = jnp.where(inside[:, None], found, jnp.zeros((), bf))
-    rows, mixer, small_all = run(
+    rows, small_all = run(
         1,
         "enter",
         lookup(found.reshape(S, rows_own, width), S, H, 4 if S <= 8 else 1),
-        gather_seq(w_mixer[0], S),
         gather_seq(small, S),
     )
-    x0, mixer = flat(rows), flat(mixer)
+    x0 = flat(rows)
     small_all = small_all.transpose(1, 0, 2).reshape(16, width)
     gains, mom_gains_all, var_gains_all = small_all[:3], small_all[3:6], small_all[6:9]
 
@@ -613,9 +676,7 @@
     values = proj_kv[:, KD:].astype(bf)
     weighted = (keys.astype(f32) * tail_decay).astype(bf)
     update = contract_dims(weighted, values, 0, 0)
-    everyone, output = run(2, "states", gather_seq(update.astype(bf), S), gather_columns(w_output[0]))
-    output = joined(output)
-    state = state_sum(everyone, False)
+    state = state_sum(run(2, "states", gather_seq(update.astype(bf), S))[0], False)
     normed_q = matmul(picker, normed).astype(bf)
     query = rotate(matmul(normed_q, mixer[:, :KD]), cosines_q, sines_q).astype(bf)
     gate_pre = matmul(normed_q, mixer[:, 2 * KD + VD :])
@@ -629,11 +690,7 @@
         return sum_head(value.astype(bf).reshape(H, own, width), H)
 
     x0_own = matmul(lax.dynamic_slice_in_dim(picker, h * own, own, 0), x0)
-    branch, expand, contract = run(
-        3, "mid", by_head(matmul(gated, output)), gather_seq(w_expand[0], S), gather_columns(w_contract[0])
-    )
-    expand, contract = flat(expand), joined(contract)
-    x1 = x0_own + branch
+    x1 = x0_own + run(3, "mid", by_head(matmul(gated, output)))[0]
     normed_b_own = (centre(x1) * gains[1]).astype(bf)
     normed_b = flat(run(4, "normed", gather_head(normed_b_own, H))[0])
     gate_up = matmul(normed_b, expand)
@@ -667,18 +724,14 @@
         8,
         "logits_back",
         sum_seq(matmul(grad_logits, embedding).astype(bf).reshape(S, own, width), S),
-        gather_head(final_own, H),
+        late(gather_head(final_own, H), 2),
         gather_head(log_total.reshape(-1, 128), H),
     )
     grad_x2, grad_gain_final = norm_back(x2, gains[2], grad_final)
 
     pieces = {}
-    grad_branch, pieces[1], pieces[2] = run(
-        9,
-        "branch_back",
-        gather_head(grad_x2.astype(bf), H),
-        gather_seq(finals, S, ahead=1),
-        gather_seq(finals, S, ahead=2),
+    grad_branch, pieces[1] = run(
+        9, "branch_back", gather_head(grad_x2.astype(bf), H), gather_seq(finals, S, ahead=1)
     )
     grad_branch = flat(grad_branch)
     grad_hidden = contract_dims(grad_branch, contract, 1, 1)
@@ -686,20 +739,13 @@
     _, gelu_back = jax.vjp(gelu_gate, gate_up[:, :width_ff], gate_up[:, width_ff:])
     grad_gate_up = jnp.concatenate(gelu_back(grad_hidden), axis=1).astype(bf)
     grad_expand = contract_dims(normed_b, grad_gate_up, 0, 0)
-    grad_normed_b, pieces[3], grad_contract = run(
-        10,
-        "expand_back",
-        by_head(contract_dims(grad_gate_up, expand, 1, 1)),
-        gather_seq(finals, S, ahead=3),
-        sum_columns(grad_contract),
+    grad_normed_b, pieces[2] = run(
+        10, "expand_back", by_head(contract_dims(grad_gate_up, expand, 1, 1)), gather_seq(finals, S, ahead=2)
     )
     grad_x1, grad_gain_b = norm_back(x1, gains[1], grad_normed_b)
     grad_x1 = grad_x1 + grad_x2
-    grad_attn, grad_expand = run(
-        11,
-        "attn_back",
-        gather_head(grad_x1.astype(bf), H),
-        sum_seq(grad_expand.astype(bf).reshape(S, -1, grad_expand.shape[1]), S),
+    grad_attn, pieces[3] = run(
+        11, "attn_back", gather_head(grad_x1.astype(bf), H), gather_seq(finals, S, ahead=3)
     )
     grad_attn = flat(grad_attn)
     grad_gated = contract_dims(grad_attn, output, 1, 1)
@@ -709,8 +755,7 @@
     grad_cross = (lead_decay * grad_ret).astype(bf)
     grad_ret = grad_ret.astype(bf)
     grad_state = contract_dims(query, grad_cross, 0, 0)
-    everyone, grad_output = run(12, "states_back", gather_seq(grad_state.astype(bf), S), sum_columns(grad_output))
-    grad_update = state_sum(everyone, True)
+    grad_update = state_sum(run(12, "states_back", gather_seq(grad_state.astype(bf), S))[0], True)
     grad_weights = contract_dims(grad_ret, values, 1, 1)
     grad_scores = (grad_weights * within).astype(bf)
     grad_query = matmul(grad_scores, keys) + contract_dims(grad_cross, state, 1, 1)
@@ -733,39 +778,44 @@
 
     scaled = grad_normed * gains[0]
     row_sums = jnp.stack([jnp.sum(scaled, axis=1), jnp.sum(scaled * hat0, axis=1)]).reshape(-1, 128)
-    columns, row_sums, grad_mixer = run(
-        13,
-        "mixer_back",
-        sum_head(grad_normed.astype(bf), H, columns=True),
-        gather_head(row_sums, H),
-        sum_seq(grad_mixer.astype(bf).reshape(S, -1, grad_mixer.shape[1]), S),
-    )
-    row_sums = jnp.sum(row_sums, axis=0).reshape(2, span, 1) / width
+    there = lax.rem(h + jnp.arange(H), H)
+
+    def in_turn(grid):
+        return jnp.take(grid.reshape(S, H, own).transpose(1, 0, 2).reshape(H, S * own), there, axis=0)
+
+    logs = jnp.take(logs.reshape(H, S * own), there, axis=0)
+    scales = in_turn(row_weights / count_live)
+    aims = in_turn(targets) - vocab_start
+    sent = grad_normed.astype(bf)
+    sent, row_sums, logs = lax.optimization_barrier((sent, row_sums, logs))
+    column_parts, sum_parts = [own_columns(sent)], [row_sums]
+    for k in range(1, H):
+        part = lax.dynamic_slice_in_dim(sent, lax.rem(h + k, H) * quarter, quarter, 1)
+        column_parts.append(shift(part, "head", k))
+        sum_parts.append(shift(row_sums, "head", k))
+    grad_table = table_grad(
+        embedding, [final_rows, flat(pieces[1]), flat(pieces[2]), flat(pieces[3])], logs, aims, scales, h, H
+    )
+    column_parts, sum_parts, grad_table = lax.optimization_barrier((column_parts, sum_parts, grad_table))
+    columns = sum(part.astype(f32) for part in column_parts)
+    row_sums = sum(sum_parts).reshape(2, span, 1) / width
     hat_cols = own_columns(hat0)
     gain_cols = lax.dynamic_slice_in_dim(gains[0], h * quarter, quarter, 0)
     grad_gain_a = jnp.sum(columns * hat_cols, axis=0)
     grad_in = row_scale(x0.astype(f32)) * (columns * gain_cols - row_sums[0] - hat_cols * row_sums[1])
     grad_in = grad_in + contract_dims(picker, own_columns(grad_attn), 0, 0)
     piece_rows = flat(run(14, "rows", gather_seq(grad_in.astype(bf), S))[0])
-    grad_table = contract_dims(grad_logits, own_columns(final_rows), 0, 0)
-    for k in range(1, H):
-        there = lax.rem(h + k, H)
-        rows_k = flat(pieces[k])
-        logits_k = contract_dims(rows_k, embedding, 1, 1)
-        log_k = lax.dynamic_index_in_dim(logs, there, 0, keepdims=False).reshape(-1)
-        grads_k = logits_grad(logits_k, log_k, there)[0]
-        grad_table = grad_table + contract_dims(grads_k, own_columns(rows_k), 0, 0)
-
     local_id = token_ids - vocab_start
     one_hot = (jnp.arange(vocab_part)[:, None] == local_id[None, :]).astype(bf)
     grad_table = grad_table + matmul(one_hot, piece_rows)
 
-    grad_mixer, grad_output, grad_expand, grad_contract = (
-        grad_mixer[None],
-        grad_output[None],
-        grad_expand[None],
-        grad_contract[None],
-    )
+    def scattered(value, dim):
+        return lax.psum_scatter(value.astype(bf), "seq", scatter_dimension=dim, tiled=True).astype(f32)[None]
+
+    grad_contract = scattered(grad_contract, 1)
+    grad_expand = scattered(grad_expand, 0)
+    grad_output = scattered(grad_output, 1)
+    grad_mixer = scattered(grad_mixer, 0)
     grad_gains = jnp.stack(
         [lax.dynamic_update_slice_in_dim(jnp.zeros((width,), f32), grad_gain_a, h * quarter, 0), grad_gain_b, grad_gain_final]
     )

time: 698 us -> 625 us (0.90)
  Pallas kernels: 404 us -> 341 us
  matrix products: 152 us -> 103 us
  between operations: 8.59 us -> 22.3 us
  starting transfers between devices: 0 us -> 11.2 us
    pallas_call x14 -> x13, Pallas kernels: 393 us -> 285 us  [fused(): pl.pallas_call(body, out_shape=outs, in_specs=[ANY] * len(operands), out_...]
    dot_general x23 -> x19, matrix products: 94.8 us -> 48.3 us  [contract_dims(): lax.dot_general(left_side, right_side, (((left_dim,), (right_dim,)), ((),...]
    pallas_call x0 -> x1, Pallas kernels: none -> 45.6 us  [table_grad(): pl.pallas_call(body, out_shape=jax.ShapeDtypeStruct((V, Q), jnp.float32),...]
    ppermute x0 -> x6, starting transfers between devices: none -> 10.9 us  [shift(): lax.ppermute(value, axis, [(i, (i + by) % count) for i in range(count)])]
    reduce_sum x4 -> x5, other arithmetic: 9.44 us -> 16.5 us  [local(): jnp.sum(p[2] * p[2])]
  transfers between devices with their start and end apart: 0 -> 14, of which waited for: 0 -> 0; matrix products, arithmetic and copies ran while one was open for 0% -> 24% of each run, Pallas kernels for 0% -> 32%
where the time goes in v3:
time: 625 us; the launch traced here: 614 us
  Pallas kernels  341 us (55%)
  matrix products  103 us (16%)
  other arithmetic  85 us (14%)
  local copies, waits for them, and re-layouts  48.8 us (8%)
  between operations  22.3 us (4%)
  starting transfers between devices  11.2 us (2%)
    pallas_call x13, Pallas kernels, fused(): pl.pallas_call(body, out_shape=outs, in_specs=[ANY] * len(operands), out_...  285 us
    dot_general x14, matrix products, matmul(): return jnp.dot(left_side, right_side, preferred_element_type=jnp.float32)  54.8 us
    dot_general x19, matrix products, contract_dims(): lax.dot_general(left_side, right_side, (((left_dim,), (right_dim,)), ((),...  48.3 us
    pallas_call x1, Pallas kernels, table_grad(): pl.pallas_call(body, out_shape=jax.ShapeDtypeStruct((V, Q), jnp.float32),...  45.6 us
    reduce_sum x5, other arithmetic, local(): jnp.sum(p[2] * p[2])  16.5 us
    unnamed x245, local copies, waits for them, and re-layouts  13 us
  transfers between devices with their start and end apart: 14, of which 0 were waited for; matrix products, arithmetic and copies ran while one was open for 24% of the time, Pallas kernels for 32%

profile of v3, /device:TPU:0, one launch (start us, length us, event | category | flops | bytes accessed | tf_op | source)
XLA Modules:
  0.0 613.8 jit_solution(10300190418334386617)
XLA Ops:
  11.8 11.5 %gather_fusion = bf16[1536,1024]{1,0:T(8,128)(2,1)S(1)} fusion(bf16[4000,1024]{1,0:T(8,128)(2,1)} %e_ref.1, s32[2048]{0:T(1024)S(1)} %pad_clamp_fusion), kind=kCustom, calls=%fused_computation.2 | custom fusion | bytes 6297600 | tf_op jit(solution)/shard_map/jit(_take)/gather | solution.py:627
  26.0 50.9 %enter.1 = (bf16[4,192,1024]{2,1,0:T(8,128)(2,1)}, f32[8,16,128]{2,1,0:T(8,128)}) custom-call(bf16[8,192,1024]{2,1,0:T(8,128)(2,1)} %select_select_fusion.refs_0_, f32[16,128]{1,0:T(8,128)} %maximum_maximum_fusion.refs_1_), custom_call_target="tpu_custom_call" | custom-call | bytes 33554432 | tf_op jit(solution)/shard_map/enter/pallas_call | solution.py:106
  95.5 2.9 select_reduce_fusion.2
  103.2 2.8 fusion.16
  109.2 17.8 %states.1 = bf16[8,256,512]{2,1,0:T(8,128)(2,1)} custom-call(bf16[256,512]{1,0:T(8,128)(2,1)} %convolution_convert_fusion.9.refs_0_), custom_call_target="tpu_custom_call" | custom-call | bytes 33554432 | tf_op jit(solution)/shard_map/states/pallas_call | solution.py:106
  139.0 19.1 %mid.1 = f32[96,1024]{1,0:T(8,128)} custom-call(bf16[4,96,1024]{2,1,0:T(8,128)(2,1)} %bitcast.223), custom_call_target="tpu_custom_call" | custom-call | bytes 33554432 | tf_op jit(solution)/shard_map/mid/pallas_call | solution.py:106
  160.8 20.9 %normed.1 = bf16[4,96,1024]{2,1,0:T(8,128)(2,1)} custom-call(bf16[96,1024]{1,0:T(8,128)(2,1)} %multiply_convert_fusion.11.refs_0_), custom_call_target="tpu_custom_call" | custom-call | bytes 33554432 | tf_op jit(solution)/shard_map/normed/pallas_call | solution.py:106
  188.8 20.9 %feed.1 = f32[96,1024]{1,0:T(8,128)} custom-call(bf16[4,96,1024]{2,1,0:T(8,128)(2,1)} %bitcast.224), custom_call_target="tpu_custom_call" | custom-call | bytes 33554432 | tf_op jit(solution)/shard_map/feed/pallas_call | solution.py:106
  211.9 12.9 %final.1 = bf16[8,96,1024]{2,1,0:T(8,128)(2,1)} custom-call(bf16[96,1024]{1,0:T(8,128)(2,1)} %multiply_convert_fusion.10.refs_0_.refs_1_), custom_call_target="tpu_custom_call" | custom-call | bytes 33554432 | tf_op jit(solution)/shard_map/final/pallas_call | solution.py:106
  224.8 9.6 %fusion.179 = (f32[768]{0:T(1024)S(1)}, f32[768,4000]{0,1:T(8,128)S(1)}) fusion(bf16[768,1024]{1,0:T(8,128)(2,1)} %bitcast.212, bf16[4000,1024]{1,0:T(8,128)(2,1)} %e_ref.1), kind=kOutput, calls=%fused_computation.373 | convolution fusion | flops 6294526976 | bytes 22055936 | tf_op jit(solution)/shard_map/dot_general | solution.py:500
  234.5 3.2 select_reduce_fusion
  239.5 6.2 %stats.1 = f32[8,12,128]{2,1,0:T(8,128)} custom-call(f32[12,128]{1,0:T(8,128)} %reshape.591.refs_0_), custom_call_target="tpu_custom_call" | custom-call | bytes 33554432 | tf_op jit(solution)/shard_map/stats/pallas_call | solution.py:106
  248.7 13.5 %fusion.15 = bf16[768,1024]{1,0:T(8,128)(2,1)} fusion(bf16[4000,1024]{1,0:T(8,128)(2,1)} %e_ref.1, f32[768,4000]{0,1:T(8,128)} %copy-done.3, f32[768]{0:T(1024)S(1)} %div.197, s32[768]{0:T(1024)S(1)} %copy-done.81, f32[768]{0:T(1024)S(1)} %log_add_fusion), kind=kOutput, calls=%fused_computation.46 | convolution fusion | flops 6310674432 | bytes 22062080 | tf_op jit(solution)/shard_map/dot_general | solution.py:509
  262.3 26.1 %logits_back.1 = (f32[96,1024]{1,0:T(8,128)}, bf16[4,96,1024]{2,1,0:T(8,128)(2,1)}, f32[4,6,128]{2,1,0:T(8,128)}) custom-call(bf16[8,96,1024]{2,1,0:T(8,128)(2,1)} %bitcast.215, bf16[96,1024]{1,0:T(8,128)(2,1)} %multiply_convert_fusion.10.refs_0_.refs_1_, f32[6,128]{1,0:T(8,128)} %bitcast.239), custom_call_target="tpu_custom_call" | custom-call | bytes 33554432 | tf_op jit(solution)/shard_map/logits_back/pallas_call | solution.py:106
  291.6 24.2 %branch_back.1 = (bf16[4,96,1024]{2,1,0:T(8,128)(2,1)}, bf16[8,96,1024]{2,1,0:T(8,128)(2,1)}) custom-call(bf16[96,1024]{1,0:T(8,128)(2,1)} %get-tuple-element.108.refs_0_, bf16[4,96,1024]{2,1,0:T(8,128)(2,1)} %get-tuple-element.47.refs_1_), custom_call_target="tpu_custom_call" | custom-call | bytes 33554432 | tf_op jit(solution)/shard_map/branch_back/pallas_call | solution.py:106
  320.1 23.4 %expand_back.1 = (f32[96,1024]{1,0:T(8,128)}, bf16[8,96,1024]{2,1,0:T(8,128)(2,1)}) custom-call(bf16[4,96,1024]{2,1,0:T(8,128)(2,1)} %bitcast.222, bf16[4,96,1024]{2,1,0:T(8,128)(2,1)} %get-tuple-element.47.refs_1_), custom_call_target="tpu_custom_call" | custom-call | bytes 33554432 | tf_op jit(solution)/shard_map/expand_back/pallas_call | solution.py:106
  347.3 23.2 %attn_back.1 = (bf16[4,96,1024]{2,1,0:T(8,128)(2,1)}, bf16[8,96,1024]{2,1,0:T(8,128)(2,1)}) custom-call(bf16[96,1024]{1,0:T(8,128)(2,1)} %add_convert_fusion.1.refs_0_, bf16[4,96,1024]{2,1,0:T(8,128)(2,1)} %get-tuple-element.47.refs_1_), custom_call_target="tpu_custom_call" | custom-call | bytes 33554432 | tf_op jit(solution)/shard_map/attn_back/pallas_call | solution.py:106
  376.6 3.0 add_add_fusion
  380.7 17.2 %states_back.1 = bf16[8,256,512]{2,1,0:T(8,128)(2,1)} custom-call(bf16[256,512]{1,0:T(8,128)(2,1)} %convolution_convert_fusion.8.refs_0_), custom_call_target="tpu_custom_call" | custom-call | bytes 33554432 | tf_op jit(solution)/shard_map/states_back/pallas_call | solution.py:106
  417.3 2.9 fusion.119
  420.3 2.9 fusion.118
  427.2 7.1 %multiply_reduce_fusion.4 = (f32[768]{0:T(1024)S(1)}, f32[768]{0:T(1024)S(1)}, bf16[768,1024]{1,0:T(8,128)(2,1)}, f32[768,1024]{1,0:T(8,128)}) fusion(f32[1024]{0:T(1024)S(1)} %bitcast.242, f32[768]{0:T(1024)S(1)} %copy-done.78, f32[768]{0:T(1024)S(1)} %copy-done.80, bf16[4,192,1024]{2,1,0:T(8,128)(2,1)S(1)} %copy-done, ...), kind=kOutput, calls=%fused_computation.38 | convolution fusion | flops 2422209024 | bytes 11812864 | tf_op jit(solution)/shard_map/dot_general | solution.py:500
  435.1 4.1 collective-permute-start.3
  441.7 5.7 convolution_convert_fusion
  453.2 45.6 %table_grad.1 = f32[4000,256]{1,0:T(8,128)} custom-call(s32[1]{0:T(128)} %bitcast.42.head_ref, bf16[4000,1024]{1,0:T(8,128)(2,1)} %e_ref.1, bf16[768,1024]{1,0:T(8,128)(2,1)} %bitcast.213, bf16[768,1024]{1,0:T(8,128)(2,1)} %bitcast.253, bf16[768,1024]{1,0:T(8,128)(2,1)} %bitcast.255, bf16[768,1024]{1,0:T(8,128)(2,1)} %bitcast.257, ...), custom_call_target="tpu_custom_call" | custom-call | flops 31457280000 | bytes 18579456 | tf_op jit(solution)/shard_map/table_grad/pallas_call | solution.py:466
  504.4 22.1 %rows.1 = bf16[8,768,256]{2,1,0:T(8,128)(2,1)} custom-call(bf16[768,256]{1,0:T(8,128)(2,1)} %fusion.26.refs_0_), custom_call_target="tpu_custom_call" | custom-call | bytes 33554432 | tf_op jit(solution)/shard_map/rows/pallas_call | solution.py:106
  526.6 20.0 %fusion = f32[4000,256]{1,0:T(8,128)S(1)} fusion(bf16[6144,256]{1,0:T(8,128)(2,1)} %bitcast.211, s32[6144]{0:T(1024)S(1)} %copy-done.69), kind=kOutput, calls=%fused_computation.5 | convolution fusion | flops 12607488000 | bytes 7266304 | tf_op jit(solution)/shard_map/dot_general | solution.py:509
  546.7 8.1 %multiply_reduce_fusion.2 = (f32[]{:T(128)}, f32[4000,256]{1,0:T(8,128)}, f32[4000,256]{1,0:T(8,128)}, f32[4000,256]{1,0:T(8,128)}, f32[]{:T(128)}) fusion(bf16[4000,1024]{1,0:T(8,128)(2,1)} %e_ref.1, s32[]{:T(128)S(6)} %select_n.142, f32[4000,256]{1,0:T(8,128)S(1)} %copy-done.7, f32[4000,256]{1,0:T(8,128)S(1)} %fusion, f32[4000,256]{1,0:T(8,128)S(1)} %copy-done.5, ...), kind=kLoop, calls=%fused_computation.27 | loop fusion | flops 19456000 | bytes 30720012 | tf_op jit(solution)/shard_map/reduce_sum | solution.py:837
  562.4 3.2 multiply_reduce_fusion.6
  565.5 6.5 %stack.92 = f32[11]{0:T(128)S(1)} concatenate(f32[1]{0:T(128)} %bitcast, f32[1]{0:T(128)} %bitcast.1, f32[1]{0:T(128)} %bitcast.2, f32[1]{0:T(128)} %bitcast.3, f32[1]{0:T(128)} %bitcast.4, f32[1]{0:T(128)} %bitcast.32, f32[1]{0:T(128)} %bitcast.35, f32[1]{0:T(128)} %bitcast.38, f32[1]{0:T(128)} %bitcast.41, f32[1]{0:T(128)} %bitcast.52, f32[1]{0:T(128)} %bitcast.53), dimensions={0} | concatenate | bytes 88 | tf_op jit(solution)/shard_map/stack | solution.py:836
  572.7 10.1 %all_sum.1 = f32[32,128]{1,0:T(8,128)} custom-call(f32[32,128]{1,0:T(8,128)} %pad_maximum_fusion.5.x_ref), custom_call_target="tpu_custom_call" | custom-call | tf_op jit(solution)/shard_map/all_sum/pallas_call | solution.py:396
  594.6 5.3 convert_subtract_fusion
  (454 shorter events, 138.4 us)
Async XLA Ops:
  7.2 96.0 %all-gather.9.cloned.1.call-start = ((), (), s32[]{:S(2)}) async-start(), calls=%async_computation.6 | async-start | bytes 3538944 | tf_op jit(solution)/shard_map/all_gather | solution.py:616
  7.9 128.4 %all-gather.11.cloned.1.call-start = ((), (), s32[]{:S(2)}) async-start(), calls=%async_computation.7 | async-start | bytes 1179648 | tf_op jit(solution)/shard_map/all_gather | solution.py:617
  8.7 173.0 %all-gather.13.cloned.1.call-start = ((), (), s32[]{:S(2)}) async-start(), calls=%async_computation.8 | async-start | bytes 2359296 | tf_op jit(solution)/shard_map/all_gather | solution.py:618
  9.4 176.6 %all-gather.15.cloned.1.call-start = ((), (), s32[]{:S(2)}) async-start(), calls=%async_computation.9 | async-start | bytes 1179648 | tf_op jit(solution)/shard_map/all_gather | solution.py:619
  10.0 544.9 %reduce-scatter.13.cloned.1.call-start = ((), (), s32[]{:S(2)}) async-start(), calls=%async_computation.10 | async-start | bytes 1179648
  26.0 56.7 %copy-start.49 = (s32[6144]{0:T(1024)S(1)}, s32[6144]{0:T(1024)}, u32[]{:S(2)}) copy-start(s32[6144]{0:T(1024)} %param.24) | copy-start | bytes 73732
  26.0 60.3 %copy-start.54 = (s32[6144]{0:T(1024)S(1)}, s32[6144]{0:T(1024)}, u32[]{:S(2)}) copy-start(s32[6144]{0:T(1024)} %param.23) | copy-start | bytes 73732
  185.7 25.5 %copy-start.61 = (f32[1,8,128]{2,0,1:T(1,128)S(1)}, f32[1,8,128]{2,0,1:T(1,128)}, u32[]{:S(2)}) copy-start(f32[1,8,128]{2,0,1:T(1,128)} %get-tuple-element.133) | copy-start | bytes 12292
  210.9 77.5 %copy-start.88 = (f32[96]{0:T(128)}, f32[96]{0:T(128)S(1)}, u32[]{:S(2)}) copy-start(f32[96]{0:T(128)S(1)} %broadcast_multiply_fusion.6) | copy-start | bytes 1156
  211.1 77.3 %copy-start.94 = (f32[96]{0:T(128)}, f32[96]{0:T(128)S(1)}, u32[]{:S(2)}) copy-start(f32[96]{0:T(128)S(1)} %add_rsqrt_fusion.1) | copy-start | bytes 1156
  248.7 41.0 %copy-start.62 = (f32[1,8,128]{2,0,1:T(1,128)S(1)}, f32[1,8,128]{2,0,1:T(1,128)}, u32[]{:S(2)}) copy-start(f32[1,8,128]{2,0,1:T(1,128)} %get-tuple-element.133) | copy-start | bytes 12292
  262.3 53.5 %copy-start.32 = (f32[384,1024]{1,0:T(8,128)S(1)}, f32[384,1024]{1,0:T(8,128)}, u32[]{:S(2)}) copy-start(f32[384,1024]{1,0:T(8,128)} %copy-done.31) | copy-start | bytes 4718596
  262.3 53.5 %copy-start.112 = (bf16[1,512,1024]{2,1,0:T(8,128)(2,1)S(1)}, bf16[1,512,1024]{2,1,0:T(8,128)(2,1)}, u32[]{:S(2)}) copy-start(bf16[1,512,1024]{2,1,0:T(8,128)(2,1)} %all-gather.15.cloned.1.call-done) | copy-start | bytes 3145732
  318.2 25.3 %copy-start.60 = (f32[1,8,128]{2,0,1:T(1,128)S(1)}, f32[1,8,128]{2,0,1:T(1,128)}, u32[]{:S(2)}) copy-start(f32[1,8,128]{2,0,1:T(1,128)} %get-tuple-element.134) | copy-start | bytes 12292
  318.2 25.3 %copy-start.87 = (f32[96]{0:T(128)S(1)}, f32[96]{0:T(128)}, u32[]{:S(2)}) copy-start(f32[96]{0:T(128)} %copy-done.86) | copy-start | bytes 1156
  343.5 29.0 %copy-start.10 = (f32[384,512]{1,0:T(8,128)S(1)}, f32[384,512]{1,0:T(8,128)}, u32[]{:S(2)}) copy-start(f32[384,512]{1,0:T(8,128)} %copy-done.9) | copy-start | bytes 2359300
  343.5 29.0 %copy-start.46 = (f32[384,512]{1,0:T(8,128)S(1)}, f32[384,512]{1,0:T(8,128)}, u32[]{:S(2)}) copy-start(f32[384,512]{1,0:T(8,128)} %get-tuple-element.162) | copy-start | bytes 2359300
  343.5 29.0 %copy-start.111 = (bf16[1,512,1024]{2,1,0:T(8,128)(2,1)S(1)}, bf16[1,512,1024]{2,1,0:T(8,128)(2,1)}, u32[]{:S(2)}) copy-start(bf16[1,512,1024]{2,1,0:T(8,128)(2,1)} %all-gather.11.cloned.1.call-done) | copy-start | bytes 3145732
  376.6 179.5 %reduce-scatter.15.cloned.1.call-start = ((), (), s32[]{:S(2)}) async-start(), calls=%async_computation.11 | async-start | bytes 1179648
  408.6 151.7 %reduce-scatter.11.cloned.1.call-start = ((), (), s32[]{:S(2)}) async-start(), calls=%async_computation.5 | async-start | bytes 2359296 | tf_op jit(solution)/shard_map/reduce_scatter | solution.py:813
  417.3 145.1 %reduce-scatter.9.cloned.1.call-start = ((), (), s32[]{:S(2)}) async-start(), calls=%async_computation.4 | async-start | bytes 3538944 | tf_op jit(solution)/shard_map/reduce_scatter | solution.py:813
  435.1 16.3 %collective-permute-start.3 = (f32[12,128]{1,0:T(8,128)S(1)}, f32[12,128]{1,0:T(8,128)S(1)}, u32[]{:S(2)}, u32[]{:S(2)}) collective-permute-start(f32[12,128]{1,0:T(8,128)S(1)} %reshape.600), channel_id=1, source_target_pairs={{0,1},{1,2},{2,3},{3,0},{4,5},{5,6},{6,7},{7,4},{8,9},{9,10},{10,1... | collective-permute-start | bytes 18440 | tf_op jit(solution)/shard_map/ppermute | solution.py:570
  439.2 60.9 %collective-permute-start.4 = (f32[12,128]{1,0:T(8,128)S(1)}, f32[12,128]{1,0:T(8,128)S(1)}, u32[]{:S(2)}, u32[]{:S(2)}) collective-permute-start(f32[12,128]{1,0:T(8,128)S(1)} %reshape.600), channel_id=1, source_target_pairs={{0,2},{1,3},{2,0},{3,1},{4,6},{5,7},{6,4},{7,5},{8,10},{9,11},{10,... | collective-permute-start | bytes 18440 | tf_op jit(solution)/shard_map/ppermute | solution.py:570
  441.5 58.7 %collective-permute-start.5 = (f32[12,128]{1,0:T(8,128)S(1)}, f32[12,128]{1,0:T(8,128)S(1)}, u32[]{:S(2)}, u32[]{:S(2)}) collective-permute-start(f32[12,128]{1,0:T(8,128)S(1)} %reshape.600), channel_id=1, source_target_pairs={{0,3},{1,0},{2,1},{3,2},{4,7},{5,4},{6,5},{7,6},{8,11},{9,8},{10,9... | collective-permute-start | bytes 18440 | tf_op jit(solution)/shard_map/ppermute | solution.py:570
  448.8 51.4 %collective-permute-start = (bf16[768,256]{1,0:T(8,128)(2,1)S(1)}, bf16[768,256]{1,0:T(8,128)(2,1)S(1)}, u32[]{:S(2)}, u32[]{:S(2)}) collective-permute-start(bf16[768,256]{1,0:T(8,128)(2,1)S(1)} %get-tuple-element.125), channel_id=1, source_target_pairs={{0,1},{1,2},{2,3},{3,0},{4,5},{5,6},{6,7},{7,4},{8,9},{9,10},{10,1... | collective-permute-start | bytes 1179656 | tf_op jit(solution)/shard_map/ppermute | solution.py:570
  450.7 49.5 %collective-permute-start.1 = (bf16[768,256]{1,0:T(8,128)(2,1)S(1)}, bf16[768,256]{1,0:T(8,128)(2,1)S(1)}, u32[]{:S(2)}, u32[]{:S(2)}) collective-permute-start(bf16[768,256]{1,0:T(8,128)(2,1)S(1)} %get-tuple-element.124), channel_id=1, source_target_pairs={{0,2},{1,3},{2,0},{3,1},{4,6},{5,7},{6,4},{7,5},{8,10},{9,11},{10,... | collective-permute-start | bytes 1179656 | tf_op jit(solution)/shard_map/ppermute | solution.py:570
  451.4 48.8 %collective-permute-start.2 = (bf16[768,256]{1,0:T(8,128)(2,1)S(1)}, bf16[768,256]{1,0:T(8,128)(2,1)S(1)}, u32[]{:S(2)}, u32[]{:S(2)}) collective-permute-start(bf16[768,256]{1,0:T(8,128)(2,1)S(1)} %get-tuple-element.123), channel_id=1, source_target_pairs={{0,3},{1,0},{2,1},{3,2},{4,7},{5,4},{6,5},{7,6},{8,11},{9,8},{10,9... | collective-permute-start | bytes 1179656 | tf_op jit(solution)/shard_map/ppermute | solution.py:570
  453.2 48.4 %copy-start.105 = (f32[256]{0:T(256)S(1)}, f32[256]{0:T(256)}, u32[]{:S(2)}) copy-start(f32[256]{0:T(256)} %dynamic_slice.61) | copy-start | bytes 3076
  562.4 39.6 %copy-start.21 = (f32[1,128,1024]{2,1,0:T(8,128)}, f32[1,128,1024]{2,1,0:T(8,128)S(1)}, u32[]{:S(2)}) copy-start(f32[1,128,1024]{2,1,0:T(8,128)S(1)} %get-tuple-element.102) | copy-start | bytes 1572868
  562.4 39.6 %copy-start.22 = (f32[1,128,1024]{2,1,0:T(8,128)}, f32[1,128,1024]{2,1,0:T(8,128)S(1)}, u32[]{:S(2)}) copy-start(f32[1,128,1024]{2,1,0:T(8,128)S(1)} %get-tuple-element.103) | copy-start | bytes 1572868
  565.5 38.3 %copy-start.11 = (f32[1,128,1536]{2,1,0:T(8,128)}, f32[1,128,1536]{2,1,0:T(8,128)S(1)}, u32[]{:S(2)}) copy-start(f32[1,128,1536]{2,1,0:T(8,128)S(1)} %get-tuple-element.106) | copy-start | bytes 2359300
  565.5 38.3 %copy-start.12 = (f32[1,128,1536]{2,1,0:T(8,128)}, f32[1,128,1536]{2,1,0:T(8,128)S(1)}, u32[]{:S(2)}) copy-start(f32[1,128,1536]{2,1,0:T(8,128)S(1)} %get-tuple-element.107) | copy-start | bytes 2359300
  (101 other events, 890.3 us)
Sparse Core Ops, SparseCore 0:
  9.9 51.0 all-gather.8
  62.9 22.5 all-gather.10
  87.3 29.0 all-gather.12
  118.2 27.3 all-gather.14
  376.7 38.8 reduce-scatter.12
  418.6 35.9 reduce-scatter.14
  457.8 41.0 reduce-scatter.10
  502.4 46.0 reduce-scatter.8
